TPU v7x, 32 devices: a whole 2x2x4 slice. The times are simulated.
32 devices in a mesh: chan: 4 (over y, x), tm: 8 (over z, core).
Axes of the slice: x: 2, y: 2, z: 4, core: 2. Of those that a mesh axis runs over, the one named last changes fastest.
Arguments:
- volts: bfloat16 [4, 2048, 512], P('chan', 'tm'), may hold values from -120 to 120
- picks: int32 [4, 8], P('chan'), may hold values from 0 to 63, as said below
- angles: float32 [64], replicated, may hold values from -3.140625 to 3.140625
Outputs:
- cleaned: float32 [4, 2048, 512], P('chan', 'tm')
Inputs may be any that keep to these rules, and one draw needn't show every extreme that they name: No index appears twice among all groups' picks.
All inputs are finite; a program needn't handle non-finite values.
Results may differ from a plain program's by a relative error of at most 0.00035.
Values sent between devices are 32-bit elements; how exact they have to be, the bound alone decides.
No kernel may reach another device: no remote copies, remote signals or barrier semaphores. Data moves between devices by JAX's collectives and lax.ppermute only.
A program may use at most 64 MiB of HBM per device.

v0:
```python
import jax
import jax.numpy as jnp
from jax import lax
from jax.experimental import pallas as pl
from jax.experimental.pallas import tpu as pltpu
from jax.sharding import PartitionSpec as P


SEG = 256
HORIZON = 256
LOADING = 0.1
STEER_LOADING = 0.05
TINY_LEVEL = 1e-06
PRECISE = lax.Precision.HIGHEST
F32 = jnp.float32
BF16 = jnp.bfloat16
VM = pl.BlockSpec(memory_space=pltpu.VMEM)
SM = pl.BlockSpec(memory_space=pltpu.SMEM)
PARAMS = pltpu.CompilerParams(vmem_limit_bytes=24 * 2**20)


def gram_kernel(parity_ref, volts_ref, keep_ref, give_ref, power_ref, mixed_ref):
    antennas = volts_ref.shape[1] // 2
    segments = volts_ref.shape[0] // SEG
    half = antennas // 2
    forget = 1.0 - 1.0 / HORIZON
    mixed = None
    for seg in range(segments):
        a = volts_ref[seg * SEG : (seg + 1) * SEG, :antennas]
        b = volts_ref[seg * SEG : (seg + 1) * SEG, antennas:]
        left = jnp.concatenate([a, b, b, -a], axis=0)
        right = jnp.concatenate([a, b, a, b], axis=0)
        term = lax.dot_general(
            left, right, (((0,), (0,)), ((), ())), preferred_element_type=F32
        )
        mixed = term if mixed is None else forget * mixed + term
    mixed_ref[...] = mixed
    row = lax.broadcasted_iota(jnp.int32, mixed.shape, 0)
    column = lax.broadcasted_iota(jnp.int32, mixed.shape, 1)
    trace = jnp.sum(jnp.where(row == column, mixed, 0.0))
    power_ref[...] = jnp.full(power_ref.shape, trace / antennas, F32)
    parity = parity_ref[0]
    keep_ref[...] = mixed_ref[pl.ds(pl.multiple_of(parity * half, half), half), :]
    give_ref[...] = mixed_ref[pl.ds(pl.multiple_of((1 - parity) * half, half), half), :]


def split(value):
    high = value.astype(BF16)
    return high, (value - high.astype(F32)).astype(BF16)


def dot3(left, right):
    (lh, ll), (rh, rl) = left, right
    return (
        jnp.dot(lh, rh, preferred_element_type=F32)
        + jnp.dot(lh, rl, preferred_element_type=F32)
        + jnp.dot(ll, rh, preferred_element_type=F32)
    )


def beside(first, second):
    return jnp.concatenate([first, second], axis=1)


def over(first, second):
    return jnp.concatenate([first, second], axis=0)


def square_kernel(parity_ref, own_ref, other_ref, cov_ref, square_ref, stats_ref, mixed_ref):
    half, antennas = own_ref.shape
    parity = parity_ref[0]
    mixed_ref[pl.ds(pl.multiple_of(parity * half, half), half), :] = own_ref[...]
    mixed_ref[pl.ds(pl.multiple_of((1 - parity) * half, half), half), :] = other_ref[...]
    mixed = mixed_ref[...]
    row = lax.broadcasted_iota(jnp.int32, mixed.shape, 0)
    column = lax.broadcasted_iota(jnp.int32, mixed.shape, 1)
    trace = jnp.sum(jnp.where(row == column, mixed, 0.0), keepdims=True)
    unit = 1.0 / (trace / antennas + TINY_LEVEL)
    mixed = mixed * unit
    flipped = mixed.T
    re, im = 0.5 * (mixed + flipped), 0.5 * (mixed - flipped)
    cov_ref[:antennas, :], cov_ref[antennas:, :] = re, im
    (rh, rl), (ih, il) = split(re), split(im)
    full = tuple(over(beside(r, -i), beside(i, r)) for r, i in ((rh, ih), (rl, il)))
    square_ref[...] = dot3(full, (over(rh, ih), over(rl, il)))
    norm = jnp.sum(mixed * mixed, keepdims=True)
    lane = lax.broadcasted_iota(jnp.int32, stats_ref.shape, 1)
    stats_ref[...] = jnp.where(lane == 0, norm, jnp.where(lane == 1, trace * unit, unit))


def whiten_kernel(band_ref, stats_ref, cov_ref, square_ref, w_ref, out_ref):
    samples = w_ref.shape[0]
    antennas = cov_ref.shape[1]
    norm, trace, unit = stats_ref[0:1, 0:1], stats_ref[0:1, 1:2], stats_ref[0:1, 2:3]
    beta = 1.0 / (unit * band_ref[0:1, 0:1])
    total = 2.0 * (
        beta * (beta * norm + 2.0 * LOADING * trace) + LOADING * LOADING * antennas
    )
    omega = 1.0 / jnp.sqrt(total)
    slope, shift = omega * beta, omega * LOADING
    cov, square = cov_ref[...], square_ref[...]
    bend = (slope * slope) * square
    first = split(bend + (2.0 * slope * (shift - 1.0)) * cov)
    second = split((slope * (3.0 - 2.0 * shift)) * cov - bend)
    left, right = slice(0, antennas), slice(antennas, 2 * antennas)

    def turn(u, v):
        parts = zip(split(u), split(v), strict=True)
        return tuple(over(beside(p, q), beside(q, -p)) for p, q in parts)

    w_u, w_v = w_ref[:, left], w_ref[:, right]
    step = dot3(turn(w_u, w_v), first)
    keep = 2.0 + shift * (shift - 2.0)
    u, v = keep * w_u + step[:samples], keep * w_v + step[samples:]
    step = dot3(turn(u, v), second)
    keep = 2.0 - shift * (3.0 - shift)
    out_ref[:, left] = omega * (w_u + keep * u - step[:samples])
    out_ref[:, right] = omega * (w_v + keep * v - step[samples:])


def complex_inverse(re, im):
    size = re.shape[0]
    row = lax.broadcasted_iota(jnp.int32, re.shape, 0)
    column = lax.broadcasted_iota(jnp.int32, re.shape, 1)
    for j in range(size):
        here = column[:1] == j
        col_re, col_im = re[:, j : j + 1], im[:, j : j + 1]
        scale = 1.0 / re[j : j + 1, j : j + 1]
        row_re = jnp.where(here, scale, re[j : j + 1] * scale)
        row_im = jnp.where(here, 0.0, im[j : j + 1] * scale)
        rest_re, rest_im = jnp.where(column == j, 0.0, re), jnp.where(column == j, 0.0, im)
        rest_re = rest_re - (col_re * row_re - col_im * row_im)
        rest_im = rest_im - (col_re * row_im + col_im * row_re)
        re = jnp.where(row == j, row_re, rest_re)
        im = jnp.where(row == j, row_im, rest_im)
    return re, im


def across(left, right):
    return lax.dot_general(
        left, right, (((1,), (1,)), ((), ())), precision=PRECISE, preferred_element_type=F32
    )


def null_kernel(picks_ref, angles_ref, volts_ref, out_ref):
    antennas = volts_ref.shape[1] // 2
    count = picks_ref.shape[1]
    row = lax.broadcasted_iota(jnp.int32, (count, 128), 0)
    angle = jnp.zeros((count, 128), F32)
    for k in range(count):
        angle = jnp.where(row == k, angles_ref[picks_ref[0, k]], angle)
    turn = (jnp.pi * jnp.sin(angle))[:, :1]
    position = lax.broadcasted_iota(jnp.int32, (count, antennas), 1).astype(F32)
    phase = turn * position
    norming = antennas**0.5
    re, im = jnp.cos(phase) / norming, jnp.sin(phase) / norming
    both = jnp.concatenate([re, im], axis=1)
    turned = jnp.concatenate([-im, re], axis=1)
    eye = lax.broadcasted_iota(jnp.int32, (count, count), 0) == lax.broadcasted_iota(
        jnp.int32, (count, count), 1
    )
    gram_re = across(both, both) + jnp.where(eye, STEER_LOADING, 0.0)
    gram_im = across(both, turned)
    inv_re, inv_im = complex_inverse(gram_re, gram_im)
    steer = jnp.concatenate([both, turned], axis=0)
    inverse = jnp.concatenate(
        [
            jnp.concatenate([inv_re, inv_im], axis=1),
            jnp.concatenate([-inv_im, inv_re], axis=1),
        ],
        axis=0,
    )
    back = jnp.dot(inverse, steer, precision=PRECISE, preferred_element_type=F32)
    volts = volts_ref[...]
    nt = (((1,), (1,)), ((), ()))
    inner = sum(
        lax.dot_general(volts, part, nt, preferred_element_type=F32) for part in split(steer)
    )
    out_ref[...] = volts.astype(F32) - dot3(split(inner), split(back))


def exchange(value, axis, mask):
    return lax.ppermute(value, axis, [(i, i ^ mask) for i in range(lax.axis_size(axis))])


def choose(index, values):
    chosen = jnp.asarray(values[0], F32)
    for i, value in enumerate(values[1:], 1):
        chosen = jnp.where(index == i, value, chosen)
    return chosen


def earlier_chips(value, decay, mirrored):
    chips = lax.axis_size("tm") // 2
    chip = lax.axis_index("tm") // 2
    length, total, before = 1, value, None
    while length < chips:
        mask = 2 * length - 1 if mirrored else length
        got = exchange(total, "tm", 2 * mask)
        upper = (chip // length) % 2 == 1
        weight = jnp.where(upper, choose(chip % length, [decay**i for i in range(length)]), 0.0)
        before = weight * got if before is None else before + weight * got
        if 2 * length < chips:
            far = decay**length
            total = jnp.where(upper, 1.0, far) * total + jnp.where(upper, far, 1.0) * got
        length *= 2
    return jnp.zeros_like(value) if before is None else before


def sum_groups(value):
    groups = lax.axis_size("chan")
    if groups & (groups - 1):
        return lax.psum(value, "chan")
    step = 1
    while step < groups:
        got = exchange(value, "chan", step)
        value = value + got
        step *= 2
    return value


def steps(volts, picks, angles):
    voltage = volts[0]
    rows, width = voltage.shape
    antennas = width // 2
    half = antennas // 2
    segments = rows // SEG
    odd = lax.axis_index("tm") % 2
    parity = odd.reshape(1).astype(jnp.int32)
    is_odd = odd == 1
    decay = (1.0 - 1.0 / HORIZON) ** segments

    keep, give, power = pl.pallas_call(
        gram_kernel,
        out_shape=(
            jax.ShapeDtypeStruct((half, antennas), F32),
            jax.ShapeDtypeStruct((half, antennas), F32),
            jax.ShapeDtypeStruct((8, 128), F32),
        ),
        in_specs=[SM, VM],
        out_specs=(VM, VM, VM),
        scratch_shapes=[pltpu.VMEM((antennas, antennas), F32)],
        cost_estimate=pl.CostEstimate(
            flops=4 * rows * width * antennas, bytes_accessed=rows * width * 2, transcendentals=0
        ),
        compiler_params=PARAMS,
        name="segment_gram",
    )(parity, voltage)

    got = exchange(give, "tm", 1)
    mine, theirs = jnp.where(is_odd, 1.0, decay), jnp.where(is_odd, decay, 1.0)
    pair = mine * keep + theirs * got
    before = earlier_chips(pair, decay * decay, True)
    even_cov = decay * before + jnp.where(is_odd, got, keep)
    odd_cov = decay * decay * before + pair
    own = jnp.where(is_odd, odd_cov, even_cov)
    other = exchange(jnp.where(is_odd, even_cov, odd_cov), "tm", 1)

    level = sum_groups(power)
    level_before = earlier_chips(level, decay * decay, False)
    levels = jnp.concatenate([level, level_before], axis=0)
    got_levels = exchange(levels, "tm", 1)
    level_even = jnp.where(is_odd, got_levels, levels)
    level_odd = jnp.where(is_odd, levels, got_levels)
    level_own = decay * (decay * level_even[8:] + level_odd[8:]) + level_even[:8]
    level_own = jnp.where(is_odd, decay * level_own + level_odd[:8], level_own)
    band = level_own / lax.axis_size("chan") + TINY_LEVEL

    projected = pl.pallas_call(
        null_kernel,
        out_shape=jax.ShapeDtypeStruct((rows, width), F32),
        in_specs=[SM, SM, VM],
        out_specs=VM,
        cost_estimate=pl.CostEstimate(
            flops=4 * rows * width * 128, bytes_accessed=rows * width * 6, transcendentals=0
        ),
        compiler_params=PARAMS,
        name="null",
    )(picks, angles, voltage)

    cov, square, stats = pl.pallas_call(
        square_kernel,
        out_shape=(
            jax.ShapeDtypeStruct((width, antennas), F32),
            jax.ShapeDtypeStruct((width, antennas), F32),
            jax.ShapeDtypeStruct((8, 128), F32),
        ),
        in_specs=[SM, VM, VM],
        out_specs=(VM, VM, VM),
        scratch_shapes=[pltpu.VMEM((antennas, antennas), F32)],
        cost_estimate=pl.CostEstimate(
            flops=6 * width * width * antennas, bytes_accessed=width * antennas * 8, transcendentals=0
        ),
        compiler_params=PARAMS,
        name="square",
    )(parity, own, other)

    cleaned = pl.pallas_call(
        whiten_kernel,
        out_shape=jax.ShapeDtypeStruct((rows, width), F32),
        in_specs=[VM] * 5,
        out_specs=VM,
        cost_estimate=pl.CostEstimate(
            flops=12 * rows * width * width, bytes_accessed=rows * width * 8, transcendentals=0
        ),
        compiler_params=PARAMS,
        name="whiten",
    )(band, stats, cov, square, projected)
    return cleaned[None]


def solution(mesh):
    placed = (P("chan", "tm", None), P("chan", None), P())
    return jax.shard_map(
        steps, mesh=mesh, in_specs=placed, out_specs=P("chan", "tm", None), check_vma=False
    )
```

profile of v0, /device:TPU:0, one launch (start us, length us, event | category | flops | bytes accessed | tf_op | source)
XLA Modules:
  0.0 34.0 jit_solution(10749298257523629581)
XLA Ops:
  0.0 0.0 copy-start
  0.0 0.9 %copy-done = bf16[1,256,512]{2,1,0:T(8,128)(2,1)S(1)} copy-done((bf16[1,256,512]{2,1,0:T(8,128)(2,1)S(1)}, bf16[1,256,512]{2,1,0:T(8,128)(2,1)}, u32[]{:S(2)}) %copy-start) | copy-done | bytes 262168
  1.0 0.0 copy-start.1
  1.0 0.5 %segment_gram.1 = (f32[128,256]{1,0:T(8,128)S(1)}, f32[128,256]{1,0:T(8,128)S(1)}, f32[8,128]{1,0:T(8,128)S(1)}) custom-call(s32[1]{0:T(128)} %bitcast.parity_ref, bf16[256,512]{1,0:T(8,128)(2,1)S(1)} %bitcast.3), custom_call_target="tpu_custom_call" | custom-call | flops 134217728 | bytes 262144 | tf_op jit(solution)/shard_map/segment_gram/pallas_call | solution.py:233
  1.4 3.0 %collective-permute-start = (f32[8,128]{1,0:T(8,128)S(1)}, f32[8,128]{1,0:T(8,128)S(1)}, u32[]{:S(2)}, u32[]{:S(2)}) collective-permute-start(f32[8,128]{1,0:T(8,128)S(1)} %get-tuple-element.11), channel_id=1, source_target_pairs={{0,8},{8,0},{16,24},{24,16},{1,9},{9,1},{17,25},{25,17},{2,10},{10... | collective-permute-start | bytes 12296 | tf_op jit(solution)/shard_map/ppermute | solution.py:183
  4.5 1.6 %collective-permute-done = f32[8,128]{1,0:T(8,128)S(1)} collective-permute-done((f32[8,128]{1,0:T(8,128)S(1)}, f32[8,128]{1,0:T(8,128)S(1)}, u32[]{:S(2)}, u32[]{:S(2)}) %collective-permute-start) | collective-permute-done | bytes 4128 | tf_op jit(solution)/shard_map/ppermute | solution.py:183
  6.0 2.0 %collective-permute-start.1 = (f32[8,128]{1,0:T(8,128)S(1)}, f32[8,128]{1,0:T(8,128)S(1)}, u32[]{:S(2)}, u32[]{:S(2)}) collective-permute-start(f32[8,128]{1,0:T(8,128)S(1)} %add.60), channel_id=1, source_target_pairs={{0,16},{8,24},{16,0},{24,8},{1,17},{9,25},{17,1},{25,9},{2,18},{10... | collective-permute-start | bytes 12296 | tf_op jit(solution)/shard_map/ppermute | solution.py:183
  8.1 0.0 collective-permute-start.5
  8.1 0.0 copy-start.2
  8.1 0.0 copy-start.3
  8.1 1.6 %collective-permute-done.1 = f32[8,128]{1,0:T(8,128)S(1)} collective-permute-done((f32[8,128]{1,0:T(8,128)S(1)}, f32[8,128]{1,0:T(8,128)S(1)}, u32[]{:S(2)}, u32[]{:S(2)}) %collective-permute-start.1) | collective-permute-done | bytes 4128 | tf_op jit(solution)/shard_map/ppermute | solution.py:183
  9.7 2.1 %collective-permute-start.2 = (f32[8,128]{1,0:T(8,128)S(1)}, f32[8,128]{1,0:T(8,128)S(1)}, u32[]{:S(2)}, u32[]{:S(2)}) collective-permute-start(f32[8,128]{1,0:T(8,128)S(1)} %add.61), channel_id=1, source_target_pairs={{0,2},{1,3},{2,0},{3,1},{4,6},{5,7},{6,4},{7,5},{8,10},{9,11},{10,... | collective-permute-start | bytes 12296 | tf_op jit(solution)/shard_map/ppermute | solution.py:183
  11.8 0.0 copy-done.1
  11.8 0.0 copy-done.2
  11.8 0.0 copy-done.3
  11.8 2.4 %null.1.w_ref = f32[256,512]{1,0:T(8,128)S(1)} custom-call(s32[1,8]{1,0:T(1,128)S(1)} %copy-done.2, f32[64]{0:T(128)S(1)} %copy-done.3, bf16[256,512]{1,0:T(8,128)(2,1)S(1)} %bitcast.4), custom_call_target="tpu_custom_call" | custom-call | flops 67108864 | bytes 786432 | tf_op jit(solution)/shard_map/null/pallas_call | solution.py:269
  14.1 0.0 collective-permute-done.2
  14.2 2.7 %collective-permute-start.3 = (f32[8,128]{1,0:T(8,128)S(1)}, f32[8,128]{1,0:T(8,128)S(1)}, u32[]{:S(2)}, u32[]{:S(2)}) collective-permute-start(f32[8,128]{1,0:T(8,128)S(1)} %multiply_add_fusion.5), channel_id=1, source_target_pairs={{0,4},{1,5},{2,6},{3,7},{4,0},{5,1},{6,2},{7,3},{8,12},{9,13},{10,... | collective-permute-start | bytes 12296 | tf_op jit(solution)/shard_map/ppermute | solution.py:183
  16.8 0.0 collective-permute-done.5
  16.8 1.2 %collective-permute-start.6 = (f32[128,256]{1,0:T(8,128)S(1)}, f32[128,256]{1,0:T(8,128)S(1)}, u32[]{:S(2)}, u32[]{:S(2)}) collective-permute-start(f32[128,256]{1,0:T(8,128)S(1)} %multiply_add_fusion.3), channel_id=1, source_target_pairs={{0,2},{1,3},{2,0},{3,1},{4,6},{5,7},{6,4},{7,5},{8,10},{9,11},{10,... | collective-permute-start | bytes 393224 | tf_op jit(solution)/shard_map/ppermute | solution.py:183
  18.1 0.8 %collective-permute-done.3 = f32[8,128]{1,0:T(8,128)S(1)} collective-permute-done((f32[8,128]{1,0:T(8,128)S(1)}, f32[8,128]{1,0:T(8,128)S(1)}, u32[]{:S(2)}, u32[]{:S(2)}) %collective-permute-start.3) | collective-permute-done | bytes 4128 | tf_op jit(solution)/shard_map/ppermute | solution.py:183
  18.8 0.0 collective-permute-start.4
  18.8 3.0 %collective-permute-done.6 = f32[128,256]{1,0:T(8,128)S(1)} collective-permute-done((f32[128,256]{1,0:T(8,128)S(1)}, f32[128,256]{1,0:T(8,128)S(1)}, u32[]{:S(2)}, u32[]{:S(2)}) %collective-permute-start.6) | collective-permute-done | bytes 131104 | tf_op jit(solution)/shard_map/ppermute | solution.py:183
  21.9 1.0 %collective-permute-start.7 = (f32[128,256]{1,0:T(8,128)S(1)}, f32[128,256]{1,0:T(8,128)S(1)}, u32[]{:S(2)}, u32[]{:S(2)}) collective-permute-start(f32[128,256]{1,0:T(8,128)S(1)} %multiply_add_fusion.2), channel_id=1, source_target_pairs={{0,6},{1,7},{2,4},{3,5},{4,2},{5,3},{6,0},{7,1},{8,14},{9,15},{10,... | collective-permute-start | bytes 393224 | tf_op jit(solution)/shard_map/ppermute | solution.py:183
  22.9 0.0 collective-permute-done.4
  22.9 5.9 %collective-permute-done.7 = f32[128,256]{1,0:T(8,128)S(1)} collective-permute-done((f32[128,256]{1,0:T(8,128)S(1)}, f32[128,256]{1,0:T(8,128)S(1)}, u32[]{:S(2)}, u32[]{:S(2)}) %collective-permute-start.7) | collective-permute-done | bytes 131104 | tf_op jit(solution)/shard_map/ppermute | solution.py:183
  28.8 0.1 broadcast_select_fusion
  28.9 0.1 collective-permute-start.8
  29.0 1.3 %collective-permute-done.8.other_ref = f32[128,256]{1,0:T(8,128)S(1)} collective-permute-done((f32[128,256]{1,0:T(8,128)S(1)}, f32[128,256]{1,0:T(8,128)S(1)}, u32[]{:S(2)}, u32[]{:S(2)}) %collective-permute-start.8) | collective-permute-done | bytes 131104 | tf_op jit(solution)/shard_map/ppermute | solution.py:183
  30.3 0.9 %square.1 = (f32[512,256]{1,0:T(8,128)S(1)}, f32[512,256]{1,0:T(8,128)S(1)}, f32[8,128]{1,0:T(8,128)S(1)}) custom-call(s32[1]{0:T(128)} %bitcast.parity_ref, f32[128,256]{1,0:T(8,128)S(1)} %get-tuple-element.18.own_ref, f32[128,256]{1,0:T(8,128)S(1)} %collective-permute-done.8.other_ref), custom_call_target="tpu_custom_call" | custom-call | flops 402653184 | bytes 1048576 | tf_op jit(solution)/shard_map/square/pallas_call | solution.py:281
  31.2 2.9 %whiten.1 = f32[256,512]{1,0:T(8,128)} custom-call(f32[8,128]{1,0:T(8,128)S(1)} %fusion.2.band_ref, f32[8,128]{1,0:T(8,128)S(1)} %get-tuple-element.14.stats_ref, f32[512,256]{1,0:T(8,128)S(1)} %get-tuple-element.15.cov_ref, f32[512,256]{1,0:T(8,128)S(1)} %get-tuple-element.16.square_ref, f32[256,512]{1,0:T(8,128)S(1)} %null.1.w_ref), custom_call_target="tpu_custom_call" | custom-call | flops 805306368 | bytes 1048576 | tf_op jit(solution)/shard_map/whiten/pallas_call | solution.py:298
  (9 shorter events, 0.1 us)
Async XLA Ops:
  0.0 0.9 %copy-start = (bf16[1,256,512]{2,1,0:T(8,128)(2,1)S(1)}, bf16[1,256,512]{2,1,0:T(8,128)(2,1)}, u32[]{:S(2)}) copy-start(bf16[1,256,512]{2,1,0:T(8,128)(2,1)} %param.3) | copy-start | bytes 786436
  1.0 10.8 %copy-start.1 = (bf16[1,256,512]{2,1,0:T(8,128)(2,1)S(1)}, bf16[1,256,512]{2,1,0:T(8,128)(2,1)}, u32[]{:S(2)}) copy-start(bf16[1,256,512]{2,1,0:T(8,128)(2,1)} %param.3) | copy-start | bytes 786436
  1.4 4.6 %collective-permute-start = (f32[8,128]{1,0:T(8,128)S(1)}, f32[8,128]{1,0:T(8,128)S(1)}, u32[]{:S(2)}, u32[]{:S(2)}) collective-permute-start(f32[8,128]{1,0:T(8,128)S(1)} %get-tuple-element.11), channel_id=1, source_target_pairs={{0,8},{8,0},{16,24},{24,16},{1,9},{9,1},{17,25},{25,17},{2,10},{10... | collective-permute-start | bytes 12296 | tf_op jit(solution)/shard_map/ppermute | solution.py:183
  6.0 3.6 %collective-permute-start.1 = (f32[8,128]{1,0:T(8,128)S(1)}, f32[8,128]{1,0:T(8,128)S(1)}, u32[]{:S(2)}, u32[]{:S(2)}) collective-permute-start(f32[8,128]{1,0:T(8,128)S(1)} %add.60), channel_id=1, source_target_pairs={{0,16},{8,24},{16,0},{24,8},{1,17},{9,25},{17,1},{25,9},{2,18},{10... | collective-permute-start | bytes 12296 | tf_op jit(solution)/shard_map/ppermute | solution.py:183
  8.1 8.7 %collective-permute-start.5 = (f32[128,256]{1,0:T(8,128)S(1)}, f32[128,256]{1,0:T(8,128)S(1)}, u32[]{:S(2)}, u32[]{:S(2)}) collective-permute-start(f32[128,256]{1,0:T(8,128)S(1)} %get-tuple-element.13), channel_id=1, source_target_pairs={{0,1},{1,0},{2,3},{3,2},{4,5},{5,4},{6,7},{7,6},{8,9},{9,8},{10,11... | collective-permute-start | bytes 393224 | tf_op jit(solution)/shard_map/ppermute | solution.py:183
  8.1 3.7 %copy-start.2 = (s32[1,8]{1,0:T(1,128)S(1)}, s32[1,8]{1,0:T(1,128)}, u32[]{:S(2)}) copy-start(s32[1,8]{1,0:T(1,128)} %picks_ref.1) | copy-start | bytes 100
  8.1 3.7 %copy-start.3 = (f32[64]{0:T(128)S(1)}, f32[64]{0:T(128)}, u32[]{:S(2)}) copy-start(f32[64]{0:T(128)} %angles_ref.1) | copy-start | bytes 772
  9.7 4.5 %collective-permute-start.2 = (f32[8,128]{1,0:T(8,128)S(1)}, f32[8,128]{1,0:T(8,128)S(1)}, u32[]{:S(2)}, u32[]{:S(2)}) collective-permute-start(f32[8,128]{1,0:T(8,128)S(1)} %add.61), channel_id=1, source_target_pairs={{0,2},{1,3},{2,0},{3,1},{4,6},{5,7},{6,4},{7,5},{8,10},{9,11},{10,... | collective-permute-start | bytes 12296 | tf_op jit(solution)/shard_map/ppermute | solution.py:183
  14.2 4.7 %collective-permute-start.3 = (f32[8,128]{1,0:T(8,128)S(1)}, f32[8,128]{1,0:T(8,128)S(1)}, u32[]{:S(2)}, u32[]{:S(2)}) collective-permute-start(f32[8,128]{1,0:T(8,128)S(1)} %multiply_add_fusion.5), channel_id=1, source_target_pairs={{0,4},{1,5},{2,6},{3,7},{4,0},{5,1},{6,2},{7,3},{8,12},{9,13},{10,... | collective-permute-start | bytes 12296 | tf_op jit(solution)/shard_map/ppermute | solution.py:183
  16.8 5.0 %collective-permute-start.6 = (f32[128,256]{1,0:T(8,128)S(1)}, f32[128,256]{1,0:T(8,128)S(1)}, u32[]{:S(2)}, u32[]{:S(2)}) collective-permute-start(f32[128,256]{1,0:T(8,128)S(1)} %multiply_add_fusion.3), channel_id=1, source_target_pairs={{0,2},{1,3},{2,0},{3,1},{4,6},{5,7},{6,4},{7,5},{8,10},{9,11},{10,... | collective-permute-start | bytes 393224 | tf_op jit(solution)/shard_map/ppermute | solution.py:183
  18.8 4.1 %collective-permute-start.4 = (f32[16,128]{1,0:T(8,128)S(1)}, f32[16,128]{1,0:T(8,128)S(1)}, u32[]{:S(2)}, u32[]{:S(2)}) collective-permute-start(f32[16,128]{1,0:T(8,128)S(1)} %pad_maximum_fusion), channel_id=1, source_target_pairs={{0,1},{1,0},{2,3},{3,2},{4,5},{5,4},{6,7},{7,6},{8,9},{9,8},{10,11... | collective-permute-start | bytes 24584 | tf_op jit(solution)/shard_map/ppermute | solution.py:183
  21.9 6.9 %collective-permute-start.7 = (f32[128,256]{1,0:T(8,128)S(1)}, f32[128,256]{1,0:T(8,128)S(1)}, u32[]{:S(2)}, u32[]{:S(2)}) collective-permute-start(f32[128,256]{1,0:T(8,128)S(1)} %multiply_add_fusion.2), channel_id=1, source_target_pairs={{0,6},{1,7},{2,4},{3,5},{4,2},{5,3},{6,0},{7,1},{8,14},{9,15},{10,... | collective-permute-start | bytes 393224 | tf_op jit(solution)/shard_map/ppermute | solution.py:183
  28.9 1.4 %collective-permute-start.8 = (f32[128,256]{1,0:T(8,128)S(1)}, f32[128,256]{1,0:T(8,128)S(1)}, u32[]{:S(2)}, u32[]{:S(2)}) collective-permute-start(f32[128,256]{1,0:T(8,128)S(1)} %get-tuple-element.17), channel_id=1, source_target_pairs={{0,1},{1,0},{2,3},{3,2},{4,5},{5,4},{6,7},{7,6},{8,9},{9,8},{10,11... | collective-permute-start | bytes 393224 | tf_op jit(solution)/shard_map/ppermute | solution.py:183
where the time goes:
time: 34.2 us; the launch traced here: 34 us
  waiting for transfers between devices  14.2 us (42%)
  starting transfers between devices  12.1 us (35%)
  Pallas kernels  6.54 us (19%)
  local copies, waits for them, and re-layouts  0.96 us (3%)
    ppermute x9, waiting for transfers between devices, exchange(): lax.ppermute(value, axis, [(i, i ^ mask) for i in range(lax.axis_size(axi...  14.2 us
    ppermute x9, starting transfers between devices, exchange(): lax.ppermute(value, axis, [(i, i ^ mask) for i in range(lax.axis_size(axi...  12.1 us
    pallas_call x1, Pallas kernels, steps(): pl.pallas_call(whiten_kernel, out_shape=jax.ShapeDtypeStruct((rows, width...  2.86 us
    pallas_call x1, Pallas kernels, steps(): pl.pallas_call(null_kernel, out_shape=jax.ShapeDtypeStruct((rows, width),...  2.36 us
    unnamed x8, local copies, waits for them, and re-layouts  0.96 us
    pallas_call x1, Pallas kernels, steps(): pl.pallas_call(square_kernel, out_shape=(jax.ShapeDtypeStruct((width, ant...  0.87 us
  transfers between devices with their start and end apart: 9, of which 6 were waited for; matrix products, arithmetic and copies ran while one was open for 0% of the time, Pallas kernels for 7%

commit v1 on v0

--- a/solution.py
+++ b/solution.py
@@ -8,6 +8,7 @@
 
 SEG = 256
 HORIZON = 256
+DIRECT = 4
 LOADING = 0.1
 STEER_LOADING = 0.05
 TINY_LEVEL = 1e-06
@@ -190,21 +191,42 @@
     return chosen
 
 
-def earlier_chips(value, decay, mirrored):
+def earlier_chips(value, decay, mirrored=False, rider=None):
     chips = lax.axis_size("tm") // 2
     chip = lax.axis_index("tm") // 2
     length, total, before = 1, value, None
     while length < chips:
+        last = 2 * length == chips
         mask = 2 * length - 1 if mirrored else length
+        rows = total.shape[0]
+        if last and rider is not None:
+            total = jnp.concatenate([total, rider], axis=0)
         got = exchange(total, "tm", 2 * mask)
+        if last and rider is not None:
+            got, rider = got[:rows], got[rows:]
         upper = (chip // length) % 2 == 1
         weight = jnp.where(upper, choose(chip % length, [decay**i for i in range(length)]), 0.0)
         before = weight * got if before is None else before + weight * got
-        if 2 * length < chips:
+        if not last:
             far = decay**length
             total = jnp.where(upper, 1.0, far) * total + jnp.where(upper, far, 1.0) * got
         length *= 2
-    return jnp.zeros_like(value) if before is None else before
+    before = jnp.zeros_like(value) if before is None else before
+    return before if rider is None else (before, rider)
+
+
+def earlier_levels(level, opposite, decay):
+    chips = lax.axis_size("tm") // 2
+    chip = lax.axis_index("tm") // 2
+    before = 0.0
+    for mask in range(1, chips):
+        if mask == chips - 1:
+            got = opposite
+        else:
+            got = exchange(level, "tm", 2 * mask)
+        weights = [decay ** (c - 1 - (c ^ mask)) if c ^ mask < c else 0.0 for c in range(chips)]
+        before = before + choose(chip, weights) * got
+    return before
 
 
 def sum_groups(value):
@@ -250,14 +272,20 @@
     got = exchange(give, "tm", 1)
     mine, theirs = jnp.where(is_odd, 1.0, decay), jnp.where(is_odd, decay, 1.0)
     pair = mine * keep + theirs * got
-    before = earlier_chips(pair, decay * decay, True)
+    level = sum_groups(power)
+    direct = lax.axis_size("tm") // 2 == DIRECT
+    if direct:
+        wide = jnp.concatenate([level] * (antennas // level.shape[1]), axis=1)
+        before, opposite = earlier_chips(pair, decay * decay, True, wide)
+        level_before = earlier_levels(level, opposite[:, : level.shape[1]], decay * decay)
+    else:
+        before = earlier_chips(pair, decay * decay, True)
+        level_before = earlier_chips(level, decay * decay)
     even_cov = decay * before + jnp.where(is_odd, got, keep)
     odd_cov = decay * decay * before + pair
     own = jnp.where(is_odd, odd_cov, even_cov)
     other = exchange(jnp.where(is_odd, even_cov, odd_cov), "tm", 1)
 
-    level = sum_groups(power)
-    level_before = earlier_chips(level, decay * decay, False)
     levels = jnp.concatenate([level, level_before], axis=0)
     got_levels = exchange(levels, "tm", 1)
     level_even = jnp.where(is_odd, got_levels, levels)

time: 34.2 us -> 26.4 us (0.77)
  waiting for transfers between devices: 14.2 us -> 6.85 us
  starting transfers between devices: 12.1 us -> 11.6 us
    ppermute x9, waiting for transfers between devices: 14.2 us -> 6.85 us  [exchange(): lax.ppermute(value, axis, [(i, i ^ mask) for i in range(lax.axis_size(axi...]
    ppermute x9, starting transfers between devices: 12.1 us -> 11.6 us  [exchange(): lax.ppermute(value, axis, [(i, i ^ mask) for i in range(lax.axis_size(axi...]
  transfers between devices with their start and end apart: 9 -> 9, of which waited for: 6 -> 6; matrix products, arithmetic and copies ran while one was open for 0% -> 0% of each run, Pallas kernels for 7% -> 9%
where the time goes in v1:
time: 26.4 us; the launch traced here: 26.2 us
  starting transfers between devices  11.6 us (44%)
  waiting for transfers between devices  6.85 us (26%)
  Pallas kernels  6.55 us (25%)
  local copies, waits for them, and re-layouts  0.96 us (4%)
    ppermute x9, starting transfers between devices, exchange(): lax.ppermute(value, axis, [(i, i ^ mask) for i in range(lax.axis_size(axi...  11.6 us
    ppermute x9, waiting for transfers between devices, exchange(): lax.ppermute(value, axis, [(i, i ^ mask) for i in range(lax.axis_size(axi...  6.85 us
    pallas_call x1, Pallas kernels, steps(): pl.pallas_call(whiten_kernel, out_shape=jax.ShapeDtypeStruct((rows, width...  2.86 us
    pallas_call x1, Pallas kernels, steps(): pl.pallas_call(null_kernel, out_shape=jax.ShapeDtypeStruct((rows, width),...  2.36 us
    unnamed x8, local copies, waits for them, and re-layouts  0.96 us
    pallas_call x1, Pallas kernels, steps(): pl.pallas_call(square_kernel, out_shape=(jax.ShapeDtypeStruct((width, ant...  0.87 us
  transfers between devices with their start and end apart: 9, of which 6 were waited for; matrix products, arithmetic and copies ran while one was open for 0% of the time, Pallas kernels for 9%

profile of v1, /device:TPU:0, one launch (start us, length us, event | category | flops | bytes accessed | tf_op | source)
XLA Modules:
  0.0 26.2 jit_solution(9439419056573340185)
XLA Ops:
  0.0 0.0 copy-start
  0.0 0.9 %copy-done = bf16[1,256,512]{2,1,0:T(8,128)(2,1)S(1)} copy-done((bf16[1,256,512]{2,1,0:T(8,128)(2,1)S(1)}, bf16[1,256,512]{2,1,0:T(8,128)(2,1)}, u32[]{:S(2)}) %copy-start) | copy-done | bytes 262168
  1.0 0.5 %segment_gram.1 = (f32[128,256]{1,0:T(8,128)S(1)}, f32[128,256]{1,0:T(8,128)S(1)}, f32[8,128]{1,0:T(8,128)S(1)}) custom-call(s32[1]{0:T(128)} %bitcast.parity_ref, bf16[256,512]{1,0:T(8,128)(2,1)S(1)} %bitcast.3), custom_call_target="tpu_custom_call" | custom-call | flops 134217728 | bytes 262144 | tf_op jit(solution)/shard_map/segment_gram/pallas_call | solution.py:255
  1.4 0.6 %collective-permute-start.4 = (f32[128,256]{1,0:T(8,128)S(1)}, f32[128,256]{1,0:T(8,128)S(1)}, u32[]{:S(2)}, u32[]{:S(2)}) collective-permute-start(f32[128,256]{1,0:T(8,128)S(1)} %get-tuple-element.13), channel_id=1, source_target_pairs={{0,1},{1,0},{2,3},{3,2},{4,5},{5,4},{6,7},{7,6},{8,9},{9,8},{10,11... | collective-permute-start | bytes 393224 | tf_op jit(solution)/shard_map/ppermute | solution.py:184
  2.0 1.0 %collective-permute-done.4 = f32[128,256]{1,0:T(8,128)S(1)} collective-permute-done((f32[128,256]{1,0:T(8,128)S(1)}, f32[128,256]{1,0:T(8,128)S(1)}, u32[]{:S(2)}, u32[]{:S(2)}) %collective-permute-start.4) | collective-permute-done | bytes 131104 | tf_op jit(solution)/shard_map/ppermute | solution.py:184
  3.0 3.0 %collective-permute-start.5 = (f32[128,256]{1,0:T(8,128)S(1)}, f32[128,256]{1,0:T(8,128)S(1)}, u32[]{:S(2)}, u32[]{:S(2)}) collective-permute-start(f32[128,256]{1,0:T(8,128)S(1)} %multiply_add_fusion.2), channel_id=1, source_target_pairs={{0,2},{1,3},{2,0},{3,1},{4,6},{5,7},{6,4},{7,5},{8,10},{9,11},{10,... | collective-permute-start | bytes 393224 | tf_op jit(solution)/shard_map/ppermute | solution.py:184
  6.0 1.5 %collective-permute-start = (f32[8,128]{1,0:T(8,128)S(1)}, f32[8,128]{1,0:T(8,128)S(1)}, u32[]{:S(2)}, u32[]{:S(2)}) collective-permute-start(f32[8,128]{1,0:T(8,128)S(1)} %get-tuple-element.11), channel_id=1, source_target_pairs={{0,8},{8,0},{16,24},{24,16},{1,9},{9,1},{17,25},{25,17},{2,10},{10... | collective-permute-start | bytes 12296 | tf_op jit(solution)/shard_map/ppermute | solution.py:184
  7.5 2.1 %collective-permute-done = f32[8,128]{1,0:T(8,128)S(1)} collective-permute-done((f32[8,128]{1,0:T(8,128)S(1)}, f32[8,128]{1,0:T(8,128)S(1)}, u32[]{:S(2)}, u32[]{:S(2)}) %collective-permute-start) | collective-permute-done | bytes 4128 | tf_op jit(solution)/shard_map/ppermute | solution.py:184
  9.6 1.5 %collective-permute-start.1 = (f32[8,128]{1,0:T(8,128)S(1)}, f32[8,128]{1,0:T(8,128)S(1)}, u32[]{:S(2)}, u32[]{:S(2)}) collective-permute-start(f32[8,128]{1,0:T(8,128)S(1)} %add.57), channel_id=1, source_target_pairs={{0,16},{8,24},{16,0},{24,8},{1,17},{9,25},{17,1},{25,9},{2,18},{10... | collective-permute-start | bytes 12296 | tf_op jit(solution)/shard_map/ppermute | solution.py:184
  11.1 2.1 %collective-permute-done.1 = f32[8,128]{1,0:T(8,128)S(1)} collective-permute-done((f32[8,128]{1,0:T(8,128)S(1)}, f32[8,128]{1,0:T(8,128)S(1)}, u32[]{:S(2)}, u32[]{:S(2)}) %collective-permute-start.1) | collective-permute-done | bytes 4128 | tf_op jit(solution)/shard_map/ppermute | solution.py:184
  13.2 0.0 collective-permute-done.5
  13.2 0.0 copy-start.1
  13.2 2.5 %collective-permute-start.6 = (f32[136,256]{1,0:T(8,128)S(1)}, f32[136,256]{1,0:T(8,128)S(1)}, u32[]{:S(2)}, u32[]{:S(2)}) collective-permute-start(f32[136,256]{1,0:T(8,128)S(1)} %maximum_maximum_fusion), channel_id=1, source_target_pairs={{0,6},{1,7},{2,4},{3,5},{4,2},{5,3},{6,0},{7,1},{8,14},{9,15},{10,... | collective-permute-start | bytes 417800 | tf_op jit(solution)/shard_map/ppermute | solution.py:184
  15.8 0.0 copy-start.2
  15.8 0.0 copy-start.3
  15.8 0.3 %collective-permute-start.3 = (f32[8,128]{1,0:T(8,128)S(1)}, f32[8,128]{1,0:T(8,128)S(1)}, u32[]{:S(2)}, u32[]{:S(2)}) collective-permute-start(f32[8,128]{1,0:T(8,128)S(1)} %add.58), channel_id=1, source_target_pairs={{0,4},{1,5},{2,6},{3,7},{4,0},{5,1},{6,2},{7,3},{8,12},{9,13},{10,... | collective-permute-start | bytes 12296 | tf_op jit(solution)/shard_map/ppermute | solution.py:184
  16.1 1.6 %collective-permute-start.2 = (f32[8,128]{1,0:T(8,128)S(1)}, f32[8,128]{1,0:T(8,128)S(1)}, u32[]{:S(2)}, u32[]{:S(2)}) collective-permute-start(f32[8,128]{1,0:T(8,128)S(1)} %add.58), channel_id=1, source_target_pairs={{0,2},{1,3},{2,0},{3,1},{4,6},{5,7},{6,4},{7,5},{8,10},{9,11},{10,... | collective-permute-start | bytes 12296 | tf_op jit(solution)/shard_map/ppermute | solution.py:184
  17.7 0.0 copy-done.1
  17.7 0.0 copy-done.2
  17.7 0.0 copy-done.3
  17.7 2.4 %null.1.w_ref = f32[256,512]{1,0:T(8,128)S(1)} custom-call(s32[1,8]{1,0:T(1,128)S(1)} %copy-done.2, f32[64]{0:T(128)S(1)} %copy-done.3, bf16[256,512]{1,0:T(8,128)(2,1)S(1)} %bitcast.4), custom_call_target="tpu_custom_call" | custom-call | flops 67108864 | bytes 786432 | tf_op jit(solution)/shard_map/null/pallas_call | solution.py:297
  20.1 0.7 %collective-permute-done.3 = f32[8,128]{1,0:T(8,128)S(1)} collective-permute-done((f32[8,128]{1,0:T(8,128)S(1)}, f32[8,128]{1,0:T(8,128)S(1)}, u32[]{:S(2)}, u32[]{:S(2)}) %collective-permute-start.3) | collective-permute-done | bytes 4128 | tf_op jit(solution)/shard_map/ppermute | solution.py:184
  20.8 0.0 collective-permute-done.2
  20.8 0.0 collective-permute-done.6
  20.8 0.1 collective-permute-start.7
  20.9 0.1 broadcast_select_fusion
  21.0 0.6 %collective-permute-start.8 = (f32[128,256]{1,0:T(8,128)S(1)}, f32[128,256]{1,0:T(8,128)S(1)}, u32[]{:S(2)}, u32[]{:S(2)}) collective-permute-start(f32[128,256]{1,0:T(8,128)S(1)} %get-tuple-element.17), channel_id=1, source_target_pairs={{0,1},{1,0},{2,3},{3,2},{4,5},{5,4},{6,7},{7,6},{8,9},{9,8},{10,11... | collective-permute-start | bytes 393224 | tf_op jit(solution)/shard_map/ppermute | solution.py:184
  21.5 0.5 %collective-permute-done.7 = f32[16,128]{1,0:T(8,128)S(1)} collective-permute-done((f32[16,128]{1,0:T(8,128)S(1)}, f32[16,128]{1,0:T(8,128)S(1)}, u32[]{:S(2)}, u32[]{:S(2)}) %collective-permute-start.7) | collective-permute-done | bytes 8224 | tf_op jit(solution)/shard_map/ppermute | solution.py:184
  22.1 0.4 %collective-permute-done.8.other_ref = f32[128,256]{1,0:T(8,128)S(1)} collective-permute-done((f32[128,256]{1,0:T(8,128)S(1)}, f32[128,256]{1,0:T(8,128)S(1)}, u32[]{:S(2)}, u32[]{:S(2)}) %collective-permute-start.8) | collective-permute-done | bytes 131104 | tf_op jit(solution)/shard_map/ppermute | solution.py:184
  22.5 0.9 %square.1 = (f32[512,256]{1,0:T(8,128)S(1)}, f32[512,256]{1,0:T(8,128)S(1)}, f32[8,128]{1,0:T(8,128)S(1)}) custom-call(s32[1]{0:T(128)} %bitcast.parity_ref, f32[128,256]{1,0:T(8,128)S(1)} %get-tuple-element.18.own_ref, f32[128,256]{1,0:T(8,128)S(1)} %collective-permute-done.8.other_ref), custom_call_target="tpu_custom_call" | custom-call | flops 402653184 | bytes 1048576 | tf_op jit(solution)/shard_map/square/pallas_call | solution.py:309
  23.4 2.9 %whiten.1 = f32[256,512]{1,0:T(8,128)} custom-call(f32[8,128]{1,0:T(8,128)S(1)} %fusion.3.band_ref, f32[8,128]{1,0:T(8,128)S(1)} %get-tuple-element.14.stats_ref, f32[512,256]{1,0:T(8,128)S(1)} %get-tuple-element.15.cov_ref, f32[512,256]{1,0:T(8,128)S(1)} %get-tuple-element.16.square_ref, f32[256,512]{1,0:T(8,128)S(1)} %null.1.w_ref), custom_call_target="tpu_custom_call" | custom-call | flops 805306368 | bytes 1048576 | tf_op jit(solution)/shard_map/whiten/pallas_call | solution.py:326
  (9 shorter events, 0.1 us)
Async XLA Ops:
  0.0 0.9 %copy-start = (bf16[1,256,512]{2,1,0:T(8,128)(2,1)S(1)}, bf16[1,256,512]{2,1,0:T(8,128)(2,1)}, u32[]{:S(2)}) copy-start(bf16[1,256,512]{2,1,0:T(8,128)(2,1)} %param.3) | copy-start | bytes 786436
  1.4 1.5 %collective-permute-start.4 = (f32[128,256]{1,0:T(8,128)S(1)}, f32[128,256]{1,0:T(8,128)S(1)}, u32[]{:S(2)}, u32[]{:S(2)}) collective-permute-start(f32[128,256]{1,0:T(8,128)S(1)} %get-tuple-element.13), channel_id=1, source_target_pairs={{0,1},{1,0},{2,3},{3,2},{4,5},{5,4},{6,7},{7,6},{8,9},{9,8},{10,11... | collective-permute-start | bytes 393224 | tf_op jit(solution)/shard_map/ppermute | solution.py:184
  3.0 10.2 %collective-permute-start.5 = (f32[128,256]{1,0:T(8,128)S(1)}, f32[128,256]{1,0:T(8,128)S(1)}, u32[]{:S(2)}, u32[]{:S(2)}) collective-permute-start(f32[128,256]{1,0:T(8,128)S(1)} %multiply_add_fusion.2), channel_id=1, source_target_pairs={{0,2},{1,3},{2,0},{3,1},{4,6},{5,7},{6,4},{7,5},{8,10},{9,11},{10,... | collective-permute-start | bytes 393224 | tf_op jit(solution)/shard_map/ppermute | solution.py:184
  6.0 3.6 %collective-permute-start = (f32[8,128]{1,0:T(8,128)S(1)}, f32[8,128]{1,0:T(8,128)S(1)}, u32[]{:S(2)}, u32[]{:S(2)}) collective-permute-start(f32[8,128]{1,0:T(8,128)S(1)} %get-tuple-element.11), channel_id=1, source_target_pairs={{0,8},{8,0},{16,24},{24,16},{1,9},{9,1},{17,25},{25,17},{2,10},{10... | collective-permute-start | bytes 12296 | tf_op jit(solution)/shard_map/ppermute | solution.py:184
  9.6 3.6 %collective-permute-start.1 = (f32[8,128]{1,0:T(8,128)S(1)}, f32[8,128]{1,0:T(8,128)S(1)}, u32[]{:S(2)}, u32[]{:S(2)}) collective-permute-start(f32[8,128]{1,0:T(8,128)S(1)} %add.57), channel_id=1, source_target_pairs={{0,16},{8,24},{16,0},{24,8},{1,17},{9,25},{17,1},{25,9},{2,18},{10... | collective-permute-start | bytes 12296 | tf_op jit(solution)/shard_map/ppermute | solution.py:184
  13.2 4.5 %copy-start.1 = (bf16[1,256,512]{2,1,0:T(8,128)(2,1)S(1)}, bf16[1,256,512]{2,1,0:T(8,128)(2,1)}, u32[]{:S(2)}) copy-start(bf16[1,256,512]{2,1,0:T(8,128)(2,1)} %param.3) | copy-start | bytes 786436
  13.2 7.5 %collective-permute-start.6 = (f32[136,256]{1,0:T(8,128)S(1)}, f32[136,256]{1,0:T(8,128)S(1)}, u32[]{:S(2)}, u32[]{:S(2)}) collective-permute-start(f32[136,256]{1,0:T(8,128)S(1)} %maximum_maximum_fusion), channel_id=1, source_target_pairs={{0,6},{1,7},{2,4},{3,5},{4,2},{5,3},{6,0},{7,1},{8,14},{9,15},{10,... | collective-permute-start | bytes 417800 | tf_op jit(solution)/shard_map/ppermute | solution.py:184
  15.8 1.9 %copy-start.2 = (s32[1,8]{1,0:T(1,128)S(1)}, s32[1,8]{1,0:T(1,128)}, u32[]{:S(2)}) copy-start(s32[1,8]{1,0:T(1,128)} %picks_ref.1) | copy-start | bytes 100
  15.8 1.9 %copy-start.3 = (f32[64]{0:T(128)S(1)}, f32[64]{0:T(128)}, u32[]{:S(2)}) copy-start(f32[64]{0:T(128)} %angles_ref.1) | copy-start | bytes 772
  15.8 5.0 %collective-permute-start.3 = (f32[8,128]{1,0:T(8,128)S(1)}, f32[8,128]{1,0:T(8,128)S(1)}, u32[]{:S(2)}, u32[]{:S(2)}) collective-permute-start(f32[8,128]{1,0:T(8,128)S(1)} %add.58), channel_id=1, source_target_pairs={{0,4},{1,5},{2,6},{3,7},{4,0},{5,1},{6,2},{7,3},{8,12},{9,13},{10,... | collective-permute-start | bytes 12296 | tf_op jit(solution)/shard_map/ppermute | solution.py:184
  16.1 4.7 %collective-permute-start.2 = (f32[8,128]{1,0:T(8,128)S(1)}, f32[8,128]{1,0:T(8,128)S(1)}, u32[]{:S(2)}, u32[]{:S(2)}) collective-permute-start(f32[8,128]{1,0:T(8,128)S(1)} %add.58), channel_id=1, source_target_pairs={{0,2},{1,3},{2,0},{3,1},{4,6},{5,7},{6,4},{7,5},{8,10},{9,11},{10,... | collective-permute-start | bytes 12296 | tf_op jit(solution)/shard_map/ppermute | solution.py:184
  20.8 1.2 %collective-permute-start.7 = (f32[16,128]{1,0:T(8,128)S(1)}, f32[16,128]{1,0:T(8,128)S(1)}, u32[]{:S(2)}, u32[]{:S(2)}) collective-permute-start(f32[16,128]{1,0:T(8,128)S(1)} %pad_maximum_fusion), channel_id=1, source_target_pairs={{0,1},{1,0},{2,3},{3,2},{4,5},{5,4},{6,7},{7,6},{8,9},{9,8},{10,11... | collective-permute-start | bytes 24584 | tf_op jit(solution)/shard_map/ppermute | solution.py:184
  21.0 1.5 %collective-permute-start.8 = (f32[128,256]{1,0:T(8,128)S(1)}, f32[128,256]{1,0:T(8,128)S(1)}, u32[]{:S(2)}, u32[]{:S(2)}) collective-permute-start(f32[128,256]{1,0:T(8,128)S(1)} %get-tuple-element.17), channel_id=1, source_target_pairs={{0,1},{1,0},{2,3},{3,2},{4,5},{5,4},{6,7},{7,6},{8,9},{9,8},{10,11... | collective-permute-start | bytes 393224 | tf_op jit(solution)/shard_map/ppermute | solution.py:184

commit v2 on v1

--- a/solution.py
+++ b/solution.py
@@ -8,6 +8,7 @@
 
 SEG = 256
 HORIZON = 256
+CHUNKS = 4
 DIRECT = 4
 LOADING = 0.1
 STEER_LOADING = 0.05
@@ -67,36 +68,44 @@
     return jnp.concatenate([first, second], axis=0)
 
 
+def turn(u, v):
+    parts = zip(split(u), split(v), strict=True)
+    return tuple(over(beside(p, q), beside(q, -p)) for p, q in parts)
+
+
 def square_kernel(parity_ref, own_ref, other_ref, cov_ref, square_ref, stats_ref, mixed_ref):
     half, antennas = own_ref.shape
     parity = parity_ref[0]
     mixed_ref[pl.ds(pl.multiple_of(parity * half, half), half), :] = own_ref[...]
     mixed_ref[pl.ds(pl.multiple_of((1 - parity) * half, half), half), :] = other_ref[...]
     mixed = mixed_ref[...]
-    row = lax.broadcasted_iota(jnp.int32, mixed.shape, 0)
-    column = lax.broadcasted_iota(jnp.int32, mixed.shape, 1)
-    trace = jnp.sum(jnp.where(row == column, mixed, 0.0), keepdims=True)
-    unit = 1.0 / (trace / antennas + TINY_LEVEL)
-    mixed = mixed * unit
     flipped = mixed.T
     re, im = 0.5 * (mixed + flipped), 0.5 * (mixed - flipped)
     cov_ref[:antennas, :], cov_ref[antennas:, :] = re, im
     (rh, rl), (ih, il) = split(re), split(im)
     full = tuple(over(beside(r, -i), beside(i, r)) for r, i in ((rh, ih), (rl, il)))
     square_ref[...] = dot3(full, (over(rh, ih), over(rl, il)))
+    row = lax.broadcasted_iota(jnp.int32, mixed.shape, 0)
+    column = lax.broadcasted_iota(jnp.int32, mixed.shape, 1)
+    trace = jnp.sum(jnp.where(row == column, mixed, 0.0), keepdims=True)
     norm = jnp.sum(mixed * mixed, keepdims=True)
-    lane = lax.broadcasted_iota(jnp.int32, stats_ref.shape, 1)
-    stats_ref[...] = jnp.where(lane == 0, norm, jnp.where(lane == 1, trace * unit, unit))
-
-
-def whiten_kernel(band_ref, stats_ref, cov_ref, square_ref, w_ref, out_ref):
+    stats_ref[:8, :] = jnp.broadcast_to(norm, (8, stats_ref.shape[1]))
+    stats_ref[8:, :] = jnp.broadcast_to(trace, (8, stats_ref.shape[1]))
+
+
+def whiten_kernel(
+    band_ref, stats_ref, cov_ref, square_ref, w_ref, high_ref, low_ref, out_ref, done_ref, sems
+):
     samples = w_ref.shape[0]
     antennas = cov_ref.shape[1]
-    norm, trace, unit = stats_ref[0:1, 0:1], stats_ref[0:1, 1:2], stats_ref[0:1, 2:3]
-    beta = 1.0 / (unit * band_ref[0:1, 0:1])
-    total = 2.0 * (
-        beta * (beta * norm + 2.0 * LOADING * trace) + LOADING * LOADING * antennas
-    )
+    size = samples // CHUNKS
+
+    def wide(row):
+        return jnp.concatenate([row] * (antennas // row.shape[1]), axis=1)
+
+    norm, trace, band = wide(stats_ref[0:1, :]), wide(stats_ref[8:9, :]), wide(band_ref[0:1, :])
+    beta = 1.0 / band
+    total = 2.0 * (beta * (beta * norm + 2.0 * LOADING * trace) + LOADING * LOADING * antennas)
     omega = 1.0 / jnp.sqrt(total)
     slope, shift = omega * beta, omega * LOADING
     cov, square = cov_ref[...], square_ref[...]
@@ -104,19 +113,19 @@
     first = split(bend + (2.0 * slope * (shift - 1.0)) * cov)
     second = split((slope * (3.0 - 2.0 * shift)) * cov - bend)
     left, right = slice(0, antennas), slice(antennas, 2 * antennas)
-
-    def turn(u, v):
-        parts = zip(split(u), split(v), strict=True)
-        return tuple(over(beside(p, q), beside(q, -p)) for p, q in parts)
-
-    w_u, w_v = w_ref[:, left], w_ref[:, right]
-    step = dot3(turn(w_u, w_v), first)
-    keep = 2.0 + shift * (shift - 2.0)
-    u, v = keep * w_u + step[:samples], keep * w_v + step[samples:]
-    step = dot3(turn(u, v), second)
-    keep = 2.0 - shift * (3.0 - shift)
-    out_ref[:, left] = omega * (w_u + keep * u - step[:samples])
-    out_ref[:, right] = omega * (w_v + keep * v - step[samples:])
+    keep_first, keep_second = 2.0 + shift * (shift - 2.0), 2.0 - shift * (3.0 - shift)
+    for n in range(CHUNKS):
+        rows, both = slice(n * size, (n + 1) * size), slice(2 * n * size, 2 * (n + 1) * size)
+        w_u, w_v = w_ref[rows, left], w_ref[rows, right]
+        step = dot3((high_ref[both, :], low_ref[both, :]), first)
+        u, v = keep_first * w_u + step[:size], keep_first * w_v + step[size:]
+        step = dot3(turn(u, v), second)
+        done_ref[rows, left] = omega * (w_u + keep_second * u - step[:size])
+        done_ref[rows, right] = omega * (w_v + keep_second * v - step[size:])
+        pltpu.make_async_copy(done_ref.at[rows], out_ref.at[rows], sems.at[n]).start()
+    for n in range(CHUNKS):
+        rows = slice(n * size, (n + 1) * size)
+        pltpu.make_async_copy(done_ref.at[rows], out_ref.at[rows], sems.at[n]).wait()
 
 
 def complex_inverse(re, im):
@@ -143,16 +152,16 @@
     )
 
 
-def null_kernel(picks_ref, angles_ref, volts_ref, out_ref):
+def null_kernel(picks_ref, angles_ref, volts_ref, out_ref, high_ref, low_ref):
     antennas = volts_ref.shape[1] // 2
     count = picks_ref.shape[1]
     row = lax.broadcasted_iota(jnp.int32, (count, 128), 0)
     angle = jnp.zeros((count, 128), F32)
     for k in range(count):
         angle = jnp.where(row == k, angles_ref[picks_ref[0, k]], angle)
-    turn = (jnp.pi * jnp.sin(angle))[:, :1]
+    rate = (jnp.pi * jnp.sin(angle))[:, :1]
     position = lax.broadcasted_iota(jnp.int32, (count, antennas), 1).astype(F32)
-    phase = turn * position
+    phase = rate * position
     norming = antennas**0.5
     re, im = jnp.cos(phase) / norming, jnp.sin(phase) / norming
     both = jnp.concatenate([re, im], axis=1)
@@ -177,7 +186,13 @@
     inner = sum(
         lax.dot_general(volts, part, nt, preferred_element_type=F32) for part in split(steer)
     )
-    out_ref[...] = volts.astype(F32) - dot3(split(inner), split(back))
+    nulled = volts.astype(F32) - dot3(split(inner), split(back))
+    out_ref[...] = nulled
+    size = volts.shape[0] // CHUNKS
+    for n in range(CHUNKS):
+        rows, both = slice(n * size, (n + 1) * size), slice(2 * n * size, 2 * (n + 1) * size)
+        high, low = turn(nulled[rows, :antennas], nulled[rows, antennas:])
+        high_ref[both, :], low_ref[both, :] = high, low
 
 
 def exchange(value, axis, mask):
@@ -294,11 +309,15 @@
     level_own = jnp.where(is_odd, decay * level_own + level_odd[:8], level_own)
     band = level_own / lax.axis_size("chan") + TINY_LEVEL
 
-    projected = pl.pallas_call(
+    projected, high, low = pl.pallas_call(
         null_kernel,
-        out_shape=jax.ShapeDtypeStruct((rows, width), F32),
+        out_shape=(
+            jax.ShapeDtypeStruct((rows, width), F32),
+            jax.ShapeDtypeStruct((2 * rows, width), BF16),
+            jax.ShapeDtypeStruct((2 * rows, width), BF16),
+        ),
         in_specs=[SM, SM, VM],
-        out_specs=VM,
+        out_specs=(VM, VM, VM),
         cost_estimate=pl.CostEstimate(
             flops=4 * rows * width * 128, bytes_accessed=rows * width * 6, transcendentals=0
         ),
@@ -311,7 +330,7 @@
         out_shape=(
             jax.ShapeDtypeStruct((width, antennas), F32),
             jax.ShapeDtypeStruct((width, antennas), F32),
-            jax.ShapeDtypeStruct((8, 128), F32),
+            jax.ShapeDtypeStruct((16, 128), F32),
         ),
         in_specs=[SM, VM, VM],
         out_specs=(VM, VM, VM),
@@ -326,14 +345,15 @@
     cleaned = pl.pallas_call(
         whiten_kernel,
         out_shape=jax.ShapeDtypeStruct((rows, width), F32),
-        in_specs=[VM] * 5,
-        out_specs=VM,
+        in_specs=[VM] * 7,
+        out_specs=pl.BlockSpec(memory_space=pl.ANY),
+        scratch_shapes=[pltpu.VMEM((rows, width), F32), pltpu.SemaphoreType.DMA((CHUNKS,))],
         cost_estimate=pl.CostEstimate(
             flops=12 * rows * width * width, bytes_accessed=rows * width * 8, transcendentals=0
         ),
         compiler_params=PARAMS,
         name="whiten",
-    )(band, stats, cov, square, projected)
+    )(band, stats, cov, square, projected, high, low)
     return cleaned[None]
 
 

time: 26.4 us -> 25.5 us (0.966)
  Pallas kernels: 6.55 us -> 5.66 us
    pallas_call x1, Pallas kernels: 2.86 us -> 2.12 us  [steps(): pl.pallas_call(whiten_kernel, out_shape=jax.ShapeDtypeStruct((rows, width...]
where the time goes in v2:
time: 25.5 us; the launch traced here: 25.3 us
  starting transfers between devices  11.6 us (45%)
  waiting for transfers between devices  6.85 us (27%)
  Pallas kernels  5.66 us (22%)
  local copies, waits for them, and re-layouts  0.96 us (4%)
    ppermute x9, starting transfers between devices, exchange(): lax.ppermute(value, axis, [(i, i ^ mask) for i in range(lax.axis_size(axi...  11.6 us
    ppermute x9, waiting for transfers between devices, exchange(): lax.ppermute(value, axis, [(i, i ^ mask) for i in range(lax.axis_size(axi...  6.85 us
    pallas_call x1, Pallas kernels, steps(): pl.pallas_call(null_kernel, out_shape=(jax.ShapeDtypeStruct((rows, width)...  2.37 us
    pallas_call x1, Pallas kernels, steps(): pl.pallas_call(whiten_kernel, out_shape=jax.ShapeDtypeStruct((rows, width...  2.12 us
    unnamed x8, local copies, waits for them, and re-layouts  0.96 us
    pallas_call x1, Pallas kernels, steps(): pl.pallas_call(square_kernel, out_shape=(jax.ShapeDtypeStruct((width, ant...  0.71 us
  transfers between devices with their start and end apart: 9, of which 6 were waited for; matrix products, arithmetic and copies ran while one was open for 0% of the time, Pallas kernels for 9%

profile of v2, /device:TPU:0, one launch (start us, length us, event | category | flops | bytes accessed | tf_op | source)
XLA Modules:
  0.0 25.3 jit_solution(14337590093884301303)
XLA Ops:
  0.0 0.0 copy-start
  0.0 0.9 %copy-done = bf16[1,256,512]{2,1,0:T(8,128)(2,1)S(1)} copy-done((bf16[1,256,512]{2,1,0:T(8,128)(2,1)S(1)}, bf16[1,256,512]{2,1,0:T(8,128)(2,1)}, u32[]{:S(2)}) %copy-start) | copy-done | bytes 262168
  1.0 0.5 %segment_gram.1 = (f32[128,256]{1,0:T(8,128)S(1)}, f32[128,256]{1,0:T(8,128)S(1)}, f32[8,128]{1,0:T(8,128)S(1)}) custom-call(s32[1]{0:T(128)} %bitcast.parity_ref, bf16[256,512]{1,0:T(8,128)(2,1)S(1)} %bitcast.3), custom_call_target="tpu_custom_call" | custom-call | flops 134217728 | bytes 262144 | tf_op jit(solution)/shard_map/segment_gram/pallas_call | solution.py:270
  1.4 0.6 %collective-permute-start.4 = (f32[128,256]{1,0:T(8,128)S(1)}, f32[128,256]{1,0:T(8,128)S(1)}, u32[]{:S(2)}, u32[]{:S(2)}) collective-permute-start(f32[128,256]{1,0:T(8,128)S(1)} %get-tuple-element.16), channel_id=1, source_target_pairs={{0,1},{1,0},{2,3},{3,2},{4,5},{5,4},{6,7},{7,6},{8,9},{9,8},{10,11... | collective-permute-start | bytes 393224 | tf_op jit(solution)/shard_map/ppermute | solution.py:199
  2.0 1.0 %collective-permute-done.4 = f32[128,256]{1,0:T(8,128)S(1)} collective-permute-done((f32[128,256]{1,0:T(8,128)S(1)}, f32[128,256]{1,0:T(8,128)S(1)}, u32[]{:S(2)}, u32[]{:S(2)}) %collective-permute-start.4) | collective-permute-done | bytes 131104 | tf_op jit(solution)/shard_map/ppermute | solution.py:199
  3.0 3.0 %collective-permute-start.5 = (f32[128,256]{1,0:T(8,128)S(1)}, f32[128,256]{1,0:T(8,128)S(1)}, u32[]{:S(2)}, u32[]{:S(2)}) collective-permute-start(f32[128,256]{1,0:T(8,128)S(1)} %multiply_add_fusion.2), channel_id=1, source_target_pairs={{0,2},{1,3},{2,0},{3,1},{4,6},{5,7},{6,4},{7,5},{8,10},{9,11},{10,... | collective-permute-start | bytes 393224 | tf_op jit(solution)/shard_map/ppermute | solution.py:199
  6.0 1.5 %collective-permute-start = (f32[8,128]{1,0:T(8,128)S(1)}, f32[8,128]{1,0:T(8,128)S(1)}, u32[]{:S(2)}, u32[]{:S(2)}) collective-permute-start(f32[8,128]{1,0:T(8,128)S(1)} %get-tuple-element.14), channel_id=1, source_target_pairs={{0,8},{8,0},{16,24},{24,16},{1,9},{9,1},{17,25},{25,17},{2,10},{10... | collective-permute-start | bytes 12296 | tf_op jit(solution)/shard_map/ppermute | solution.py:199
  7.5 2.1 %collective-permute-done = f32[8,128]{1,0:T(8,128)S(1)} collective-permute-done((f32[8,128]{1,0:T(8,128)S(1)}, f32[8,128]{1,0:T(8,128)S(1)}, u32[]{:S(2)}, u32[]{:S(2)}) %collective-permute-start) | collective-permute-done | bytes 4128 | tf_op jit(solution)/shard_map/ppermute | solution.py:199
  9.6 1.5 %collective-permute-start.1 = (f32[8,128]{1,0:T(8,128)S(1)}, f32[8,128]{1,0:T(8,128)S(1)}, u32[]{:S(2)}, u32[]{:S(2)}) collective-permute-start(f32[8,128]{1,0:T(8,128)S(1)} %add.57), channel_id=1, source_target_pairs={{0,16},{8,24},{16,0},{24,8},{1,17},{9,25},{17,1},{25,9},{2,18},{10... | collective-permute-start | bytes 12296 | tf_op jit(solution)/shard_map/ppermute | solution.py:199
  11.1 2.1 %collective-permute-done.1 = f32[8,128]{1,0:T(8,128)S(1)} collective-permute-done((f32[8,128]{1,0:T(8,128)S(1)}, f32[8,128]{1,0:T(8,128)S(1)}, u32[]{:S(2)}, u32[]{:S(2)}) %collective-permute-start.1) | collective-permute-done | bytes 4128 | tf_op jit(solution)/shard_map/ppermute | solution.py:199
  13.2 0.0 collective-permute-done.5
  13.2 0.0 copy-start.1
  13.2 2.5 %collective-permute-start.6 = (f32[136,256]{1,0:T(8,128)S(1)}, f32[136,256]{1,0:T(8,128)S(1)}, u32[]{:S(2)}, u32[]{:S(2)}) collective-permute-start(f32[136,256]{1,0:T(8,128)S(1)} %maximum_maximum_fusion), channel_id=1, source_target_pairs={{0,6},{1,7},{2,4},{3,5},{4,2},{5,3},{6,0},{7,1},{8,14},{9,15},{10,... | collective-permute-start | bytes 417800 | tf_op jit(solution)/shard_map/ppermute | solution.py:199
  15.8 0.0 copy-start.2
  15.8 0.0 copy-start.3
  15.8 0.3 %collective-permute-start.3 = (f32[8,128]{1,0:T(8,128)S(1)}, f32[8,128]{1,0:T(8,128)S(1)}, u32[]{:S(2)}, u32[]{:S(2)}) collective-permute-start(f32[8,128]{1,0:T(8,128)S(1)} %add.58), channel_id=1, source_target_pairs={{0,4},{1,5},{2,6},{3,7},{4,0},{5,1},{6,2},{7,3},{8,12},{9,13},{10,... | collective-permute-start | bytes 12296 | tf_op jit(solution)/shard_map/ppermute | solution.py:199
  16.1 1.6 %collective-permute-start.2 = (f32[8,128]{1,0:T(8,128)S(1)}, f32[8,128]{1,0:T(8,128)S(1)}, u32[]{:S(2)}, u32[]{:S(2)}) collective-permute-start(f32[8,128]{1,0:T(8,128)S(1)} %add.58), channel_id=1, source_target_pairs={{0,2},{1,3},{2,0},{3,1},{4,6},{5,7},{6,4},{7,5},{8,10},{9,11},{10,... | collective-permute-start | bytes 12296 | tf_op jit(solution)/shard_map/ppermute | solution.py:199
  17.7 0.0 copy-done.1
  17.7 0.0 copy-done.2
  17.7 0.0 copy-done.3
  17.7 2.4 %null.1 = (f32[256,512]{1,0:T(8,128)S(1)}, bf16[512,512]{1,0:T(8,128)(2,1)S(1)}, bf16[512,512]{1,0:T(8,128)(2,1)S(1)}) custom-call(s32[1,8]{1,0:T(1,128)S(1)} %copy-done.2, f32[64]{0:T(128)S(1)} %copy-done.3, bf16[256,512]{1,0:T(8,128)(2,1)S(1)} %bitcast.4), custom_call_target="tpu_custom_call" | custom-call | flops 67108864 | bytes 786432 | tf_op jit(solution)/shard_map/null/pallas_call | solution.py:312
  20.1 0.7 %collective-permute-done.3 = f32[8,128]{1,0:T(8,128)S(1)} collective-permute-done((f32[8,128]{1,0:T(8,128)S(1)}, f32[8,128]{1,0:T(8,128)S(1)}, u32[]{:S(2)}, u32[]{:S(2)}) %collective-permute-start.3) | collective-permute-done | bytes 4128 | tf_op jit(solution)/shard_map/ppermute | solution.py:199
  20.8 0.0 collective-permute-done.2
  20.8 0.0 collective-permute-done.6
  20.8 0.1 collective-permute-start.7
  20.9 0.1 broadcast_select_fusion
  21.0 0.6 %collective-permute-start.8 = (f32[128,256]{1,0:T(8,128)S(1)}, f32[128,256]{1,0:T(8,128)S(1)}, u32[]{:S(2)}, u32[]{:S(2)}) collective-permute-start(f32[128,256]{1,0:T(8,128)S(1)} %get-tuple-element.23), channel_id=1, source_target_pairs={{0,1},{1,0},{2,3},{3,2},{4,5},{5,4},{6,7},{7,6},{8,9},{9,8},{10,11... | collective-permute-start | bytes 393224 | tf_op jit(solution)/shard_map/ppermute | solution.py:199
  21.5 0.5 %collective-permute-done.7 = f32[16,128]{1,0:T(8,128)S(1)} collective-permute-done((f32[16,128]{1,0:T(8,128)S(1)}, f32[16,128]{1,0:T(8,128)S(1)}, u32[]{:S(2)}, u32[]{:S(2)}) %collective-permute-start.7) | collective-permute-done | bytes 8224 | tf_op jit(solution)/shard_map/ppermute | solution.py:199
  22.1 0.4 %collective-permute-done.8.other_ref = f32[128,256]{1,0:T(8,128)S(1)} collective-permute-done((f32[128,256]{1,0:T(8,128)S(1)}, f32[128,256]{1,0:T(8,128)S(1)}, u32[]{:S(2)}, u32[]{:S(2)}) %collective-permute-start.8) | collective-permute-done | bytes 131104 | tf_op jit(solution)/shard_map/ppermute | solution.py:199
  22.5 0.7 %square.1 = (f32[512,256]{1,0:T(8,128)S(1)}, f32[512,256]{1,0:T(8,128)S(1)}, f32[16,128]{1,0:T(8,128)S(1)}) custom-call(s32[1]{0:T(128)} %bitcast.parity_ref, f32[128,256]{1,0:T(8,128)S(1)} %get-tuple-element.24.own_ref, f32[128,256]{1,0:T(8,128)S(1)} %collective-permute-done.8.other_ref), custom_call_target="tpu_custom_call" | custom-call | flops 402653184 | bytes 1048576 | tf_op jit(solution)/shard_map/square/pallas_call | solution.py:328
  23.2 2.1 %whiten.1 = f32[256,512]{1,0:T(8,128)} custom-call(f32[8,128]{1,0:T(8,128)S(1)} %fusion.3.band_ref, f32[16,128]{1,0:T(8,128)S(1)} %get-tuple-element.17.stats_ref, f32[512,256]{1,0:T(8,128)S(1)} %get-tuple-element.18.cov_ref, f32[512,256]{1,0:T(8,128)S(1)} %get-tuple-element.19.square_ref, f32[256,512]{1,0:T(8,128)S(1)} %get-tuple-element.20.w_ref, ...), custom_call_target="tpu_custom_call" | custom-call | flops 805306368 | bytes 1048576 | tf_op jit(solution)/shard_map/whiten/pallas_call | solution.py:345
  (9 shorter events, 0.1 us)
Async XLA Ops:
  0.0 0.9 %copy-start = (bf16[1,256,512]{2,1,0:T(8,128)(2,1)S(1)}, bf16[1,256,512]{2,1,0:T(8,128)(2,1)}, u32[]{:S(2)}) copy-start(bf16[1,256,512]{2,1,0:T(8,128)(2,1)} %param.3) | copy-start | bytes 786436
  1.4 1.5 %collective-permute-start.4 = (f32[128,256]{1,0:T(8,128)S(1)}, f32[128,256]{1,0:T(8,128)S(1)}, u32[]{:S(2)}, u32[]{:S(2)}) collective-permute-start(f32[128,256]{1,0:T(8,128)S(1)} %get-tuple-element.16), channel_id=1, source_target_pairs={{0,1},{1,0},{2,3},{3,2},{4,5},{5,4},{6,7},{7,6},{8,9},{9,8},{10,11... | collective-permute-start | bytes 393224 | tf_op jit(solution)/shard_map/ppermute | solution.py:199
  3.0 10.2 %collective-permute-start.5 = (f32[128,256]{1,0:T(8,128)S(1)}, f32[128,256]{1,0:T(8,128)S(1)}, u32[]{:S(2)}, u32[]{:S(2)}) collective-permute-start(f32[128,256]{1,0:T(8,128)S(1)} %multiply_add_fusion.2), channel_id=1, source_target_pairs={{0,2},{1,3},{2,0},{3,1},{4,6},{5,7},{6,4},{7,5},{8,10},{9,11},{10,... | collective-permute-start | bytes 393224 | tf_op jit(solution)/shard_map/ppermute | solution.py:199
  6.0 3.6 %collective-permute-start = (f32[8,128]{1,0:T(8,128)S(1)}, f32[8,128]{1,0:T(8,128)S(1)}, u32[]{:S(2)}, u32[]{:S(2)}) collective-permute-start(f32[8,128]{1,0:T(8,128)S(1)} %get-tuple-element.14), channel_id=1, source_target_pairs={{0,8},{8,0},{16,24},{24,16},{1,9},{9,1},{17,25},{25,17},{2,10},{10... | collective-permute-start | bytes 12296 | tf_op jit(solution)/shard_map/ppermute | solution.py:199
  9.6 3.6 %collective-permute-start.1 = (f32[8,128]{1,0:T(8,128)S(1)}, f32[8,128]{1,0:T(8,128)S(1)}, u32[]{:S(2)}, u32[]{:S(2)}) collective-permute-start(f32[8,128]{1,0:T(8,128)S(1)} %add.57), channel_id=1, source_target_pairs={{0,16},{8,24},{16,0},{24,8},{1,17},{9,25},{17,1},{25,9},{2,18},{10... | collective-permute-start | bytes 12296 | tf_op jit(solution)/shard_map/ppermute | solution.py:199
  13.2 4.5 %copy-start.1 = (bf16[1,256,512]{2,1,0:T(8,128)(2,1)S(1)}, bf16[1,256,512]{2,1,0:T(8,128)(2,1)}, u32[]{:S(2)}) copy-start(bf16[1,256,512]{2,1,0:T(8,128)(2,1)} %param.3) | copy-start | bytes 786436
  13.2 7.5 %collective-permute-start.6 = (f32[136,256]{1,0:T(8,128)S(1)}, f32[136,256]{1,0:T(8,128)S(1)}, u32[]{:S(2)}, u32[]{:S(2)}) collective-permute-start(f32[136,256]{1,0:T(8,128)S(1)} %maximum_maximum_fusion), channel_id=1, source_target_pairs={{0,6},{1,7},{2,4},{3,5},{4,2},{5,3},{6,0},{7,1},{8,14},{9,15},{10,... | collective-permute-start | bytes 417800 | tf_op jit(solution)/shard_map/ppermute | solution.py:199
  15.8 1.9 %copy-start.2 = (s32[1,8]{1,0:T(1,128)S(1)}, s32[1,8]{1,0:T(1,128)}, u32[]{:S(2)}) copy-start(s32[1,8]{1,0:T(1,128)} %picks_ref.1) | copy-start | bytes 100
  15.8 1.9 %copy-start.3 = (f32[64]{0:T(128)S(1)}, f32[64]{0:T(128)}, u32[]{:S(2)}) copy-start(f32[64]{0:T(128)} %angles_ref.1) | copy-start | bytes 772
  15.8 5.0 %collective-permute-start.3 = (f32[8,128]{1,0:T(8,128)S(1)}, f32[8,128]{1,0:T(8,128)S(1)}, u32[]{:S(2)}, u32[]{:S(2)}) collective-permute-start(f32[8,128]{1,0:T(8,128)S(1)} %add.58), channel_id=1, source_target_pairs={{0,4},{1,5},{2,6},{3,7},{4,0},{5,1},{6,2},{7,3},{8,12},{9,13},{10,... | collective-permute-start | bytes 12296 | tf_op jit(solution)/shard_map/ppermute | solution.py:199
  16.1 4.7 %collective-permute-start.2 = (f32[8,128]{1,0:T(8,128)S(1)}, f32[8,128]{1,0:T(8,128)S(1)}, u32[]{:S(2)}, u32[]{:S(2)}) collective-permute-start(f32[8,128]{1,0:T(8,128)S(1)} %add.58), channel_id=1, source_target_pairs={{0,2},{1,3},{2,0},{3,1},{4,6},{5,7},{6,4},{7,5},{8,10},{9,11},{10,... | collective-permute-start | bytes 12296 | tf_op jit(solution)/shard_map/ppermute | solution.py:199
  20.8 1.2 %collective-permute-start.7 = (f32[16,128]{1,0:T(8,128)S(1)}, f32[16,128]{1,0:T(8,128)S(1)}, u32[]{:S(2)}, u32[]{:S(2)}) collective-permute-start(f32[16,128]{1,0:T(8,128)S(1)} %pad_maximum_fusion), channel_id=1, source_target_pairs={{0,1},{1,0},{2,3},{3,2},{4,5},{5,4},{6,7},{7,6},{8,9},{9,8},{10,11... | collective-permute-start | bytes 24584 | tf_op jit(solution)/shard_map/ppermute | solution.py:199
  21.0 1.5 %collective-permute-start.8 = (f32[128,256]{1,0:T(8,128)S(1)}, f32[128,256]{1,0:T(8,128)S(1)}, u32[]{:S(2)}, u32[]{:S(2)}) collective-permute-start(f32[128,256]{1,0:T(8,128)S(1)} %get-tuple-element.23), channel_id=1, source_target_pairs={{0,1},{1,0},{2,3},{3,2},{4,5},{5,4},{6,7},{7,6},{8,9},{9,8},{10,11... | collective-permute-start | bytes 393224 | tf_op jit(solution)/shard_map/ppermute | solution.py:199

commit v3 on v2

--- a/solution.py
+++ b/solution.py
@@ -8,6 +8,7 @@
 
 SEG = 256
 HORIZON = 256
+PIECES = 2
 CHUNKS = 4
 DIRECT = 4
 LOADING = 0.1
@@ -73,11 +74,14 @@
     return tuple(over(beside(p, q), beside(q, -p)) for p, q in parts)
 
 
-def square_kernel(parity_ref, own_ref, other_ref, cov_ref, square_ref, stats_ref, mixed_ref):
-    half, antennas = own_ref.shape
+def square_kernel(parity_ref, *refs):
+    pieces, (cov_ref, square_ref, stats_ref, mixed_ref) = refs[:-4], refs[-4:]
+    size, antennas = pieces[0].shape
+    half = antennas // 2
     parity = parity_ref[0]
-    mixed_ref[pl.ds(pl.multiple_of(parity * half, half), half), :] = own_ref[...]
-    mixed_ref[pl.ds(pl.multiple_of((1 - parity) * half, half), half), :] = other_ref[...]
+    for k, (own_ref, other_ref) in enumerate(zip(pieces[:PIECES], pieces[PIECES:], strict=True)):
+        mixed_ref[pl.ds(pl.multiple_of(parity * half + k * size, size), size), :] = own_ref[...]
+        mixed_ref[pl.ds(pl.multiple_of((1 - parity) * half + k * size, size), size), :] = other_ref[...]
     mixed = mixed_ref[...]
     flipped = mixed.T
     re, im = 0.5 * (mixed + flipped), 0.5 * (mixed - flipped)
@@ -206,27 +210,29 @@
     return chosen
 
 
-def earlier_chips(value, decay, mirrored=False, rider=None):
+def earlier_chips(values, decay, mirrored=False, rider=None):
     chips = lax.axis_size("tm") // 2
     chip = lax.axis_index("tm") // 2
-    length, total, before = 1, value, None
+    length, totals, before = 1, list(values), [None] * len(values)
     while length < chips:
         last = 2 * length == chips
         mask = 2 * length - 1 if mirrored else length
-        rows = total.shape[0]
-        if last and rider is not None:
-            total = jnp.concatenate([total, rider], axis=0)
-        got = exchange(total, "tm", 2 * mask)
-        if last and rider is not None:
-            got, rider = got[:rows], got[rows:]
         upper = (chip // length) % 2 == 1
         weight = jnp.where(upper, choose(chip % length, [decay**i for i in range(length)]), 0.0)
-        before = weight * got if before is None else before + weight * got
-        if not last:
-            far = decay**length
-            total = jnp.where(upper, 1.0, far) * total + jnp.where(upper, far, 1.0) * got
+        far = decay**length
+        for k, total in enumerate(totals):
+            rows = total.shape[0]
+            loaded = last and rider is not None and k == len(totals) - 1
+            if loaded:
+                total = jnp.concatenate([total, rider], axis=0)
+            got = exchange(total, "tm", 2 * mask)
+            if loaded:
+                got, rider = got[:rows], got[rows:]
+            before[k] = weight * got if before[k] is None else before[k] + weight * got
+            if not last:
+                totals[k] = jnp.where(upper, 1.0, far) * total + jnp.where(upper, far, 1.0) * got
         length *= 2
-    before = jnp.zeros_like(value) if before is None else before
+    before = [jnp.zeros_like(v) if b is None else b for v, b in zip(values, before, strict=True)]
     return before if rider is None else (before, rider)
 
 
@@ -286,20 +292,23 @@
 
     got = exchange(give, "tm", 1)
     mine, theirs = jnp.where(is_odd, 1.0, decay), jnp.where(is_odd, decay, 1.0)
-    pair = mine * keep + theirs * got
+    size = half // PIECES
+    cut = [slice(k * size, (k + 1) * size) for k in range(PIECES)]
+    pairs = lax.optimization_barrier([mine * keep[c] + theirs * got[c] for c in cut])
     level = sum_groups(power)
-    direct = lax.axis_size("tm") // 2 == DIRECT
-    if direct:
+    if lax.axis_size("tm") // 2 == DIRECT:
         wide = jnp.concatenate([level] * (antennas // level.shape[1]), axis=1)
-        before, opposite = earlier_chips(pair, decay * decay, True, wide)
+        before, opposite = earlier_chips(pairs, decay * decay, True, wide)
         level_before = earlier_levels(level, opposite[:, : level.shape[1]], decay * decay)
     else:
-        before = earlier_chips(pair, decay * decay, True)
-        level_before = earlier_chips(level, decay * decay)
-    even_cov = decay * before + jnp.where(is_odd, got, keep)
-    odd_cov = decay * decay * before + pair
-    own = jnp.where(is_odd, odd_cov, even_cov)
-    other = exchange(jnp.where(is_odd, even_cov, odd_cov), "tm", 1)
+        before = earlier_chips(pairs, decay * decay, True)
+        (level_before,) = earlier_chips([level], decay * decay)
+    owns, others = [], []
+    for k, c in enumerate(cut):
+        even_cov = decay * before[k] + jnp.where(is_odd, got[c], keep[c])
+        odd_cov = decay * decay * before[k] + pairs[k]
+        owns.append(jnp.where(is_odd, odd_cov, even_cov))
+        others.append(exchange(jnp.where(is_odd, even_cov, odd_cov), "tm", 1))
 
     levels = jnp.concatenate([level, level_before], axis=0)
     got_levels = exchange(levels, "tm", 1)
@@ -332,7 +341,7 @@
             jax.ShapeDtypeStruct((width, antennas), F32),
             jax.ShapeDtypeStruct((16, 128), F32),
         ),
-        in_specs=[SM, VM, VM],
+        in_specs=[SM] + [VM] * (2 * PIECES),
         out_specs=(VM, VM, VM),
         scratch_shapes=[pltpu.VMEM((antennas, antennas), F32)],
         cost_estimate=pl.CostEstimate(
@@ -340,7 +349,7 @@
         ),
         compiler_params=PARAMS,
         name="square",
-    )(parity, own, other)
+    )(parity, *owns, *others)
 
     cleaned = pl.pallas_call(
         whiten_kernel,

time: 25.5 us -> 32.3 us (1.27)
  waiting for transfers between devices: 6.85 us -> 11.8 us
  starting transfers between devices: 11.6 us -> 13.5 us
    ppermute x9 -> x12, waiting for transfers between devices: 6.85 us -> 11.8 us  [exchange(): lax.ppermute(value, axis, [(i, i ^ mask) for i in range(lax.axis_size(axi...]
    ppermute x9 -> x12, starting transfers between devices: 11.6 us -> 13.5 us  [exchange(): lax.ppermute(value, axis, [(i, i ^ mask) for i in range(lax.axis_size(axi...]
  transfers between devices with their start and end apart: 9 -> 12, of which waited for: 6 -> 7; matrix products, arithmetic and copies ran while one was open for 0% -> 0% of each run, Pallas kernels for 9% -> 7%
where the time goes in v3:
time: 32.3 us; the launch traced here: 32.2 us
  starting transfers between devices  13.5 us (42%)
  waiting for transfers between devices  11.8 us (37%)
  Pallas kernels  5.66 us (18%)
  local copies, waits for them, and re-layouts  0.96 us (3%)
    ppermute x12, starting transfers between devices, exchange(): lax.ppermute(value, axis, [(i, i ^ mask) for i in range(lax.axis_size(axi...  13.5 us
    ppermute x12, waiting for transfers between devices, exchange(): lax.ppermute(value, axis, [(i, i ^ mask) for i in range(lax.axis_size(axi...  11.8 us
    pallas_call x1, Pallas kernels, steps(): pl.pallas_call(null_kernel, out_shape=(jax.ShapeDtypeStruct((rows, width)...  2.37 us
    pallas_call x1, Pallas kernels, steps(): pl.pallas_call(whiten_kernel, out_shape=jax.ShapeDtypeStruct((rows, width...  2.12 us
    unnamed x8, local copies, waits for them, and re-layouts  0.96 us
    pallas_call x1, Pallas kernels, steps(): pl.pallas_call(square_kernel, out_shape=(jax.ShapeDtypeStruct((width, ant...  0.71 us
  transfers between devices with their start and end apart: 12, of which 7 were waited for; matrix products, arithmetic and copies ran while one was open for 0% of the time, Pallas kernels for 7%

profile of v3, /device:TPU:0, one launch (start us, length us, event | category | flops | bytes accessed | tf_op | source)
XLA Modules:
  0.0 32.2 jit_solution(17338874526446105154)
XLA Ops:
  0.0 0.0 copy-start
  0.0 0.9 %copy-done = bf16[1,256,512]{2,1,0:T(8,128)(2,1)S(1)} copy-done((bf16[1,256,512]{2,1,0:T(8,128)(2,1)S(1)}, bf16[1,256,512]{2,1,0:T(8,128)(2,1)}, u32[]{:S(2)}) %copy-start) | copy-done | bytes 262168
  1.0 0.5 %segment_gram.1 = (f32[128,256]{1,0:T(8,128)S(1)}, f32[128,256]{1,0:T(8,128)S(1)}, f32[8,128]{1,0:T(8,128)S(1)}) custom-call(s32[1]{0:T(128)} %bitcast.parity_ref, bf16[256,512]{1,0:T(8,128)(2,1)S(1)} %bitcast.3), custom_call_target="tpu_custom_call" | custom-call | flops 134217728 | bytes 262144 | tf_op jit(solution)/shard_map/segment_gram/pallas_call | solution.py:276
  1.4 0.6 %collective-permute-start.4 = (f32[128,256]{1,0:T(8,128)S(1)}, f32[128,256]{1,0:T(8,128)S(1)}, u32[]{:S(2)}, u32[]{:S(2)}) collective-permute-start(f32[128,256]{1,0:T(8,128)S(1)} %get-tuple-element.18), channel_id=1, source_target_pairs={{0,1},{1,0},{2,3},{3,2},{4,5},{5,4},{6,7},{7,6},{8,9},{9,8},{10,11... | collective-permute-start | bytes 393224 | tf_op jit(solution)/shard_map/ppermute | solution.py:203
  2.0 0.0 copy-start.1
  2.0 1.0 %collective-permute-done.4 = f32[128,256]{1,0:T(8,128)S(1)} collective-permute-done((f32[128,256]{1,0:T(8,128)S(1)}, f32[128,256]{1,0:T(8,128)S(1)}, u32[]{:S(2)}, u32[]{:S(2)}) %collective-permute-start.4) | collective-permute-done | bytes 131104 | tf_op jit(solution)/shard_map/ppermute | solution.py:203
  3.0 3.0 %collective-permute-start.5 = (f32[64,256]{1,0:T(8,128)S(1)}, f32[64,256]{1,0:T(8,128)S(1)}, u32[]{:S(2)}, u32[]{:S(2)}) collective-permute-start(f32[64,256]{1,0:T(8,128)S(1)} %get-tuple-element.19), channel_id=1, source_target_pairs={{0,2},{1,3},{2,0},{3,1},{4,6},{5,7},{6,4},{7,5},{8,10},{9,11},{10,... | collective-permute-start | bytes 196616 | tf_op jit(solution)/shard_map/ppermute | solution.py:203
  6.0 1.5 %collective-permute-start = (f32[8,128]{1,0:T(8,128)S(1)}, f32[8,128]{1,0:T(8,128)S(1)}, u32[]{:S(2)}, u32[]{:S(2)}) collective-permute-start(f32[8,128]{1,0:T(8,128)S(1)} %get-tuple-element.16), channel_id=1, source_target_pairs={{0,8},{8,0},{16,24},{24,16},{1,9},{9,1},{17,25},{25,17},{2,10},{10... | collective-permute-start | bytes 12296 | tf_op jit(solution)/shard_map/ppermute | solution.py:203
  7.5 0.0 copy-start.2
  7.5 0.0 copy-start.3
  7.5 2.1 %collective-permute-done = f32[8,128]{1,0:T(8,128)S(1)} collective-permute-done((f32[8,128]{1,0:T(8,128)S(1)}, f32[8,128]{1,0:T(8,128)S(1)}, u32[]{:S(2)}, u32[]{:S(2)}) %collective-permute-start) | collective-permute-done | bytes 4128 | tf_op jit(solution)/shard_map/ppermute | solution.py:203
  9.6 1.5 %collective-permute-start.1 = (f32[8,128]{1,0:T(8,128)S(1)}, f32[8,128]{1,0:T(8,128)S(1)}, u32[]{:S(2)}, u32[]{:S(2)}) collective-permute-start(f32[8,128]{1,0:T(8,128)S(1)} %add.72), channel_id=1, source_target_pairs={{0,16},{8,24},{16,0},{24,8},{1,17},{9,25},{17,1},{25,9},{2,18},{10... | collective-permute-start | bytes 12296 | tf_op jit(solution)/shard_map/ppermute | solution.py:203
  11.1 0.0 copy-done.1
  11.1 0.0 copy-done.2
  11.1 0.0 copy-done.3
  11.1 2.4 %null.1 = (f32[256,512]{1,0:T(8,128)S(1)}, bf16[512,512]{1,0:T(8,128)(2,1)S(1)}, bf16[512,512]{1,0:T(8,128)(2,1)S(1)}) custom-call(s32[1,8]{1,0:T(1,128)S(1)} %copy-done.2, f32[64]{0:T(128)S(1)} %copy-done.3, bf16[256,512]{1,0:T(8,128)(2,1)S(1)} %bitcast.4), custom_call_target="tpu_custom_call" | custom-call | flops 67108864 | bytes 786432 | tf_op jit(solution)/shard_map/null/pallas_call | solution.py:321
  13.5 0.0 collective-permute-done.1
  13.5 2.7 %collective-permute-start.3 = (f32[8,128]{1,0:T(8,128)S(1)}, f32[8,128]{1,0:T(8,128)S(1)}, u32[]{:S(2)}, u32[]{:S(2)}) collective-permute-start(f32[8,128]{1,0:T(8,128)S(1)} %add.73), channel_id=1, source_target_pairs={{0,4},{1,5},{2,6},{3,7},{4,0},{5,1},{6,2},{7,3},{8,12},{9,13},{10,... | collective-permute-start | bytes 12296 | tf_op jit(solution)/shard_map/ppermute | solution.py:203
  16.2 0.4 %collective-permute-start.2 = (f32[8,128]{1,0:T(8,128)S(1)}, f32[8,128]{1,0:T(8,128)S(1)}, u32[]{:S(2)}, u32[]{:S(2)}) collective-permute-start(f32[8,128]{1,0:T(8,128)S(1)} %add.73), channel_id=1, source_target_pairs={{0,2},{1,3},{2,0},{3,1},{4,6},{5,7},{6,4},{7,5},{8,10},{9,11},{10,... | collective-permute-start | bytes 12296 | tf_op jit(solution)/shard_map/ppermute | solution.py:203
  16.6 1.6 %collective-permute-start.8 = (f32[64,256]{1,0:T(8,128)S(1)}, f32[64,256]{1,0:T(8,128)S(1)}, u32[]{:S(2)}, u32[]{:S(2)}) collective-permute-start(f32[64,256]{1,0:T(8,128)S(1)} %get-tuple-element.20), channel_id=1, source_target_pairs={{0,2},{1,3},{2,0},{3,1},{4,6},{5,7},{6,4},{7,5},{8,10},{9,11},{10,... | collective-permute-start | bytes 196616 | tf_op jit(solution)/shard_map/ppermute | solution.py:203
  18.2 0.0 collective-permute-done.5
  18.2 0.3 collective-permute-start.6
  18.5 3.2 %collective-permute-done.8 = f32[64,256]{1,0:T(8,128)S(1)} collective-permute-done((f32[64,256]{1,0:T(8,128)S(1)}, f32[64,256]{1,0:T(8,128)S(1)}, u32[]{:S(2)}, u32[]{:S(2)}) %collective-permute-start.8) | collective-permute-done | bytes 65568 | tf_op jit(solution)/shard_map/ppermute | solution.py:203
  21.7 1.3 %collective-permute-start.9 = (f32[64,256]{1,0:T(8,128)S(1)}, f32[64,256]{1,0:T(8,128)S(1)}, u32[]{:S(2)}, u32[]{:S(2)}) collective-permute-start(f32[64,256]{1,0:T(8,128)S(1)} %multiply_add_fusion.3), channel_id=1, source_target_pairs={{0,6},{1,7},{2,4},{3,5},{4,2},{5,3},{6,0},{7,1},{8,14},{9,15},{10,... | collective-permute-start | bytes 196616 | tf_op jit(solution)/shard_map/ppermute | solution.py:203
  23.0 0.0 collective-permute-done.3
  23.0 0.0 collective-permute-done.2
  23.0 1.4 %collective-permute-done.6 = f32[72,256]{1,0:T(8,128)S(1)} collective-permute-done((f32[72,256]{1,0:T(8,128)S(1)}, f32[72,256]{1,0:T(8,128)S(1)}, u32[]{:S(2)}, u32[]{:S(2)}) %collective-permute-start.6) | collective-permute-done | bytes 73760 | tf_op jit(solution)/shard_map/ppermute | solution.py:203
  24.5 0.1 collective-permute-start.7
  24.5 3.3 %collective-permute-done.9 = f32[64,256]{1,0:T(8,128)S(1)} collective-permute-done((f32[64,256]{1,0:T(8,128)S(1)}, f32[64,256]{1,0:T(8,128)S(1)}, u32[]{:S(2)}, u32[]{:S(2)}) %collective-permute-start.9) | collective-permute-done | bytes 65568 | tf_op jit(solution)/shard_map/ppermute | solution.py:203
  27.8 0.1 broadcast_select_fusion
  27.9 0.1 collective-permute-start.11
  28.0 0.5 %collective-permute-start.10 = (f32[64,256]{1,0:T(8,128)S(1)}, f32[64,256]{1,0:T(8,128)S(1)}, u32[]{:S(2)}, u32[]{:S(2)}) collective-permute-start(f32[64,256]{1,0:T(8,128)S(1)} %get-tuple-element.32), channel_id=1, source_target_pairs={{0,1},{1,0},{2,3},{3,2},{4,5},{5,4},{6,7},{7,6},{8,9},{9,8},{10,11... | collective-permute-start | bytes 196616 | tf_op jit(solution)/shard_map/ppermute | solution.py:203
  28.4 0.0 collective-permute-done.7
  28.5 0.7 %collective-permute-done.11.refs_3_ = f32[64,256]{1,0:T(8,128)S(1)} collective-permute-done((f32[64,256]{1,0:T(8,128)S(1)}, f32[64,256]{1,0:T(8,128)S(1)}, u32[]{:S(2)}, u32[]{:S(2)}) %collective-permute-start.11) | collective-permute-done | bytes 65568 | tf_op jit(solution)/shard_map/ppermute | solution.py:203
  29.2 0.2 collective-permute-done.10.refs_2_
  29.4 0.7 %square.1 = (f32[512,256]{1,0:T(8,128)S(1)}, f32[512,256]{1,0:T(8,128)S(1)}, f32[16,128]{1,0:T(8,128)S(1)}) custom-call(s32[1]{0:T(128)} %bitcast.parity_ref, f32[64,256]{1,0:T(8,128)S(1)} %get-tuple-element.31.refs_0_, f32[64,256]{1,0:T(8,128)S(1)} %get-tuple-element.28.refs_1_, f32[64,256]{1,0:T(8,128)S(1)} %collective-permute-done.10.refs_2_, ...), custom_call_target="tpu_custom_call" | custom-call | flops 402653184 | bytes 1048576 | tf_op jit(solution)/shard_map/square/pallas_call | solution.py:337
  30.1 2.1 %whiten.1 = f32[256,512]{1,0:T(8,128)} custom-call(f32[8,128]{1,0:T(8,128)S(1)} %fusion.3.band_ref, f32[16,128]{1,0:T(8,128)S(1)} %get-tuple-element.21.stats_ref, f32[512,256]{1,0:T(8,128)S(1)} %get-tuple-element.22.cov_ref, f32[512,256]{1,0:T(8,128)S(1)} %get-tuple-element.23.square_ref, f32[256,512]{1,0:T(8,128)S(1)} %get-tuple-element.24.w_ref, ...), custom_call_target="tpu_custom_call" | custom-call | flops 805306368 | bytes 1048576 | tf_op jit(solution)/shard_map/whiten/pallas_call | solution.py:354
  (10 shorter events, 0.1 us)
Async XLA Ops:
  0.0 0.9 %copy-start = (bf16[1,256,512]{2,1,0:T(8,128)(2,1)S(1)}, bf16[1,256,512]{2,1,0:T(8,128)(2,1)}, u32[]{:S(2)}) copy-start(bf16[1,256,512]{2,1,0:T(8,128)(2,1)} %param.3) | copy-start | bytes 786436
  1.4 1.5 %collective-permute-start.4 = (f32[128,256]{1,0:T(8,128)S(1)}, f32[128,256]{1,0:T(8,128)S(1)}, u32[]{:S(2)}, u32[]{:S(2)}) collective-permute-start(f32[128,256]{1,0:T(8,128)S(1)} %get-tuple-element.18), channel_id=1, source_target_pairs={{0,1},{1,0},{2,3},{3,2},{4,5},{5,4},{6,7},{7,6},{8,9},{9,8},{10,11... | collective-permute-start | bytes 393224 | tf_op jit(solution)/shard_map/ppermute | solution.py:203
  2.0 9.1 %copy-start.1 = (bf16[1,256,512]{2,1,0:T(8,128)(2,1)S(1)}, bf16[1,256,512]{2,1,0:T(8,128)(2,1)}, u32[]{:S(2)}) copy-start(bf16[1,256,512]{2,1,0:T(8,128)(2,1)} %param.3) | copy-start | bytes 786436
  3.0 15.2 %collective-permute-start.5 = (f32[64,256]{1,0:T(8,128)S(1)}, f32[64,256]{1,0:T(8,128)S(1)}, u32[]{:S(2)}, u32[]{:S(2)}) collective-permute-start(f32[64,256]{1,0:T(8,128)S(1)} %get-tuple-element.19), channel_id=1, source_target_pairs={{0,2},{1,3},{2,0},{3,1},{4,6},{5,7},{6,4},{7,5},{8,10},{9,11},{10,... | collective-permute-start | bytes 196616 | tf_op jit(solution)/shard_map/ppermute | solution.py:203
  6.0 3.6 %collective-permute-start = (f32[8,128]{1,0:T(8,128)S(1)}, f32[8,128]{1,0:T(8,128)S(1)}, u32[]{:S(2)}, u32[]{:S(2)}) collective-permute-start(f32[8,128]{1,0:T(8,128)S(1)} %get-tuple-element.16), channel_id=1, source_target_pairs={{0,8},{8,0},{16,24},{24,16},{1,9},{9,1},{17,25},{25,17},{2,10},{10... | collective-permute-start | bytes 12296 | tf_op jit(solution)/shard_map/ppermute | solution.py:203
  7.5 3.6 %copy-start.2 = (s32[1,8]{1,0:T(1,128)S(1)}, s32[1,8]{1,0:T(1,128)}, u32[]{:S(2)}) copy-start(s32[1,8]{1,0:T(1,128)} %picks_ref.1) | copy-start | bytes 100
  7.5 3.6 %copy-start.3 = (f32[64]{0:T(128)S(1)}, f32[64]{0:T(128)}, u32[]{:S(2)}) copy-start(f32[64]{0:T(128)} %angles_ref.1) | copy-start | bytes 772
  9.6 3.9 %collective-permute-start.1 = (f32[8,128]{1,0:T(8,128)S(1)}, f32[8,128]{1,0:T(8,128)S(1)}, u32[]{:S(2)}, u32[]{:S(2)}) collective-permute-start(f32[8,128]{1,0:T(8,128)S(1)} %add.72), channel_id=1, source_target_pairs={{0,16},{8,24},{16,0},{24,8},{1,17},{9,25},{17,1},{25,9},{2,18},{10... | collective-permute-start | bytes 12296 | tf_op jit(solution)/shard_map/ppermute | solution.py:203
  13.5 9.5 %collective-permute-start.3 = (f32[8,128]{1,0:T(8,128)S(1)}, f32[8,128]{1,0:T(8,128)S(1)}, u32[]{:S(2)}, u32[]{:S(2)}) collective-permute-start(f32[8,128]{1,0:T(8,128)S(1)} %add.73), channel_id=1, source_target_pairs={{0,4},{1,5},{2,6},{3,7},{4,0},{5,1},{6,2},{7,3},{8,12},{9,13},{10,... | collective-permute-start | bytes 12296 | tf_op jit(solution)/shard_map/ppermute | solution.py:203
  16.2 6.9 %collective-permute-start.2 = (f32[8,128]{1,0:T(8,128)S(1)}, f32[8,128]{1,0:T(8,128)S(1)}, u32[]{:S(2)}, u32[]{:S(2)}) collective-permute-start(f32[8,128]{1,0:T(8,128)S(1)} %add.73), channel_id=1, source_target_pairs={{0,2},{1,3},{2,0},{3,1},{4,6},{5,7},{6,4},{7,5},{8,10},{9,11},{10,... | collective-permute-start | bytes 12296 | tf_op jit(solution)/shard_map/ppermute | solution.py:203
  16.6 5.1 %collective-permute-start.8 = (f32[64,256]{1,0:T(8,128)S(1)}, f32[64,256]{1,0:T(8,128)S(1)}, u32[]{:S(2)}, u32[]{:S(2)}) collective-permute-start(f32[64,256]{1,0:T(8,128)S(1)} %get-tuple-element.20), channel_id=1, source_target_pairs={{0,2},{1,3},{2,0},{3,1},{4,6},{5,7},{6,4},{7,5},{8,10},{9,11},{10,... | collective-permute-start | bytes 196616 | tf_op jit(solution)/shard_map/ppermute | solution.py:203
  18.2 6.2 %collective-permute-start.6 = (f32[72,256]{1,0:T(8,128)S(1)}, f32[72,256]{1,0:T(8,128)S(1)}, u32[]{:S(2)}, u32[]{:S(2)}) collective-permute-start(f32[72,256]{1,0:T(8,128)S(1)} %maximum_maximum_fusion), channel_id=1, source_target_pairs={{0,6},{1,7},{2,4},{3,5},{4,2},{5,3},{6,0},{7,1},{8,14},{9,15},{10,... | collective-permute-start | bytes 221192 | tf_op jit(solution)/shard_map/ppermute | solution.py:203
  21.7 6.1 %collective-permute-start.9 = (f32[64,256]{1,0:T(8,128)S(1)}, f32[64,256]{1,0:T(8,128)S(1)}, u32[]{:S(2)}, u32[]{:S(2)}) collective-permute-start(f32[64,256]{1,0:T(8,128)S(1)} %multiply_add_fusion.3), channel_id=1, source_target_pairs={{0,6},{1,7},{2,4},{3,5},{4,2},{5,3},{6,0},{7,1},{8,14},{9,15},{10,... | collective-permute-start | bytes 196616 | tf_op jit(solution)/shard_map/ppermute | solution.py:203
  24.5 4.0 %collective-permute-start.7 = (f32[16,128]{1,0:T(8,128)S(1)}, f32[16,128]{1,0:T(8,128)S(1)}, u32[]{:S(2)}, u32[]{:S(2)}) collective-permute-start(f32[16,128]{1,0:T(8,128)S(1)} %pad_maximum_fusion), channel_id=1, source_target_pairs={{0,1},{1,0},{2,3},{3,2},{4,5},{5,4},{6,7},{7,6},{8,9},{9,8},{10,11... | collective-permute-start | bytes 24584 | tf_op jit(solution)/shard_map/ppermute | solution.py:203
  27.9 1.3 %collective-permute-start.11 = (f32[64,256]{1,0:T(8,128)S(1)}, f32[64,256]{1,0:T(8,128)S(1)}, u32[]{:S(2)}, u32[]{:S(2)}) collective-permute-start(f32[64,256]{1,0:T(8,128)S(1)} %get-tuple-element.27), channel_id=1, source_target_pairs={{0,1},{1,0},{2,3},{3,2},{4,5},{5,4},{6,7},{7,6},{8,9},{9,8},{10,11... | collective-permute-start | bytes 196616 | tf_op jit(solution)/shard_map/ppermute | solution.py:203
  28.0 1.4 %collective-permute-start.10 = (f32[64,256]{1,0:T(8,128)S(1)}, f32[64,256]{1,0:T(8,128)S(1)}, u32[]{:S(2)}, u32[]{:S(2)}) collective-permute-start(f32[64,256]{1,0:T(8,128)S(1)} %get-tuple-element.32), channel_id=1, source_target_pairs={{0,1},{1,0},{2,3},{3,2},{4,5},{5,4},{6,7},{7,6},{8,9},{9,8},{10,11... | collective-permute-start | bytes 196616 | tf_op jit(solution)/shard_map/ppermute | solution.py:203

commit v4 on v2

--- a/solution.py
+++ b/solution.py
@@ -248,10 +248,11 @@
     groups = lax.axis_size("chan")
     if groups & (groups - 1):
         return lax.psum(value, "chan")
+    if groups <= DIRECT:
+        return sum((exchange(value, "chan", k) for k in range(1, groups)), value)
     step = 1
     while step < groups:
-        got = exchange(value, "chan", step)
-        value = value + got
+        value = value + exchange(value, "chan", step)
         step *= 2
     return value
 

time: 25.5 us -> 24.9 us (0.976)
  waiting for transfers between devices: 6.85 us -> 5.98 us
  starting transfers between devices: 11.6 us -> 11.9 us
    ppermute x9 -> x10, waiting for transfers between devices: 6.85 us -> 5.98 us  [exchange(): lax.ppermute(value, axis, [(i, i ^ mask) for i in range(lax.axis_size(axi...]
    ppermute x9 -> x10, starting transfers between devices: 11.6 us -> 11.9 us  [exchange(): lax.ppermute(value, axis, [(i, i ^ mask) for i in range(lax.axis_size(axi...]
  transfers between devices with their start and end apart: 9 -> 10, of which waited for: 6 -> 6; matrix products, arithmetic and copies ran while one was open for 0% -> 0% of each run, Pallas kernels for 9% -> 10%
where the time goes in v4:
time: 24.9 us; the launch traced here: 24.8 us
  starting transfers between devices  11.9 us (48%)
  waiting for transfers between devices  5.98 us (24%)
  Pallas kernels  5.66 us (23%)
  local copies, waits for them, and re-layouts  0.96 us (4%)
    ppermute x10, starting transfers between devices, exchange(): lax.ppermute(value, axis, [(i, i ^ mask) for i in range(lax.axis_size(axi...  11.9 us
    ppermute x10, waiting for transfers between devices, exchange(): lax.ppermute(value, axis, [(i, i ^ mask) for i in range(lax.axis_size(axi...  5.98 us
    pallas_call x1, Pallas kernels, steps(): pl.pallas_call(null_kernel, out_shape=(jax.ShapeDtypeStruct((rows, width)...  2.37 us
    pallas_call x1, Pallas kernels, steps(): pl.pallas_call(whiten_kernel, out_shape=jax.ShapeDtypeStruct((rows, width...  2.12 us
    unnamed x8, local copies, waits for them, and re-layouts  0.96 us
    pallas_call x1, Pallas kernels, steps(): pl.pallas_call(square_kernel, out_shape=(jax.ShapeDtypeStruct((width, ant...  0.71 us
  transfers between devices with their start and end apart: 10, of which 6 were waited for; matrix products, arithmetic and copies ran while one was open for 0% of the time, Pallas kernels for 10%

profile of v4, /device:TPU:0, one launch (start us, length us, event | category | flops | bytes accessed | tf_op | source)
XLA Modules:
  0.0 24.8 jit_solution(15519082874390867898)
XLA Ops:
  0.0 0.0 copy-start
  0.0 0.9 %copy-done = bf16[1,256,512]{2,1,0:T(8,128)(2,1)S(1)} copy-done((bf16[1,256,512]{2,1,0:T(8,128)(2,1)S(1)}, bf16[1,256,512]{2,1,0:T(8,128)(2,1)}, u32[]{:S(2)}) %copy-start) | copy-done | bytes 262168
  1.0 0.5 %segment_gram.1 = (f32[128,256]{1,0:T(8,128)S(1)}, f32[128,256]{1,0:T(8,128)S(1)}, f32[8,128]{1,0:T(8,128)S(1)}) custom-call(s32[1]{0:T(128)} %bitcast.parity_ref, bf16[256,512]{1,0:T(8,128)(2,1)S(1)} %bitcast.3), custom_call_target="tpu_custom_call" | custom-call | flops 134217728 | bytes 262144 | tf_op jit(solution)/shard_map/segment_gram/pallas_call | solution.py:271
  1.4 0.6 %collective-permute-start.5 = (f32[128,256]{1,0:T(8,128)S(1)}, f32[128,256]{1,0:T(8,128)S(1)}, u32[]{:S(2)}, u32[]{:S(2)}) collective-permute-start(f32[128,256]{1,0:T(8,128)S(1)} %get-tuple-element.16), channel_id=1, source_target_pairs={{0,1},{1,0},{2,3},{3,2},{4,5},{5,4},{6,7},{7,6},{8,9},{9,8},{10,11... | collective-permute-start | bytes 393224 | tf_op jit(solution)/shard_map/ppermute | solution.py:199
  2.0 3.5 %collective-permute-start.2 = (f32[8,128]{1,0:T(8,128)S(1)}, f32[8,128]{1,0:T(8,128)S(1)}, u32[]{:S(2)}, u32[]{:S(2)}) collective-permute-start(f32[8,128]{1,0:T(8,128)S(1)} %get-tuple-element.14), channel_id=1, source_target_pairs={{0,24},{8,16},{16,8},{24,0},{1,25},{9,17},{17,9},{25,1},{2,26},{10... | collective-permute-start | bytes 12296 | tf_op jit(solution)/shard_map/ppermute | solution.py:199
  5.5 0.5 %collective-permute-start.1 = (f32[8,128]{1,0:T(8,128)S(1)}, f32[8,128]{1,0:T(8,128)S(1)}, u32[]{:S(2)}, u32[]{:S(2)}) collective-permute-start(f32[8,128]{1,0:T(8,128)S(1)} %get-tuple-element.14), channel_id=1, source_target_pairs={{0,16},{8,24},{16,0},{24,8},{1,17},{9,25},{17,1},{25,9},{2,18},{10... | collective-permute-start | bytes 12296 | tf_op jit(solution)/shard_map/ppermute | solution.py:199
  6.0 0.1 collective-permute-start
  6.1 0.0 collective-permute-done.5
  6.2 2.0 %collective-permute-start.6 = (f32[128,256]{1,0:T(8,128)S(1)}, f32[128,256]{1,0:T(8,128)S(1)}, u32[]{:S(2)}, u32[]{:S(2)}) collective-permute-start(f32[128,256]{1,0:T(8,128)S(1)} %multiply_add_fusion.2), channel_id=1, source_target_pairs={{0,2},{1,3},{2,0},{3,1},{4,6},{5,7},{6,4},{7,5},{8,10},{9,11},{10,... | collective-permute-start | bytes 393224 | tf_op jit(solution)/shard_map/ppermute | solution.py:199
  8.2 0.0 collective-permute-done.2
  8.2 0.9 %collective-permute-done.1 = f32[8,128]{1,0:T(8,128)S(1)} collective-permute-done((f32[8,128]{1,0:T(8,128)S(1)}, f32[8,128]{1,0:T(8,128)S(1)}, u32[]{:S(2)}, u32[]{:S(2)}) %collective-permute-start.1) | collective-permute-done | bytes 4128 | tf_op jit(solution)/shard_map/ppermute | solution.py:199
  9.1 0.5 %collective-permute-done = f32[8,128]{1,0:T(8,128)S(1)} collective-permute-done((f32[8,128]{1,0:T(8,128)S(1)}, f32[8,128]{1,0:T(8,128)S(1)}, u32[]{:S(2)}, u32[]{:S(2)}) %collective-permute-start) | collective-permute-done | bytes 4128 | tf_op jit(solution)/shard_map/ppermute | solution.py:199
  9.6 1.8 %collective-permute-done.6 = f32[128,256]{1,0:T(8,128)S(1)} collective-permute-done((f32[128,256]{1,0:T(8,128)S(1)}, f32[128,256]{1,0:T(8,128)S(1)}, u32[]{:S(2)}, u32[]{:S(2)}) %collective-permute-start.6) | collective-permute-done | bytes 131104 | tf_op jit(solution)/shard_map/ppermute | solution.py:199
  11.5 0.0 copy-start.1
  11.5 3.8 %collective-permute-start.7 = (f32[136,256]{1,0:T(8,128)S(1)}, f32[136,256]{1,0:T(8,128)S(1)}, u32[]{:S(2)}, u32[]{:S(2)}) collective-permute-start(f32[136,256]{1,0:T(8,128)S(1)} %maximum_maximum_fusion), channel_id=1, source_target_pairs={{0,6},{1,7},{2,4},{3,5},{4,2},{5,3},{6,0},{7,1},{8,14},{9,15},{10,... | collective-permute-start | bytes 417800 | tf_op jit(solution)/shard_map/ppermute | solution.py:199
  15.3 0.0 copy-start.2
  15.3 0.0 copy-start.3
  15.3 0.0 collective-permute-start.4
  15.3 0.7 %collective-permute-start.3 = (f32[8,128]{1,0:T(8,128)S(1)}, f32[8,128]{1,0:T(8,128)S(1)}, u32[]{:S(2)}, u32[]{:S(2)}) collective-permute-start(f32[8,128]{1,0:T(8,128)S(1)} %add_add_fusion), channel_id=1, source_target_pairs={{0,2},{1,3},{2,0},{3,1},{4,6},{5,7},{6,4},{7,5},{8,10},{9,11},{10,... | collective-permute-start | bytes 12296 | tf_op jit(solution)/shard_map/ppermute | solution.py:199
  16.1 0.0 copy-done.1
  16.1 0.0 copy-done.2
  16.1 0.0 copy-done.3
  16.1 2.4 %null.1 = (f32[256,512]{1,0:T(8,128)S(1)}, bf16[512,512]{1,0:T(8,128)(2,1)S(1)}, bf16[512,512]{1,0:T(8,128)(2,1)S(1)}) custom-call(s32[1,8]{1,0:T(1,128)S(1)} %copy-done.2, f32[64]{0:T(128)S(1)} %copy-done.3, bf16[256,512]{1,0:T(8,128)(2,1)S(1)} %bitcast.4), custom_call_target="tpu_custom_call" | custom-call | flops 67108864 | bytes 786432 | tf_op jit(solution)/shard_map/null/pallas_call | solution.py:313
  18.5 1.8 %collective-permute-done.4 = f32[8,128]{1,0:T(8,128)S(1)} collective-permute-done((f32[8,128]{1,0:T(8,128)S(1)}, f32[8,128]{1,0:T(8,128)S(1)}, u32[]{:S(2)}, u32[]{:S(2)}) %collective-permute-start.4) | collective-permute-done | bytes 4128 | tf_op jit(solution)/shard_map/ppermute | solution.py:199
  20.2 0.0 collective-permute-done.3
  20.2 0.0 collective-permute-done.7
  20.2 0.1 collective-permute-start.8
  20.3 0.1 broadcast_select_fusion
  20.4 0.6 %collective-permute-start.9 = (f32[128,256]{1,0:T(8,128)S(1)}, f32[128,256]{1,0:T(8,128)S(1)}, u32[]{:S(2)}, u32[]{:S(2)}) collective-permute-start(f32[128,256]{1,0:T(8,128)S(1)} %get-tuple-element.23), channel_id=1, source_target_pairs={{0,1},{1,0},{2,3},{3,2},{4,5},{5,4},{6,7},{7,6},{8,9},{9,8},{10,11... | collective-permute-start | bytes 393224 | tf_op jit(solution)/shard_map/ppermute | solution.py:199
  20.9 0.5 %collective-permute-done.8 = f32[16,128]{1,0:T(8,128)S(1)} collective-permute-done((f32[16,128]{1,0:T(8,128)S(1)}, f32[16,128]{1,0:T(8,128)S(1)}, u32[]{:S(2)}, u32[]{:S(2)}) %collective-permute-start.8) | collective-permute-done | bytes 8224 | tf_op jit(solution)/shard_map/ppermute | solution.py:199
  21.5 0.4 %collective-permute-done.9.other_ref = f32[128,256]{1,0:T(8,128)S(1)} collective-permute-done((f32[128,256]{1,0:T(8,128)S(1)}, f32[128,256]{1,0:T(8,128)S(1)}, u32[]{:S(2)}, u32[]{:S(2)}) %collective-permute-start.9) | collective-permute-done | bytes 131104 | tf_op jit(solution)/shard_map/ppermute | solution.py:199
  21.9 0.7 %square.1 = (f32[512,256]{1,0:T(8,128)S(1)}, f32[512,256]{1,0:T(8,128)S(1)}, f32[16,128]{1,0:T(8,128)S(1)}) custom-call(s32[1]{0:T(128)} %bitcast.parity_ref, f32[128,256]{1,0:T(8,128)S(1)} %get-tuple-element.24.own_ref, f32[128,256]{1,0:T(8,128)S(1)} %collective-permute-done.9.other_ref), custom_call_target="tpu_custom_call" | custom-call | flops 402653184 | bytes 1048576 | tf_op jit(solution)/shard_map/square/pallas_call | solution.py:329
  22.7 2.1 %whiten.1 = f32[256,512]{1,0:T(8,128)} custom-call(f32[8,128]{1,0:T(8,128)S(1)} %fusion.3.band_ref, f32[16,128]{1,0:T(8,128)S(1)} %get-tuple-element.17.stats_ref, f32[512,256]{1,0:T(8,128)S(1)} %get-tuple-element.18.cov_ref, f32[512,256]{1,0:T(8,128)S(1)} %get-tuple-element.19.square_ref, f32[256,512]{1,0:T(8,128)S(1)} %get-tuple-element.20.w_ref, ...), custom_call_target="tpu_custom_call" | custom-call | flops 805306368 | bytes 1048576 | tf_op jit(solution)/shard_map/whiten/pallas_call | solution.py:346
  (8 shorter events, 0.1 us)
Async XLA Ops:
  0.0 0.9 %copy-start = (bf16[1,256,512]{2,1,0:T(8,128)(2,1)S(1)}, bf16[1,256,512]{2,1,0:T(8,128)(2,1)}, u32[]{:S(2)}) copy-start(bf16[1,256,512]{2,1,0:T(8,128)(2,1)} %param.3) | copy-start | bytes 786436
  1.4 4.7 %collective-permute-start.5 = (f32[128,256]{1,0:T(8,128)S(1)}, f32[128,256]{1,0:T(8,128)S(1)}, u32[]{:S(2)}, u32[]{:S(2)}) collective-permute-start(f32[128,256]{1,0:T(8,128)S(1)} %get-tuple-element.16), channel_id=1, source_target_pairs={{0,1},{1,0},{2,3},{3,2},{4,5},{5,4},{6,7},{7,6},{8,9},{9,8},{10,11... | collective-permute-start | bytes 393224 | tf_op jit(solution)/shard_map/ppermute | solution.py:199
  2.0 6.2 %collective-permute-start.2 = (f32[8,128]{1,0:T(8,128)S(1)}, f32[8,128]{1,0:T(8,128)S(1)}, u32[]{:S(2)}, u32[]{:S(2)}) collective-permute-start(f32[8,128]{1,0:T(8,128)S(1)} %get-tuple-element.14), channel_id=1, source_target_pairs={{0,24},{8,16},{16,8},{24,0},{1,25},{9,17},{17,9},{25,1},{2,26},{10... | collective-permute-start | bytes 12296 | tf_op jit(solution)/shard_map/ppermute | solution.py:199
  5.5 3.6 %collective-permute-start.1 = (f32[8,128]{1,0:T(8,128)S(1)}, f32[8,128]{1,0:T(8,128)S(1)}, u32[]{:S(2)}, u32[]{:S(2)}) collective-permute-start(f32[8,128]{1,0:T(8,128)S(1)} %get-tuple-element.14), channel_id=1, source_target_pairs={{0,16},{8,24},{16,0},{24,8},{1,17},{9,25},{17,1},{25,9},{2,18},{10... | collective-permute-start | bytes 12296 | tf_op jit(solution)/shard_map/ppermute | solution.py:199
  6.0 3.6 %collective-permute-start = (f32[8,128]{1,0:T(8,128)S(1)}, f32[8,128]{1,0:T(8,128)S(1)}, u32[]{:S(2)}, u32[]{:S(2)}) collective-permute-start(f32[8,128]{1,0:T(8,128)S(1)} %get-tuple-element.14), channel_id=1, source_target_pairs={{0,8},{8,0},{16,24},{24,16},{1,9},{9,1},{17,25},{25,17},{2,10},{10... | collective-permute-start | bytes 12296 | tf_op jit(solution)/shard_map/ppermute | solution.py:199
  6.2 5.3 %collective-permute-start.6 = (f32[128,256]{1,0:T(8,128)S(1)}, f32[128,256]{1,0:T(8,128)S(1)}, u32[]{:S(2)}, u32[]{:S(2)}) collective-permute-start(f32[128,256]{1,0:T(8,128)S(1)} %multiply_add_fusion.2), channel_id=1, source_target_pairs={{0,2},{1,3},{2,0},{3,1},{4,6},{5,7},{6,4},{7,5},{8,10},{9,11},{10,... | collective-permute-start | bytes 393224 | tf_op jit(solution)/shard_map/ppermute | solution.py:199
  11.5 4.6 %copy-start.1 = (bf16[1,256,512]{2,1,0:T(8,128)(2,1)S(1)}, bf16[1,256,512]{2,1,0:T(8,128)(2,1)}, u32[]{:S(2)}) copy-start(bf16[1,256,512]{2,1,0:T(8,128)(2,1)} %param.3) | copy-start | bytes 786436
  11.5 8.7 %collective-permute-start.7 = (f32[136,256]{1,0:T(8,128)S(1)}, f32[136,256]{1,0:T(8,128)S(1)}, u32[]{:S(2)}, u32[]{:S(2)}) collective-permute-start(f32[136,256]{1,0:T(8,128)S(1)} %maximum_maximum_fusion), channel_id=1, source_target_pairs={{0,6},{1,7},{2,4},{3,5},{4,2},{5,3},{6,0},{7,1},{8,14},{9,15},{10,... | collective-permute-start | bytes 417800 | tf_op jit(solution)/shard_map/ppermute | solution.py:199
  15.3 0.7 %copy-start.2 = (s32[1,8]{1,0:T(1,128)S(1)}, s32[1,8]{1,0:T(1,128)}, u32[]{:S(2)}) copy-start(s32[1,8]{1,0:T(1,128)} %picks_ref.1) | copy-start | bytes 100
  15.3 0.7 %copy-start.3 = (f32[64]{0:T(128)S(1)}, f32[64]{0:T(128)}, u32[]{:S(2)}) copy-start(f32[64]{0:T(128)} %angles_ref.1) | copy-start | bytes 772
  15.3 4.9 %collective-permute-start.4 = (f32[8,128]{1,0:T(8,128)S(1)}, f32[8,128]{1,0:T(8,128)S(1)}, u32[]{:S(2)}, u32[]{:S(2)}) collective-permute-start(f32[8,128]{1,0:T(8,128)S(1)} %add_add_fusion), channel_id=1, source_target_pairs={{0,4},{1,5},{2,6},{3,7},{4,0},{5,1},{6,2},{7,3},{8,12},{9,13},{10,... | collective-permute-start | bytes 12296 | tf_op jit(solution)/shard_map/ppermute | solution.py:199
  15.3 4.9 %collective-permute-start.3 = (f32[8,128]{1,0:T(8,128)S(1)}, f32[8,128]{1,0:T(8,128)S(1)}, u32[]{:S(2)}, u32[]{:S(2)}) collective-permute-start(f32[8,128]{1,0:T(8,128)S(1)} %add_add_fusion), channel_id=1, source_target_pairs={{0,2},{1,3},{2,0},{3,1},{4,6},{5,7},{6,4},{7,5},{8,10},{9,11},{10,... | collective-permute-start | bytes 12296 | tf_op jit(solution)/shard_map/ppermute | solution.py:199
  20.2 1.2 %collective-permute-start.8 = (f32[16,128]{1,0:T(8,128)S(1)}, f32[16,128]{1,0:T(8,128)S(1)}, u32[]{:S(2)}, u32[]{:S(2)}) collective-permute-start(f32[16,128]{1,0:T(8,128)S(1)} %pad_maximum_fusion), channel_id=1, source_target_pairs={{0,1},{1,0},{2,3},{3,2},{4,5},{5,4},{6,7},{7,6},{8,9},{9,8},{10,11... | collective-permute-start | bytes 24584 | tf_op jit(solution)/shard_map/ppermute | solution.py:199
  20.4 1.5 %collective-permute-start.9 = (f32[128,256]{1,0:T(8,128)S(1)}, f32[128,256]{1,0:T(8,128)S(1)}, u32[]{:S(2)}, u32[]{:S(2)}) collective-permute-start(f32[128,256]{1,0:T(8,128)S(1)} %get-tuple-element.23), channel_id=1, source_target_pairs={{0,1},{1,0},{2,3},{3,2},{4,5},{5,4},{6,7},{7,6},{8,9},{9,8},{10,11... | collective-permute-start | bytes 393224 | tf_op jit(solution)/shard_map/ppermute | solution.py:199

commit v5 on v2

--- a/solution.py
+++ b/solution.py
@@ -114,10 +114,15 @@
     second = split((slope * (3.0 - 2.0 * shift)) * cov - bend)
     left, right = slice(0, antennas), slice(antennas, 2 * antennas)
     keep_first, keep_second = 2.0 + shift * (shift - 2.0), 2.0 - shift * (3.0 - shift)
-    for n in range(CHUNKS):
-        rows, both = slice(n * size, (n + 1) * size), slice(2 * n * size, 2 * (n + 1) * size)
+
+    def begin(n):
+        both = slice(2 * n * size, 2 * (n + 1) * size)
+        return dot3((high_ref[both, :], low_ref[both, :]), first)
+
+    steps = [begin(n) for n in range(CHUNKS)]
+    for n, step in enumerate(steps):
+        rows = slice(n * size, (n + 1) * size)
         w_u, w_v = w_ref[rows, left], w_ref[rows, right]
-        step = dot3((high_ref[both, :], low_ref[both, :]), first)
         u, v = keep_first * w_u + step[:size], keep_first * w_v + step[size:]
         step = dot3(turn(u, v), second)
         done_ref[rows, left] = omega * (w_u + keep_second * u - step[:size])
@@ -206,39 +211,29 @@
     return chosen
 
 
-def earlier_chips(value, decay, mirrored=False, rider=None):
+def earlier_chips(value, decay, mirrored=False):
     chips = lax.axis_size("tm") // 2
     chip = lax.axis_index("tm") // 2
     length, total, before = 1, value, None
     while length < chips:
-        last = 2 * length == chips
         mask = 2 * length - 1 if mirrored else length
-        rows = total.shape[0]
-        if last and rider is not None:
-            total = jnp.concatenate([total, rider], axis=0)
         got = exchange(total, "tm", 2 * mask)
-        if last and rider is not None:
-            got, rider = got[:rows], got[rows:]
         upper = (chip // length) % 2 == 1
         weight = jnp.where(upper, choose(chip % length, [decay**i for i in range(length)]), 0.0)
         before = weight * got if before is None else before + weight * got
-        if not last:
+        if 2 * length < chips:
             far = decay**length
             total = jnp.where(upper, 1.0, far) * total + jnp.where(upper, far, 1.0) * got
         length *= 2
-    before = jnp.zeros_like(value) if before is None else before
-    return before if rider is None else (before, rider)
-
-
-def earlier_levels(level, opposite, decay):
+    return jnp.zeros_like(value) if before is None else before
+
+
+def earlier_levels(level, decay):
     chips = lax.axis_size("tm") // 2
     chip = lax.axis_index("tm") // 2
-    before = 0.0
+    before = jnp.zeros_like(level)
     for mask in range(1, chips):
-        if mask == chips - 1:
-            got = opposite
-        else:
-            got = exchange(level, "tm", 2 * mask)
+        got = exchange(level, "tm", 2 * mask)
         weights = [decay ** (c - 1 - (c ^ mask)) if c ^ mask < c else 0.0 for c in range(chips)]
         before = before + choose(chip, weights) * got
     return before
@@ -287,14 +282,11 @@
     got = exchange(give, "tm", 1)
     mine, theirs = jnp.where(is_odd, 1.0, decay), jnp.where(is_odd, decay, 1.0)
     pair = mine * keep + theirs * got
+    before = earlier_chips(pair, decay * decay, True)
     level = sum_groups(power)
-    direct = lax.axis_size("tm") // 2 == DIRECT
-    if direct:
-        wide = jnp.concatenate([level] * (antennas // level.shape[1]), axis=1)
-        before, opposite = earlier_chips(pair, decay * decay, True, wide)
-        level_before = earlier_levels(level, opposite[:, : level.shape[1]], decay * decay)
+    if lax.axis_size("tm") // 2 <= DIRECT:
+        level_before = earlier_levels(level, decay * decay)
     else:
-        before = earlier_chips(pair, decay * decay, True)
         level_before = earlier_chips(level, decay * decay)
     even_cov = decay * before + jnp.where(is_odd, got, keep)
     odd_cov = decay * decay * before + pair

time: 25.5 us -> 31.2 us (1.22)
  starting transfers between devices: 11.6 us -> 14.7 us
  waiting for transfers between devices: 6.85 us -> 9.78 us
    ppermute x9 -> x10, starting transfers between devices: 11.6 us -> 14.7 us  [exchange(): lax.ppermute(value, axis, [(i, i ^ mask) for i in range(lax.axis_size(axi...]
    ppermute x9 -> x10, waiting for transfers between devices: 6.85 us -> 9.78 us  [exchange(): lax.ppermute(value, axis, [(i, i ^ mask) for i in range(lax.axis_size(axi...]
  transfers between devices with their start and end apart: 9 -> 10, of which waited for: 6 -> 5; matrix products, arithmetic and copies ran while one was open for 0% -> 0% of each run, Pallas kernels for 9% -> 8%
where the time goes in v5:
time: 31.2 us; the launch traced here: 31.1 us
  starting transfers between devices  14.7 us (47%)
  waiting for transfers between devices  9.78 us (31%)
  Pallas kernels  5.45 us (17%)
  local copies, waits for them, and re-layouts  0.96 us (3%)
    ppermute x10, starting transfers between devices, exchange(): lax.ppermute(value, axis, [(i, i ^ mask) for i in range(lax.axis_size(axi...  14.7 us
    ppermute x10, waiting for transfers between devices, exchange(): lax.ppermute(value, axis, [(i, i ^ mask) for i in range(lax.axis_size(axi...  9.78 us
    pallas_call x1, Pallas kernels, steps(): pl.pallas_call(null_kernel, out_shape=(jax.ShapeDtypeStruct((rows, width)...  2.36 us
    pallas_call x1, Pallas kernels, steps(): pl.pallas_call(whiten_kernel, out_shape=jax.ShapeDtypeStruct((rows, width...  1.91 us
    unnamed x8, local copies, waits for them, and re-layouts  0.96 us
    pallas_call x1, Pallas kernels, steps(): pl.pallas_call(square_kernel, out_shape=(jax.ShapeDtypeStruct((width, ant...  0.72 us
  transfers between devices with their start and end apart: 10, of which 5 were waited for; matrix products, arithmetic and copies ran while one was open for 0% of the time, Pallas kernels for 8%

profile of v5, /device:TPU:0, one launch (start us, length us, event | category | flops | bytes accessed | tf_op | source)
XLA Modules:
  0.0 31.1 jit_solution(15869579064126018269)
XLA Ops:
  0.0 0.0 copy-start
  0.0 0.9 %copy-done = bf16[1,256,512]{2,1,0:T(8,128)(2,1)S(1)} copy-done((bf16[1,256,512]{2,1,0:T(8,128)(2,1)S(1)}, bf16[1,256,512]{2,1,0:T(8,128)(2,1)}, u32[]{:S(2)}) %copy-start) | copy-done | bytes 262168
  1.0 0.0 copy-start.1
  1.0 0.5 %segment_gram.1 = (f32[128,256]{1,0:T(8,128)S(1)}, f32[128,256]{1,0:T(8,128)S(1)}, f32[8,128]{1,0:T(8,128)S(1)}) custom-call(s32[1]{0:T(128)} %bitcast.parity_ref, bf16[256,512]{1,0:T(8,128)(2,1)S(1)} %bitcast.3), custom_call_target="tpu_custom_call" | custom-call | flops 134217728 | bytes 262144 | tf_op jit(solution)/shard_map/segment_gram/pallas_call | solution.py:265
  1.4 0.6 %collective-permute-start.6 = (f32[128,256]{1,0:T(8,128)S(1)}, f32[128,256]{1,0:T(8,128)S(1)}, u32[]{:S(2)}, u32[]{:S(2)}) collective-permute-start(f32[128,256]{1,0:T(8,128)S(1)} %get-tuple-element.16), channel_id=1, source_target_pairs={{0,1},{1,0},{2,3},{3,2},{4,5},{5,4},{6,7},{7,6},{8,9},{9,8},{10,11... | collective-permute-start | bytes 393224 | tf_op jit(solution)/shard_map/ppermute | solution.py:204
  2.0 2.6 %collective-permute-start = (f32[8,128]{1,0:T(8,128)S(1)}, f32[8,128]{1,0:T(8,128)S(1)}, u32[]{:S(2)}, u32[]{:S(2)}) collective-permute-start(f32[8,128]{1,0:T(8,128)S(1)} %get-tuple-element.14), channel_id=1, source_target_pairs={{0,8},{8,0},{16,24},{24,16},{1,9},{9,1},{17,25},{25,17},{2,10},{10... | collective-permute-start | bytes 12296 | tf_op jit(solution)/shard_map/ppermute | solution.py:204
  4.5 0.0 copy-start.2
  4.5 0.0 copy-start.3
  4.5 1.6 %collective-permute-done = f32[8,128]{1,0:T(8,128)S(1)} collective-permute-done((f32[8,128]{1,0:T(8,128)S(1)}, f32[8,128]{1,0:T(8,128)S(1)}, u32[]{:S(2)}, u32[]{:S(2)}) %collective-permute-start) | collective-permute-done | bytes 4128 | tf_op jit(solution)/shard_map/ppermute | solution.py:204
  6.1 2.0 %collective-permute-start.1 = (f32[8,128]{1,0:T(8,128)S(1)}, f32[8,128]{1,0:T(8,128)S(1)}, u32[]{:S(2)}, u32[]{:S(2)}) collective-permute-start(f32[8,128]{1,0:T(8,128)S(1)} %add.57), channel_id=1, source_target_pairs={{0,16},{8,24},{16,0},{24,8},{1,17},{9,25},{17,1},{25,9},{2,18},{10... | collective-permute-start | bytes 12296 | tf_op jit(solution)/shard_map/ppermute | solution.py:204
  8.2 0.0 copy-done.1
  8.2 0.0 copy-done.2
  8.2 0.0 copy-done.3
  8.2 2.4 %null.1 = (f32[256,512]{1,0:T(8,128)S(1)}, bf16[512,512]{1,0:T(8,128)(2,1)S(1)}, bf16[512,512]{1,0:T(8,128)(2,1)S(1)}) custom-call(s32[1,8]{1,0:T(1,128)S(1)} %copy-done.2, f32[64]{0:T(128)S(1)} %copy-done.3, bf16[256,512]{1,0:T(8,128)(2,1)S(1)} %bitcast.4), custom_call_target="tpu_custom_call" | custom-call | flops 67108864 | bytes 786432 | tf_op jit(solution)/shard_map/null/pallas_call | solution.py:304
  10.5 0.0 collective-permute-done.1
  10.6 3.7 %collective-permute-start.4 = (f32[8,128]{1,0:T(8,128)S(1)}, f32[8,128]{1,0:T(8,128)S(1)}, u32[]{:S(2)}, u32[]{:S(2)}) collective-permute-start(f32[8,128]{1,0:T(8,128)S(1)} %add.58), channel_id=1, source_target_pairs={{0,6},{1,7},{2,4},{3,5},{4,2},{5,3},{6,0},{7,1},{8,14},{9,15},{10,... | collective-permute-start | bytes 12296 | tf_op jit(solution)/shard_map/ppermute | solution.py:204
  14.2 0.0 collective-permute-start.3
  14.2 0.8 %collective-permute-start.2 = (f32[8,128]{1,0:T(8,128)S(1)}, f32[8,128]{1,0:T(8,128)S(1)}, u32[]{:S(2)}, u32[]{:S(2)}) collective-permute-start(f32[8,128]{1,0:T(8,128)S(1)} %add.58), channel_id=1, source_target_pairs={{0,2},{1,3},{2,0},{3,1},{4,6},{5,7},{6,4},{7,5},{8,10},{9,11},{10,... | collective-permute-start | bytes 12296 | tf_op jit(solution)/shard_map/ppermute | solution.py:204
  15.0 0.0 collective-permute-done.6
  15.1 1.3 %collective-permute-start.7 = (f32[128,256]{1,0:T(8,128)S(1)}, f32[128,256]{1,0:T(8,128)S(1)}, u32[]{:S(2)}, u32[]{:S(2)}) collective-permute-start(f32[128,256]{1,0:T(8,128)S(1)} %multiply_add_fusion.3), channel_id=1, source_target_pairs={{0,2},{1,3},{2,0},{3,1},{4,6},{5,7},{6,4},{7,5},{8,10},{9,11},{10,... | collective-permute-start | bytes 393224 | tf_op jit(solution)/shard_map/ppermute | solution.py:204
  16.4 0.0 collective-permute-done.4
  16.4 2.5 %collective-permute-done.3 = f32[8,128]{1,0:T(8,128)S(1)} collective-permute-done((f32[8,128]{1,0:T(8,128)S(1)}, f32[8,128]{1,0:T(8,128)S(1)}, u32[]{:S(2)}, u32[]{:S(2)}) %collective-permute-start.3) | collective-permute-done | bytes 4128 | tf_op jit(solution)/shard_map/ppermute | solution.py:204
  18.9 0.0 collective-permute-done.2
  18.9 0.1 collective-permute-start.5
  19.0 1.2 %collective-permute-done.7 = f32[128,256]{1,0:T(8,128)S(1)} collective-permute-done((f32[128,256]{1,0:T(8,128)S(1)}, f32[128,256]{1,0:T(8,128)S(1)}, u32[]{:S(2)}, u32[]{:S(2)}) %collective-permute-start.7) | collective-permute-done | bytes 131104 | tf_op jit(solution)/shard_map/ppermute | solution.py:204
  20.2 3.6 %collective-permute-start.8 = (f32[128,256]{1,0:T(8,128)S(1)}, f32[128,256]{1,0:T(8,128)S(1)}, u32[]{:S(2)}, u32[]{:S(2)}) collective-permute-start(f32[128,256]{1,0:T(8,128)S(1)} %multiply_add_fusion.2), channel_id=1, source_target_pairs={{0,6},{1,7},{2,4},{3,5},{4,2},{5,3},{6,0},{7,1},{8,14},{9,15},{10,... | collective-permute-start | bytes 393224 | tf_op jit(solution)/shard_map/ppermute | solution.py:204
  23.8 0.0 collective-permute-done.5
  23.8 3.2 %collective-permute-done.8 = f32[128,256]{1,0:T(8,128)S(1)} collective-permute-done((f32[128,256]{1,0:T(8,128)S(1)}, f32[128,256]{1,0:T(8,128)S(1)}, u32[]{:S(2)}, u32[]{:S(2)}) %collective-permute-start.8) | collective-permute-done | bytes 131104 | tf_op jit(solution)/shard_map/ppermute | solution.py:204
  27.0 0.1 broadcast_select_fusion
  27.0 0.1 collective-permute-start.9
  27.1 1.3 %collective-permute-done.9.other_ref = f32[128,256]{1,0:T(8,128)S(1)} collective-permute-done((f32[128,256]{1,0:T(8,128)S(1)}, f32[128,256]{1,0:T(8,128)S(1)}, u32[]{:S(2)}, u32[]{:S(2)}) %collective-permute-start.9) | collective-permute-done | bytes 131104 | tf_op jit(solution)/shard_map/ppermute | solution.py:204
  28.5 0.7 %square.1 = (f32[512,256]{1,0:T(8,128)S(1)}, f32[512,256]{1,0:T(8,128)S(1)}, f32[16,128]{1,0:T(8,128)S(1)}) custom-call(s32[1]{0:T(128)} %bitcast.parity_ref, f32[128,256]{1,0:T(8,128)S(1)} %get-tuple-element.24.own_ref, f32[128,256]{1,0:T(8,128)S(1)} %collective-permute-done.9.other_ref), custom_call_target="tpu_custom_call" | custom-call | flops 402653184 | bytes 1048576 | tf_op jit(solution)/shard_map/square/pallas_call | solution.py:320
  29.2 1.9 %whiten.1 = f32[256,512]{1,0:T(8,128)} custom-call(f32[8,128]{1,0:T(8,128)S(1)} %fusion.2.band_ref, f32[16,128]{1,0:T(8,128)S(1)} %get-tuple-element.17.stats_ref, f32[512,256]{1,0:T(8,128)S(1)} %get-tuple-element.18.cov_ref, f32[512,256]{1,0:T(8,128)S(1)} %get-tuple-element.19.square_ref, f32[256,512]{1,0:T(8,128)S(1)} %get-tuple-element.20.w_ref, ...), custom_call_target="tpu_custom_call" | custom-call | flops 805306368 | bytes 1048576 | tf_op jit(solution)/shard_map/whiten/pallas_call | solution.py:337
  (8 shorter events, 0.1 us)
Async XLA Ops:
  0.0 0.9 %copy-start = (bf16[1,256,512]{2,1,0:T(8,128)(2,1)S(1)}, bf16[1,256,512]{2,1,0:T(8,128)(2,1)}, u32[]{:S(2)}) copy-start(bf16[1,256,512]{2,1,0:T(8,128)(2,1)} %param.3) | copy-start | bytes 786436
  1.0 7.2 %copy-start.1 = (bf16[1,256,512]{2,1,0:T(8,128)(2,1)S(1)}, bf16[1,256,512]{2,1,0:T(8,128)(2,1)}, u32[]{:S(2)}) copy-start(bf16[1,256,512]{2,1,0:T(8,128)(2,1)} %param.3) | copy-start | bytes 786436
  1.4 13.6 %collective-permute-start.6 = (f32[128,256]{1,0:T(8,128)S(1)}, f32[128,256]{1,0:T(8,128)S(1)}, u32[]{:S(2)}, u32[]{:S(2)}) collective-permute-start(f32[128,256]{1,0:T(8,128)S(1)} %get-tuple-element.16), channel_id=1, source_target_pairs={{0,1},{1,0},{2,3},{3,2},{4,5},{5,4},{6,7},{7,6},{8,9},{9,8},{10,11... | collective-permute-start | bytes 393224 | tf_op jit(solution)/shard_map/ppermute | solution.py:204
  2.0 4.1 %collective-permute-start = (f32[8,128]{1,0:T(8,128)S(1)}, f32[8,128]{1,0:T(8,128)S(1)}, u32[]{:S(2)}, u32[]{:S(2)}) collective-permute-start(f32[8,128]{1,0:T(8,128)S(1)} %get-tuple-element.14), channel_id=1, source_target_pairs={{0,8},{8,0},{16,24},{24,16},{1,9},{9,1},{17,25},{25,17},{2,10},{10... | collective-permute-start | bytes 12296 | tf_op jit(solution)/shard_map/ppermute | solution.py:204
  4.5 3.6 %copy-start.2 = (s32[1,8]{1,0:T(1,128)S(1)}, s32[1,8]{1,0:T(1,128)}, u32[]{:S(2)}) copy-start(s32[1,8]{1,0:T(1,128)} %picks_ref.1) | copy-start | bytes 100
  4.5 3.6 %copy-start.3 = (f32[64]{0:T(128)S(1)}, f32[64]{0:T(128)}, u32[]{:S(2)}) copy-start(f32[64]{0:T(128)} %angles_ref.1) | copy-start | bytes 772
  6.1 4.4 %collective-permute-start.1 = (f32[8,128]{1,0:T(8,128)S(1)}, f32[8,128]{1,0:T(8,128)S(1)}, u32[]{:S(2)}, u32[]{:S(2)}) collective-permute-start(f32[8,128]{1,0:T(8,128)S(1)} %add.57), channel_id=1, source_target_pairs={{0,16},{8,24},{16,0},{24,8},{1,17},{9,25},{17,1},{25,9},{2,18},{10... | collective-permute-start | bytes 12296 | tf_op jit(solution)/shard_map/ppermute | solution.py:204
  10.6 5.8 %collective-permute-start.4 = (f32[8,128]{1,0:T(8,128)S(1)}, f32[8,128]{1,0:T(8,128)S(1)}, u32[]{:S(2)}, u32[]{:S(2)}) collective-permute-start(f32[8,128]{1,0:T(8,128)S(1)} %add.58), channel_id=1, source_target_pairs={{0,6},{1,7},{2,4},{3,5},{4,2},{5,3},{6,0},{7,1},{8,14},{9,15},{10,... | collective-permute-start | bytes 12296 | tf_op jit(solution)/shard_map/ppermute | solution.py:204
  14.2 4.6 %collective-permute-start.3 = (f32[8,128]{1,0:T(8,128)S(1)}, f32[8,128]{1,0:T(8,128)S(1)}, u32[]{:S(2)}, u32[]{:S(2)}) collective-permute-start(f32[8,128]{1,0:T(8,128)S(1)} %add.58), channel_id=1, source_target_pairs={{0,4},{1,5},{2,6},{3,7},{4,0},{5,1},{6,2},{7,3},{8,12},{9,13},{10,... | collective-permute-start | bytes 12296 | tf_op jit(solution)/shard_map/ppermute | solution.py:204
  14.2 4.6 %collective-permute-start.2 = (f32[8,128]{1,0:T(8,128)S(1)}, f32[8,128]{1,0:T(8,128)S(1)}, u32[]{:S(2)}, u32[]{:S(2)}) collective-permute-start(f32[8,128]{1,0:T(8,128)S(1)} %add.58), channel_id=1, source_target_pairs={{0,2},{1,3},{2,0},{3,1},{4,6},{5,7},{6,4},{7,5},{8,10},{9,11},{10,... | collective-permute-start | bytes 12296 | tf_op jit(solution)/shard_map/ppermute | solution.py:204
  15.1 5.1 %collective-permute-start.7 = (f32[128,256]{1,0:T(8,128)S(1)}, f32[128,256]{1,0:T(8,128)S(1)}, u32[]{:S(2)}, u32[]{:S(2)}) collective-permute-start(f32[128,256]{1,0:T(8,128)S(1)} %multiply_add_fusion.3), channel_id=1, source_target_pairs={{0,2},{1,3},{2,0},{3,1},{4,6},{5,7},{6,4},{7,5},{8,10},{9,11},{10,... | collective-permute-start | bytes 393224 | tf_op jit(solution)/shard_map/ppermute | solution.py:204
  18.9 4.9 %collective-permute-start.5 = (f32[16,128]{1,0:T(8,128)S(1)}, f32[16,128]{1,0:T(8,128)S(1)}, u32[]{:S(2)}, u32[]{:S(2)}) collective-permute-start(f32[16,128]{1,0:T(8,128)S(1)} %pad_maximum_fusion), channel_id=1, source_target_pairs={{0,1},{1,0},{2,3},{3,2},{4,5},{5,4},{6,7},{7,6},{8,9},{9,8},{10,11... | collective-permute-start | bytes 24584 | tf_op jit(solution)/shard_map/ppermute | solution.py:204
  20.2 6.8 %collective-permute-start.8 = (f32[128,256]{1,0:T(8,128)S(1)}, f32[128,256]{1,0:T(8,128)S(1)}, u32[]{:S(2)}, u32[]{:S(2)}) collective-permute-start(f32[128,256]{1,0:T(8,128)S(1)} %multiply_add_fusion.2), channel_id=1, source_target_pairs={{0,6},{1,7},{2,4},{3,5},{4,2},{5,3},{6,0},{7,1},{8,14},{9,15},{10,... | collective-permute-start | bytes 393224 | tf_op jit(solution)/shard_map/ppermute | solution.py:204
  27.0 1.4 %collective-permute-start.9 = (f32[128,256]{1,0:T(8,128)S(1)}, f32[128,256]{1,0:T(8,128)S(1)}, u32[]{:S(2)}, u32[]{:S(2)}) collective-permute-start(f32[128,256]{1,0:T(8,128)S(1)} %get-tuple-element.23), channel_id=1, source_target_pairs={{0,1},{1,0},{2,3},{3,2},{4,5},{5,4},{6,7},{7,6},{8,9},{9,8},{10,11... | collective-permute-start | bytes 393224 | tf_op jit(solution)/shard_map/ppermute | solution.py:204

commit v6 on v2

--- a/solution.py
+++ b/solution.py
@@ -8,6 +8,7 @@
 
 SEG = 256
 HORIZON = 256
+LANES = 128
 CHUNKS = 4
 DIRECT = 4
 LOADING = 0.1
@@ -42,8 +43,11 @@
     trace = jnp.sum(jnp.where(row == column, mixed, 0.0))
     power_ref[...] = jnp.full(power_ref.shape, trace / antennas, F32)
     parity = parity_ref[0]
-    keep_ref[...] = mixed_ref[pl.ds(pl.multiple_of(parity * half, half), half), :]
-    give_ref[...] = mixed_ref[pl.ds(pl.multiple_of((1 - parity) * half, half), half), :]
+    lanes = keep_ref.shape[1]
+    for n in range(antennas // lanes):
+        rows, columns = slice(n * half, (n + 1) * half), slice(n * lanes, (n + 1) * lanes)
+        keep_ref[rows, :] = mixed_ref[pl.ds(pl.multiple_of(parity * half, half), half), columns]
+        give_ref[rows, :] = mixed_ref[pl.ds(pl.multiple_of((1 - parity) * half, half), half), columns]
 
 
 def split(value):
@@ -74,10 +78,13 @@
 
 
 def square_kernel(parity_ref, own_ref, other_ref, cov_ref, square_ref, stats_ref, mixed_ref):
-    half, antennas = own_ref.shape
+    antennas, lanes = mixed_ref.shape[1], own_ref.shape[1]
+    half = antennas // 2
     parity = parity_ref[0]
-    mixed_ref[pl.ds(pl.multiple_of(parity * half, half), half), :] = own_ref[...]
-    mixed_ref[pl.ds(pl.multiple_of((1 - parity) * half, half), half), :] = other_ref[...]
+    for n in range(antennas // lanes):
+        rows, columns = slice(n * half, (n + 1) * half), slice(n * lanes, (n + 1) * lanes)
+        mixed_ref[pl.ds(pl.multiple_of(parity * half, half), half), columns] = own_ref[rows, :]
+        mixed_ref[pl.ds(pl.multiple_of((1 - parity) * half, half), half), columns] = other_ref[rows, :]
     mixed = mixed_ref[...]
     flipped = mixed.T
     re, im = 0.5 * (mixed + flipped), 0.5 * (mixed - flipped)
@@ -114,12 +121,20 @@
     second = split((slope * (3.0 - 2.0 * shift)) * cov - bend)
     left, right = slice(0, antennas), slice(antennas, 2 * antennas)
     keep_first, keep_second = 2.0 + shift * (shift - 2.0), 2.0 - shift * (3.0 - shift)
+
+    def begin(n):
+        both = slice(2 * n * size, 2 * (n + 1) * size)
+        return dot3((high_ref[both, :], low_ref[both, :]), first)
+
+    steps = {n: begin(n) for n in range(4)}
     for n in range(CHUNKS):
-        rows, both = slice(n * size, (n + 1) * size), slice(2 * n * size, 2 * (n + 1) * size)
+        rows = slice(n * size, (n + 1) * size)
+        step = steps.pop(n)
         w_u, w_v = w_ref[rows, left], w_ref[rows, right]
-        step = dot3((high_ref[both, :], low_ref[both, :]), first)
         u, v = keep_first * w_u + step[:size], keep_first * w_v + step[size:]
         step = dot3(turn(u, v), second)
+        if n + 4 < CHUNKS:
+            steps[n + 4] = begin(n + 4)
         done_ref[rows, left] = omega * (w_u + keep_second * u - step[:size])
         done_ref[rows, right] = omega * (w_v + keep_second * v - step[size:])
         pltpu.make_async_copy(done_ref.at[rows], out_ref.at[rows], sems.at[n]).start()
@@ -233,15 +248,14 @@
 def earlier_levels(level, opposite, decay):
     chips = lax.axis_size("tm") // 2
     chip = lax.axis_index("tm") // 2
-    before = 0.0
+    near, far = jnp.zeros_like(level), None
     for mask in range(1, chips):
+        weights = [decay ** (c - 1 - (c ^ mask)) if c ^ mask < c else 0.0 for c in range(chips)]
         if mask == chips - 1:
-            got = opposite
+            far = choose(chip, weights) * opposite
         else:
-            got = exchange(level, "tm", 2 * mask)
-        weights = [decay ** (c - 1 - (c ^ mask)) if c ^ mask < c else 0.0 for c in range(chips)]
-        before = before + choose(chip, weights) * got
-    return before
+            near = near + choose(chip, weights) * exchange(level, "tm", 2 * mask)
+    return near + far
 
 
 def sum_groups(value):
@@ -262,17 +276,17 @@
     antennas = width // 2
     half = antennas // 2
     segments = rows // SEG
-    odd = lax.axis_index("tm") % 2
-    parity = odd.reshape(1).astype(jnp.int32)
-    is_odd = odd == 1
+    core = lax.axis_index("tm") % 2
+    parity = core.reshape(1).astype(jnp.int32)
+    is_odd = core == 1
     decay = (1.0 - 1.0 / HORIZON) ** segments
 
     keep, give, power = pl.pallas_call(
         gram_kernel,
         out_shape=(
-            jax.ShapeDtypeStruct((half, antennas), F32),
-            jax.ShapeDtypeStruct((half, antennas), F32),
-            jax.ShapeDtypeStruct((8, 128), F32),
+            jax.ShapeDtypeStruct((half * antennas // LANES, LANES), F32),
+            jax.ShapeDtypeStruct((half * antennas // LANES, LANES), F32),
+            jax.ShapeDtypeStruct((8, LANES), F32),
         ),
         in_specs=[SM, VM],
         out_specs=(VM, VM, VM),
@@ -287,26 +301,34 @@
     got = exchange(give, "tm", 1)
     mine, theirs = jnp.where(is_odd, 1.0, decay), jnp.where(is_odd, decay, 1.0)
     pair = mine * keep + theirs * got
+    tall = keep.shape[0]
     level = sum_groups(power)
     direct = lax.axis_size("tm") // 2 == DIRECT
+    opposite = None
     if direct:
-        wide = jnp.concatenate([level] * (antennas // level.shape[1]), axis=1)
-        before, opposite = earlier_chips(pair, decay * decay, True, wide)
-        level_before = earlier_levels(level, opposite[:, : level.shape[1]], decay * decay)
+        before, opposite = earlier_chips(pair, decay * decay, True, level)
     else:
         before = earlier_chips(pair, decay * decay, True)
-        level_before = earlier_chips(level, decay * decay)
     even_cov = decay * before + jnp.where(is_odd, got, keep)
     odd_cov = decay * decay * before + pair
     own = jnp.where(is_odd, odd_cov, even_cov)
-    other = exchange(jnp.where(is_odd, even_cov, odd_cov), "tm", 1)
-
-    levels = jnp.concatenate([level, level_before], axis=0)
-    got_levels = exchange(levels, "tm", 1)
-    level_even = jnp.where(is_odd, got_levels, levels)
-    level_odd = jnp.where(is_odd, levels, got_levels)
-    level_own = decay * (decay * level_even[8:] + level_odd[8:]) + level_even[:8]
-    level_own = jnp.where(is_odd, decay * level_own + level_odd[:8], level_own)
+    other = jnp.where(is_odd, even_cov, odd_cov)
+    if direct:
+        other = jnp.concatenate([other, opposite], axis=0)
+    other = exchange(other, "tm", 1)
+
+    def parities(mine, theirs):
+        return jnp.where(is_odd, theirs, mine), jnp.where(is_odd, mine, theirs)
+
+    level_even, level_odd = parities(level, exchange(level, "tm", 1))
+    chip_level = decay * level_even + level_odd
+    if direct:
+        even, odd = parities(opposite, other[tall:])
+        level_before = earlier_levels(chip_level, decay * even + odd, decay * decay)
+    else:
+        level_before = earlier_chips(chip_level, decay * decay)
+    level_own = decay * level_before + level_even
+    level_own = jnp.where(is_odd, decay * level_own + level_odd, level_own)
     band = level_own / lax.axis_size("chan") + TINY_LEVEL
 
     projected, high, low = pl.pallas_call(

time: 25.5 us -> 28.3 us (1.11)
  waiting for transfers between devices: 6.85 us -> 8.49 us
  starting transfers between devices: 11.6 us -> 12.3 us
  local copies, waits for them, and re-layouts: 0.96 us -> 1.62 us
    ppermute x9, waiting for transfers between devices: 6.85 us -> 8.49 us  [exchange(): lax.ppermute(value, axis, [(i, i ^ mask) for i in range(lax.axis_size(axi...]
    ppermute x9, starting transfers between devices: 11.6 us -> 12.3 us  [exchange(): lax.ppermute(value, axis, [(i, i ^ mask) for i in range(lax.axis_size(axi...]
    unnamed x8, local copies, waits for them, and re-layouts: 0.96 us -> 1.62 us
  transfers between devices with their start and end apart: 9 -> 9, of which waited for: 6 -> 6; matrix products, arithmetic and copies ran while one was open for 0% -> 0% of each run, Pallas kernels for 9% -> 11%
where the time goes in v6:
time: 28.3 us; the launch traced here: 28.1 us
  starting transfers between devices  12.3 us (43%)
  waiting for transfers between devices  8.49 us (30%)
  Pallas kernels  5.45 us (19%)
  local copies, waits for them, and re-layouts  1.62 us (6%)
    ppermute x9, starting transfers between devices, exchange(): lax.ppermute(value, axis, [(i, i ^ mask) for i in range(lax.axis_size(axi...  12.3 us
    ppermute x9, waiting for transfers between devices, exchange(): lax.ppermute(value, axis, [(i, i ^ mask) for i in range(lax.axis_size(axi...  8.49 us
    pallas_call x1, Pallas kernels, steps(): pl.pallas_call(null_kernel, out_shape=(jax.ShapeDtypeStruct((rows, width)...  2.36 us
    pallas_call x1, Pallas kernels, steps(): pl.pallas_call(whiten_kernel, out_shape=jax.ShapeDtypeStruct((rows, width...  1.9 us
    unnamed x8, local copies, waits for them, and re-layouts  1.62 us
    pallas_call x1, Pallas kernels, steps(): pl.pallas_call(square_kernel, out_shape=(jax.ShapeDtypeStruct((width, ant...  0.72 us
  transfers between devices with their start and end apart: 9, of which 6 were waited for; matrix products, arithmetic and copies ran while one was open for 0% of the time, Pallas kernels for 11%

profile of v6, /device:TPU:0, one launch (start us, length us, event | category | flops | bytes accessed | tf_op | source)
XLA Modules:
  0.0 28.1 jit_solution(9073053203692440818)
XLA Ops:
  0.0 0.0 copy-start
  0.0 0.9 %copy-done = bf16[1,256,512]{2,1,0:T(8,128)(2,1)S(1)} copy-done((bf16[1,256,512]{2,1,0:T(8,128)(2,1)S(1)}, bf16[1,256,512]{2,1,0:T(8,128)(2,1)}, u32[]{:S(2)}) %copy-start) | copy-done | bytes 262168
  1.0 0.5 %segment_gram.1 = (f32[256,128]{1,0:T(8,128)S(1)}, f32[256,128]{1,0:T(8,128)S(1)}, f32[8,128]{1,0:T(8,128)S(1)}) custom-call(s32[1]{0:T(128)} %bitcast.parity_ref, bf16[256,512]{1,0:T(8,128)(2,1)S(1)} %bitcast.3), custom_call_target="tpu_custom_call" | custom-call | flops 134217728 | bytes 262144 | tf_op jit(solution)/shard_map/segment_gram/pallas_call | solution.py:284
  1.4 0.6 %collective-permute-start.5 = (f32[256,128]{1,0:T(8,128)S(1)}, f32[256,128]{1,0:T(8,128)S(1)}, u32[]{:S(2)}, u32[]{:S(2)}) collective-permute-start(f32[256,128]{1,0:T(8,128)S(1)} %get-tuple-element.16), channel_id=1, source_target_pairs={{0,1},{1,0},{2,3},{3,2},{4,5},{5,4},{6,7},{7,6},{8,9},{9,8},{10,11... | collective-permute-start | bytes 393224 | tf_op jit(solution)/shard_map/ppermute | solution.py:214
  2.0 1.0 %collective-permute-done.5 = f32[256,128]{1,0:T(8,128)S(1)} collective-permute-done((f32[256,128]{1,0:T(8,128)S(1)}, f32[256,128]{1,0:T(8,128)S(1)}, u32[]{:S(2)}, u32[]{:S(2)}) %collective-permute-start.5) | collective-permute-done | bytes 131104 | tf_op jit(solution)/shard_map/ppermute | solution.py:214
  3.0 3.0 %collective-permute-start.6 = (f32[256,128]{1,0:T(8,128)S(1)}, f32[256,128]{1,0:T(8,128)S(1)}, u32[]{:S(2)}, u32[]{:S(2)}) collective-permute-start(f32[256,128]{1,0:T(8,128)S(1)} %multiply_add_fusion.2), channel_id=1, source_target_pairs={{0,2},{1,3},{2,0},{3,1},{4,6},{5,7},{6,4},{7,5},{8,10},{9,11},{10,... | collective-permute-start | bytes 393224 | tf_op jit(solution)/shard_map/ppermute | solution.py:214
  6.0 1.5 %collective-permute-start = (f32[8,128]{1,0:T(8,128)S(1)}, f32[8,128]{1,0:T(8,128)S(1)}, u32[]{:S(2)}, u32[]{:S(2)}) collective-permute-start(f32[8,128]{1,0:T(8,128)S(1)} %get-tuple-element.14), channel_id=1, source_target_pairs={{0,8},{8,0},{16,24},{24,16},{1,9},{9,1},{17,25},{25,17},{2,10},{10... | collective-permute-start | bytes 12296 | tf_op jit(solution)/shard_map/ppermute | solution.py:214
  7.5 2.1 %collective-permute-done = f32[8,128]{1,0:T(8,128)S(1)} collective-permute-done((f32[8,128]{1,0:T(8,128)S(1)}, f32[8,128]{1,0:T(8,128)S(1)}, u32[]{:S(2)}, u32[]{:S(2)}) %collective-permute-start) | collective-permute-done | bytes 4128 | tf_op jit(solution)/shard_map/ppermute | solution.py:214
  9.6 1.5 %collective-permute-start.1 = (f32[8,128]{1,0:T(8,128)S(1)}, f32[8,128]{1,0:T(8,128)S(1)}, u32[]{:S(2)}, u32[]{:S(2)}) collective-permute-start(f32[8,128]{1,0:T(8,128)S(1)} %add.60), channel_id=1, source_target_pairs={{0,16},{8,24},{16,0},{24,8},{1,17},{9,25},{17,1},{25,9},{2,18},{10... | collective-permute-start | bytes 12296 | tf_op jit(solution)/shard_map/ppermute | solution.py:214
  11.1 2.1 %collective-permute-done.1 = f32[8,128]{1,0:T(8,128)S(1)} collective-permute-done((f32[8,128]{1,0:T(8,128)S(1)}, f32[8,128]{1,0:T(8,128)S(1)}, u32[]{:S(2)}, u32[]{:S(2)}) %collective-permute-start.1) | collective-permute-done | bytes 4128 | tf_op jit(solution)/shard_map/ppermute | solution.py:214
  13.2 0.0 collective-permute-done.6
  13.2 0.0 copy-start.1
  13.3 2.5 %collective-permute-start.7 = (f32[264,128]{1,0:T(8,128)S(1)}, f32[264,128]{1,0:T(8,128)S(1)}, u32[]{:S(2)}, u32[]{:S(2)}) collective-permute-start(f32[264,128]{1,0:T(8,128)S(1)} %pad_maximum_fusion), channel_id=1, source_target_pairs={{0,6},{1,7},{2,4},{3,5},{4,2},{5,3},{6,0},{7,1},{8,14},{9,15},{10,... | collective-permute-start | bytes 405512 | tf_op jit(solution)/shard_map/ppermute | solution.py:214
  15.8 0.0 copy-start.2
  15.8 0.0 copy-start.3
  15.8 0.0 copy-done.1
  15.8 0.6 %copy-done.2 = s32[1,8]{1,0:T(1,128)S(1)} copy-done((s32[1,8]{1,0:T(1,128)S(1)}, s32[1,8]{1,0:T(1,128)}, u32[]{:S(2)}) %copy-start.2) | copy-done | bytes 56
  16.5 0.0 copy-done.3
  16.5 2.4 %null.1 = (f32[256,512]{1,0:T(8,128)S(1)}, bf16[512,512]{1,0:T(8,128)(2,1)S(1)}, bf16[512,512]{1,0:T(8,128)(2,1)S(1)}) custom-call(s32[1,8]{1,0:T(1,128)S(1)} %copy-done.2, f32[64]{0:T(128)S(1)} %copy-done.3, bf16[256,512]{1,0:T(8,128)(2,1)S(1)} %bitcast.4), custom_call_target="tpu_custom_call" | custom-call | flops 67108864 | bytes 786432 | tf_op jit(solution)/shard_map/null/pallas_call | solution.py:334
  18.8 0.1 collective-permute-start.2
  18.9 1.3 %collective-permute-done.7 = f32[264,128]{1,0:T(8,128)S(1)} collective-permute-done((f32[264,128]{1,0:T(8,128)S(1)}, f32[264,128]{1,0:T(8,128)S(1)}, u32[]{:S(2)}, u32[]{:S(2)}) %collective-permute-start.7) | collective-permute-done | bytes 135200 | tf_op jit(solution)/shard_map/ppermute | solution.py:214
  20.2 0.1 broadcast_select_fusion
  20.3 0.1 collective-permute-start.8
  20.4 0.0 collective-permute-done.2
  20.4 2.2 %collective-permute-start.4 = (f32[8,128]{1,0:T(8,128)S(1)}, f32[8,128]{1,0:T(8,128)S(1)}, u32[]{:S(2)}, u32[]{:S(2)}) collective-permute-start(f32[8,128]{1,0:T(8,128)S(1)} %multiply_add_fusion.4), channel_id=1, source_target_pairs={{0,4},{1,5},{2,6},{3,7},{4,0},{5,1},{6,2},{7,3},{8,12},{9,13},{10,... | collective-permute-start | bytes 12296 | tf_op jit(solution)/shard_map/ppermute | solution.py:214
  22.6 0.9 %collective-permute-start.3 = (f32[8,128]{1,0:T(8,128)S(1)}, f32[8,128]{1,0:T(8,128)S(1)}, u32[]{:S(2)}, u32[]{:S(2)}) collective-permute-start(f32[8,128]{1,0:T(8,128)S(1)} %multiply_add_fusion.4), channel_id=1, source_target_pairs={{0,2},{1,3},{2,0},{3,1},{4,6},{5,7},{6,4},{7,5},{8,10},{9,11},{10,... | collective-permute-start | bytes 12296 | tf_op jit(solution)/shard_map/ppermute | solution.py:214
  23.5 0.0 collective-permute-done.8.other_ref
  23.5 0.7 %square.1 = (f32[512,256]{1,0:T(8,128)S(1)}, f32[512,256]{1,0:T(8,128)S(1)}, f32[16,128]{1,0:T(8,128)S(1)}) custom-call(s32[1]{0:T(128)} %bitcast.parity_ref, f32[256,128]{1,0:T(8,128)S(1)} %get-tuple-element.23.own_ref, f32[264,128]{1,0:T(8,128)S(1)} %collective-permute-done.8.other_ref), custom_call_target="tpu_custom_call" | custom-call | flops 402653184 | bytes 1048576 | tf_op jit(solution)/shard_map/square/pallas_call | solution.py:350
  24.2 0.7 %collective-permute-done.4 = f32[8,128]{1,0:T(8,128)S(1)} collective-permute-done((f32[8,128]{1,0:T(8,128)S(1)}, f32[8,128]{1,0:T(8,128)S(1)}, u32[]{:S(2)}, u32[]{:S(2)}) %collective-permute-start.4) | collective-permute-done | bytes 4128 | tf_op jit(solution)/shard_map/ppermute | solution.py:214
  25.0 1.2 %collective-permute-done.3 = f32[8,128]{1,0:T(8,128)S(1)} collective-permute-done((f32[8,128]{1,0:T(8,128)S(1)}, f32[8,128]{1,0:T(8,128)S(1)}, u32[]{:S(2)}, u32[]{:S(2)}) %collective-permute-start.3) | collective-permute-done | bytes 4128 | tf_op jit(solution)/shard_map/ppermute | solution.py:214
  26.2 1.9 %whiten.1 = f32[256,512]{1,0:T(8,128)} custom-call(f32[8,128]{1,0:T(8,128)S(1)} %multiply_add_fusion.3.band_ref, f32[16,128]{1,0:T(8,128)S(1)} %get-tuple-element.17.stats_ref, f32[512,256]{1,0:T(8,128)S(1)} %get-tuple-element.18.cov_ref, f32[512,256]{1,0:T(8,128)S(1)} %get-tuple-element.19.square_ref, f32[256,512]{1,0:T(8,128)S(1)} %get-tuple-element.20.w_ref, ...), custom_call_target="tpu_custom_call" | custom-call | flops 805306368 | bytes 1048576 | tf_op jit(solution)/shard_map/whiten/pallas_call | solution.py:367
  (9 shorter events, 0.1 us)
Async XLA Ops:
  0.0 0.9 %copy-start = (bf16[1,256,512]{2,1,0:T(8,128)(2,1)S(1)}, bf16[1,256,512]{2,1,0:T(8,128)(2,1)}, u32[]{:S(2)}) copy-start(bf16[1,256,512]{2,1,0:T(8,128)(2,1)} %param.3) | copy-start | bytes 786436
  1.4 1.5 %collective-permute-start.5 = (f32[256,128]{1,0:T(8,128)S(1)}, f32[256,128]{1,0:T(8,128)S(1)}, u32[]{:S(2)}, u32[]{:S(2)}) collective-permute-start(f32[256,128]{1,0:T(8,128)S(1)} %get-tuple-element.16), channel_id=1, source_target_pairs={{0,1},{1,0},{2,3},{3,2},{4,5},{5,4},{6,7},{7,6},{8,9},{9,8},{10,11... | collective-permute-start | bytes 393224 | tf_op jit(solution)/shard_map/ppermute | solution.py:214
  3.0 10.2 %collective-permute-start.6 = (f32[256,128]{1,0:T(8,128)S(1)}, f32[256,128]{1,0:T(8,128)S(1)}, u32[]{:S(2)}, u32[]{:S(2)}) collective-permute-start(f32[256,128]{1,0:T(8,128)S(1)} %multiply_add_fusion.2), channel_id=1, source_target_pairs={{0,2},{1,3},{2,0},{3,1},{4,6},{5,7},{6,4},{7,5},{8,10},{9,11},{10,... | collective-permute-start | bytes 393224 | tf_op jit(solution)/shard_map/ppermute | solution.py:214
  6.0 3.6 %collective-permute-start = (f32[8,128]{1,0:T(8,128)S(1)}, f32[8,128]{1,0:T(8,128)S(1)}, u32[]{:S(2)}, u32[]{:S(2)}) collective-permute-start(f32[8,128]{1,0:T(8,128)S(1)} %get-tuple-element.14), channel_id=1, source_target_pairs={{0,8},{8,0},{16,24},{24,16},{1,9},{9,1},{17,25},{25,17},{2,10},{10... | collective-permute-start | bytes 12296 | tf_op jit(solution)/shard_map/ppermute | solution.py:214
  9.6 3.6 %collective-permute-start.1 = (f32[8,128]{1,0:T(8,128)S(1)}, f32[8,128]{1,0:T(8,128)S(1)}, u32[]{:S(2)}, u32[]{:S(2)}) collective-permute-start(f32[8,128]{1,0:T(8,128)S(1)} %add.60), channel_id=1, source_target_pairs={{0,16},{8,24},{16,0},{24,8},{1,17},{9,25},{17,1},{25,9},{2,18},{10... | collective-permute-start | bytes 12296 | tf_op jit(solution)/shard_map/ppermute | solution.py:214
  13.2 2.6 %copy-start.1 = (bf16[1,256,512]{2,1,0:T(8,128)(2,1)S(1)}, bf16[1,256,512]{2,1,0:T(8,128)(2,1)}, u32[]{:S(2)}) copy-start(bf16[1,256,512]{2,1,0:T(8,128)(2,1)} %param.3) | copy-start | bytes 786436
  13.3 7.0 %collective-permute-start.7 = (f32[264,128]{1,0:T(8,128)S(1)}, f32[264,128]{1,0:T(8,128)S(1)}, u32[]{:S(2)}, u32[]{:S(2)}) collective-permute-start(f32[264,128]{1,0:T(8,128)S(1)} %pad_maximum_fusion), channel_id=1, source_target_pairs={{0,6},{1,7},{2,4},{3,5},{4,2},{5,3},{6,0},{7,1},{8,14},{9,15},{10,... | collective-permute-start | bytes 405512 | tf_op jit(solution)/shard_map/ppermute | solution.py:214
  15.8 0.7 %copy-start.2 = (s32[1,8]{1,0:T(1,128)S(1)}, s32[1,8]{1,0:T(1,128)}, u32[]{:S(2)}) copy-start(s32[1,8]{1,0:T(1,128)} %picks_ref.1) | copy-start | bytes 100
  15.8 0.7 %copy-start.3 = (f32[64]{0:T(128)S(1)}, f32[64]{0:T(128)}, u32[]{:S(2)}) copy-start(f32[64]{0:T(128)} %angles_ref.1) | copy-start | bytes 772
  18.8 1.5 %collective-permute-start.2 = (f32[8,128]{1,0:T(8,128)S(1)}, f32[8,128]{1,0:T(8,128)S(1)}, u32[]{:S(2)}, u32[]{:S(2)}) collective-permute-start(f32[8,128]{1,0:T(8,128)S(1)} %add.61), channel_id=1, source_target_pairs={{0,1},{1,0},{2,3},{3,2},{4,5},{5,4},{6,7},{7,6},{8,9},{9,8},{10,11... | collective-permute-start | bytes 12296 | tf_op jit(solution)/shard_map/ppermute | solution.py:214
  20.3 3.2 %collective-permute-start.8 = (f32[264,128]{1,0:T(8,128)S(1)}, f32[264,128]{1,0:T(8,128)S(1)}, u32[]{:S(2)}, u32[]{:S(2)}) collective-permute-start(f32[264,128]{1,0:T(8,128)S(1)} %pad_maximum_fusion.1), channel_id=1, source_target_pairs={{0,1},{1,0},{2,3},{3,2},{4,5},{5,4},{6,7},{7,6},{8,9},{9,8},{10,11... | collective-permute-start | bytes 405512 | tf_op jit(solution)/shard_map/ppermute | solution.py:214
  20.4 4.6 %collective-permute-start.4 = (f32[8,128]{1,0:T(8,128)S(1)}, f32[8,128]{1,0:T(8,128)S(1)}, u32[]{:S(2)}, u32[]{:S(2)}) collective-permute-start(f32[8,128]{1,0:T(8,128)S(1)} %multiply_add_fusion.4), channel_id=1, source_target_pairs={{0,4},{1,5},{2,6},{3,7},{4,0},{5,1},{6,2},{7,3},{8,12},{9,13},{10,... | collective-permute-start | bytes 12296 | tf_op jit(solution)/shard_map/ppermute | solution.py:214
  22.6 3.6 %collective-permute-start.3 = (f32[8,128]{1,0:T(8,128)S(1)}, f32[8,128]{1,0:T(8,128)S(1)}, u32[]{:S(2)}, u32[]{:S(2)}) collective-permute-start(f32[8,128]{1,0:T(8,128)S(1)} %multiply_add_fusion.4), channel_id=1, source_target_pairs={{0,2},{1,3},{2,0},{3,1},{4,6},{5,7},{6,4},{7,5},{8,10},{9,11},{10,... | collective-permute-start | bytes 12296 | tf_op jit(solution)/shard_map/ppermute | solution.py:214

commit v7 on v6

--- a/solution.py
+++ b/solution.py
@@ -27,21 +27,20 @@
     segments = volts_ref.shape[0] // SEG
     half = antennas // 2
     forget = 1.0 - 1.0 / HORIZON
-    mixed = None
+    mixed = power = None
     for seg in range(segments):
         a = volts_ref[seg * SEG : (seg + 1) * SEG, :antennas]
         b = volts_ref[seg * SEG : (seg + 1) * SEG, antennas:]
-        left = jnp.concatenate([a, b, b, -a], axis=0)
+        a_t, b_t = a.T, b.T
+        left = jnp.concatenate([a_t, b_t, b_t, -a_t], axis=1)
         right = jnp.concatenate([a, b, a, b], axis=0)
-        term = lax.dot_general(
-            left, right, (((0,), (0,)), ((), ())), preferred_element_type=F32
-        )
+        term = jnp.dot(left, right, preferred_element_type=F32)
         mixed = term if mixed is None else forget * mixed + term
+        squares = a.astype(F32) ** 2 + b.astype(F32) ** 2
+        squares = jnp.sum(squares.reshape(-1, 8, antennas), axis=0)
+        power = squares if power is None else forget * power + squares
     mixed_ref[...] = mixed
-    row = lax.broadcasted_iota(jnp.int32, mixed.shape, 0)
-    column = lax.broadcasted_iota(jnp.int32, mixed.shape, 1)
-    trace = jnp.sum(jnp.where(row == column, mixed, 0.0))
-    power_ref[...] = jnp.full(power_ref.shape, trace / antennas, F32)
+    power_ref[...] = jnp.broadcast_to(jnp.sum(power, keepdims=True) / antennas, power_ref.shape)
     parity = parity_ref[0]
     lanes = keep_ref.shape[1]
     for n in range(antennas // lanes):
@@ -90,8 +89,10 @@
     re, im = 0.5 * (mixed + flipped), 0.5 * (mixed - flipped)
     cov_ref[:antennas, :], cov_ref[antennas:, :] = re, im
     (rh, rl), (ih, il) = split(re), split(im)
-    full = tuple(over(beside(r, -i), beside(i, r)) for r, i in ((rh, ih), (rl, il)))
-    square_ref[...] = dot3(full, (over(rh, ih), over(rl, il)))
+    (sh, sl), (fh, fl) = split(mixed), split(flipped)
+    product = dot3((beside(sh, fh), beside(sl, fl)), (over(rh, ih), over(rl, il)))
+    turned = product.T
+    square_ref[:antennas, :], square_ref[antennas:, :] = 0.5 * (product + turned), 0.5 * (product - turned)
     row = lax.broadcasted_iota(jnp.int32, mixed.shape, 0)
     column = lax.broadcasted_iota(jnp.int32, mixed.shape, 1)
     trace = jnp.sum(jnp.where(row == column, mixed, 0.0), keepdims=True)
@@ -381,6 +382,4 @@
 
 def solution(mesh):
     placed = (P("chan", "tm", None), P("chan", None), P())
-    return jax.shard_map(
-        steps, mesh=mesh, in_specs=placed, out_specs=P("chan", "tm", None), check_vma=False
-    )
+    return jax.shard_map(steps, mesh=mesh, in_specs=placed, out_specs=P("chan", "tm", None), check_vma=False)

time: 28.3 us -> 28.2 us (level)
  no operation moved by 1% of the time
where the time goes in v7:
time: 28.2 us; the launch traced here: 28.1 us
  starting transfers between devices  12.3 us (44%)
  waiting for transfers between devices  8.58 us (30%)
  Pallas kernels  5.27 us (19%)
  local copies, waits for them, and re-layouts  1.62 us (6%)
    ppermute x9, starting transfers between devices, exchange(): lax.ppermute(value, axis, [(i, i ^ mask) for i in range(lax.axis_size(axi...  12.3 us
    ppermute x9, waiting for transfers between devices, exchange(): lax.ppermute(value, axis, [(i, i ^ mask) for i in range(lax.axis_size(axi...  8.58 us
    pallas_call x1, Pallas kernels, steps(): pl.pallas_call(null_kernel, out_shape=(jax.ShapeDtypeStruct((rows, width)...  2.37 us
    pallas_call x1, Pallas kernels, steps(): pl.pallas_call(whiten_kernel, out_shape=jax.ShapeDtypeStruct((rows, width...  1.9 us
    unnamed x8, local copies, waits for them, and re-layouts  1.62 us
    pallas_call x1, Pallas kernels, steps(): pl.pallas_call(square_kernel, out_shape=(jax.ShapeDtypeStruct((width, ant...  0.63 us
  transfers between devices with their start and end apart: 9, of which 6 were waited for; matrix products, arithmetic and copies ran while one was open for 0% of the time, Pallas kernels for 11%

profile of v7, /device:TPU:0, one launch (start us, length us, event | category | flops | bytes accessed | tf_op | source)
XLA Modules:
  0.0 28.1 jit_solution(7372037076390339081)
XLA Ops:
  0.0 0.0 copy-start
  0.0 0.9 %copy-done = bf16[1,256,512]{2,1,0:T(8,128)(2,1)S(1)} copy-done((bf16[1,256,512]{2,1,0:T(8,128)(2,1)S(1)}, bf16[1,256,512]{2,1,0:T(8,128)(2,1)}, u32[]{:S(2)}) %copy-start) | copy-done | bytes 262168
  1.0 0.4 %segment_gram.1 = (f32[256,128]{1,0:T(8,128)S(1)}, f32[256,128]{1,0:T(8,128)S(1)}, f32[8,128]{1,0:T(8,128)S(1)}) custom-call(s32[1]{0:T(128)} %bitcast.parity_ref, bf16[256,512]{1,0:T(8,128)(2,1)S(1)} %bitcast.3), custom_call_target="tpu_custom_call" | custom-call | flops 134217728 | bytes 262144 | tf_op jit(solution)/shard_map/segment_gram/pallas_call | solution.py:285
  1.3 0.6 %collective-permute-start.5 = (f32[256,128]{1,0:T(8,128)S(1)}, f32[256,128]{1,0:T(8,128)S(1)}, u32[]{:S(2)}, u32[]{:S(2)}) collective-permute-start(f32[256,128]{1,0:T(8,128)S(1)} %get-tuple-element.16), channel_id=1, source_target_pairs={{0,1},{1,0},{2,3},{3,2},{4,5},{5,4},{6,7},{7,6},{8,9},{9,8},{10,11... | collective-permute-start | bytes 393224 | tf_op jit(solution)/shard_map/ppermute | solution.py:215
  1.9 1.0 %collective-permute-done.5 = f32[256,128]{1,0:T(8,128)S(1)} collective-permute-done((f32[256,128]{1,0:T(8,128)S(1)}, f32[256,128]{1,0:T(8,128)S(1)}, u32[]{:S(2)}, u32[]{:S(2)}) %collective-permute-start.5) | collective-permute-done | bytes 131104 | tf_op jit(solution)/shard_map/ppermute | solution.py:215
  2.9 3.0 %collective-permute-start.6 = (f32[256,128]{1,0:T(8,128)S(1)}, f32[256,128]{1,0:T(8,128)S(1)}, u32[]{:S(2)}, u32[]{:S(2)}) collective-permute-start(f32[256,128]{1,0:T(8,128)S(1)} %multiply_add_fusion.2), channel_id=1, source_target_pairs={{0,2},{1,3},{2,0},{3,1},{4,6},{5,7},{6,4},{7,5},{8,10},{9,11},{10,... | collective-permute-start | bytes 393224 | tf_op jit(solution)/shard_map/ppermute | solution.py:215
  5.9 1.5 %collective-permute-start = (f32[8,128]{1,0:T(8,128)S(1)}, f32[8,128]{1,0:T(8,128)S(1)}, u32[]{:S(2)}, u32[]{:S(2)}) collective-permute-start(f32[8,128]{1,0:T(8,128)S(1)} %get-tuple-element.14), channel_id=1, source_target_pairs={{0,8},{8,0},{16,24},{24,16},{1,9},{9,1},{17,25},{25,17},{2,10},{10... | collective-permute-start | bytes 12296 | tf_op jit(solution)/shard_map/ppermute | solution.py:215
  7.4 2.1 %collective-permute-done = f32[8,128]{1,0:T(8,128)S(1)} collective-permute-done((f32[8,128]{1,0:T(8,128)S(1)}, f32[8,128]{1,0:T(8,128)S(1)}, u32[]{:S(2)}, u32[]{:S(2)}) %collective-permute-start) | collective-permute-done | bytes 4128 | tf_op jit(solution)/shard_map/ppermute | solution.py:215
  9.5 1.5 %collective-permute-start.1 = (f32[8,128]{1,0:T(8,128)S(1)}, f32[8,128]{1,0:T(8,128)S(1)}, u32[]{:S(2)}, u32[]{:S(2)}) collective-permute-start(f32[8,128]{1,0:T(8,128)S(1)} %add.60), channel_id=1, source_target_pairs={{0,16},{8,24},{16,0},{24,8},{1,17},{9,25},{17,1},{25,9},{2,18},{10... | collective-permute-start | bytes 12296 | tf_op jit(solution)/shard_map/ppermute | solution.py:215
  11.0 2.1 %collective-permute-done.1 = f32[8,128]{1,0:T(8,128)S(1)} collective-permute-done((f32[8,128]{1,0:T(8,128)S(1)}, f32[8,128]{1,0:T(8,128)S(1)}, u32[]{:S(2)}, u32[]{:S(2)}) %collective-permute-start.1) | collective-permute-done | bytes 4128 | tf_op jit(solution)/shard_map/ppermute | solution.py:215
  13.1 0.0 collective-permute-done.6
  13.1 0.0 copy-start.1
  13.2 2.5 %collective-permute-start.7 = (f32[264,128]{1,0:T(8,128)S(1)}, f32[264,128]{1,0:T(8,128)S(1)}, u32[]{:S(2)}, u32[]{:S(2)}) collective-permute-start(f32[264,128]{1,0:T(8,128)S(1)} %pad_maximum_fusion), channel_id=1, source_target_pairs={{0,6},{1,7},{2,4},{3,5},{4,2},{5,3},{6,0},{7,1},{8,14},{9,15},{10,... | collective-permute-start | bytes 405512 | tf_op jit(solution)/shard_map/ppermute | solution.py:215
  15.7 0.0 copy-start.2
  15.7 0.0 copy-start.3
  15.7 0.0 copy-done.1
  15.7 0.6 %copy-done.2 = s32[1,8]{1,0:T(1,128)S(1)} copy-done((s32[1,8]{1,0:T(1,128)S(1)}, s32[1,8]{1,0:T(1,128)}, u32[]{:S(2)}) %copy-start.2) | copy-done | bytes 56
  16.4 0.0 copy-done.3
  16.4 2.4 %null.1 = (f32[256,512]{1,0:T(8,128)S(1)}, bf16[512,512]{1,0:T(8,128)(2,1)S(1)}, bf16[512,512]{1,0:T(8,128)(2,1)S(1)}) custom-call(s32[1,8]{1,0:T(1,128)S(1)} %copy-done.2, f32[64]{0:T(128)S(1)} %copy-done.3, bf16[256,512]{1,0:T(8,128)(2,1)S(1)} %bitcast.4), custom_call_target="tpu_custom_call" | custom-call | flops 67108864 | bytes 786432 | tf_op jit(solution)/shard_map/null/pallas_call | solution.py:335
  18.8 0.1 collective-permute-start.2
  18.8 1.3 %collective-permute-done.7 = f32[264,128]{1,0:T(8,128)S(1)} collective-permute-done((f32[264,128]{1,0:T(8,128)S(1)}, f32[264,128]{1,0:T(8,128)S(1)}, u32[]{:S(2)}, u32[]{:S(2)}) %collective-permute-start.7) | collective-permute-done | bytes 135200 | tf_op jit(solution)/shard_map/ppermute | solution.py:215
  20.2 0.1 broadcast_select_fusion
  20.2 0.1 collective-permute-start.8
  20.3 0.0 collective-permute-done.2
  20.3 2.2 %collective-permute-start.4 = (f32[8,128]{1,0:T(8,128)S(1)}, f32[8,128]{1,0:T(8,128)S(1)}, u32[]{:S(2)}, u32[]{:S(2)}) collective-permute-start(f32[8,128]{1,0:T(8,128)S(1)} %multiply_add_fusion.4), channel_id=1, source_target_pairs={{0,4},{1,5},{2,6},{3,7},{4,0},{5,1},{6,2},{7,3},{8,12},{9,13},{10,... | collective-permute-start | bytes 12296 | tf_op jit(solution)/shard_map/ppermute | solution.py:215
  22.5 0.9 %collective-permute-start.3 = (f32[8,128]{1,0:T(8,128)S(1)}, f32[8,128]{1,0:T(8,128)S(1)}, u32[]{:S(2)}, u32[]{:S(2)}) collective-permute-start(f32[8,128]{1,0:T(8,128)S(1)} %multiply_add_fusion.4), channel_id=1, source_target_pairs={{0,2},{1,3},{2,0},{3,1},{4,6},{5,7},{6,4},{7,5},{8,10},{9,11},{10,... | collective-permute-start | bytes 12296 | tf_op jit(solution)/shard_map/ppermute | solution.py:215
  23.4 0.0 collective-permute-done.8.other_ref
  23.4 0.6 %square.1 = (f32[512,256]{1,0:T(8,128)S(1)}, f32[512,256]{1,0:T(8,128)S(1)}, f32[16,128]{1,0:T(8,128)S(1)}) custom-call(s32[1]{0:T(128)} %bitcast.parity_ref, f32[256,128]{1,0:T(8,128)S(1)} %get-tuple-element.23.own_ref, f32[264,128]{1,0:T(8,128)S(1)} %collective-permute-done.8.other_ref), custom_call_target="tpu_custom_call" | custom-call | flops 402653184 | bytes 1048576 | tf_op jit(solution)/shard_map/square/pallas_call | solution.py:351
  24.1 0.8 %collective-permute-done.4 = f32[8,128]{1,0:T(8,128)S(1)} collective-permute-done((f32[8,128]{1,0:T(8,128)S(1)}, f32[8,128]{1,0:T(8,128)S(1)}, u32[]{:S(2)}, u32[]{:S(2)}) %collective-permute-start.4) | collective-permute-done | bytes 4128 | tf_op jit(solution)/shard_map/ppermute | solution.py:215
  24.9 1.2 %collective-permute-done.3 = f32[8,128]{1,0:T(8,128)S(1)} collective-permute-done((f32[8,128]{1,0:T(8,128)S(1)}, f32[8,128]{1,0:T(8,128)S(1)}, u32[]{:S(2)}, u32[]{:S(2)}) %collective-permute-start.3) | collective-permute-done | bytes 4128 | tf_op jit(solution)/shard_map/ppermute | solution.py:215
  26.2 1.9 %whiten.1 = f32[256,512]{1,0:T(8,128)} custom-call(f32[8,128]{1,0:T(8,128)S(1)} %multiply_add_fusion.3.band_ref, f32[16,128]{1,0:T(8,128)S(1)} %get-tuple-element.17.stats_ref, f32[512,256]{1,0:T(8,128)S(1)} %get-tuple-element.18.cov_ref, f32[512,256]{1,0:T(8,128)S(1)} %get-tuple-element.19.square_ref, f32[256,512]{1,0:T(8,128)S(1)} %get-tuple-element.20.w_ref, ...), custom_call_target="tpu_custom_call" | custom-call | flops 805306368 | bytes 1048576 | tf_op jit(solution)/shard_map/whiten/pallas_call | solution.py:368
  (9 shorter events, 0.1 us)
Async XLA Ops:
  0.0 0.9 %copy-start = (bf16[1,256,512]{2,1,0:T(8,128)(2,1)S(1)}, bf16[1,256,512]{2,1,0:T(8,128)(2,1)}, u32[]{:S(2)}) copy-start(bf16[1,256,512]{2,1,0:T(8,128)(2,1)} %param.3) | copy-start | bytes 786436
  1.3 1.5 %collective-permute-start.5 = (f32[256,128]{1,0:T(8,128)S(1)}, f32[256,128]{1,0:T(8,128)S(1)}, u32[]{:S(2)}, u32[]{:S(2)}) collective-permute-start(f32[256,128]{1,0:T(8,128)S(1)} %get-tuple-element.16), channel_id=1, source_target_pairs={{0,1},{1,0},{2,3},{3,2},{4,5},{5,4},{6,7},{7,6},{8,9},{9,8},{10,11... | collective-permute-start | bytes 393224 | tf_op jit(solution)/shard_map/ppermute | solution.py:215
  2.9 10.2 %collective-permute-start.6 = (f32[256,128]{1,0:T(8,128)S(1)}, f32[256,128]{1,0:T(8,128)S(1)}, u32[]{:S(2)}, u32[]{:S(2)}) collective-permute-start(f32[256,128]{1,0:T(8,128)S(1)} %multiply_add_fusion.2), channel_id=1, source_target_pairs={{0,2},{1,3},{2,0},{3,1},{4,6},{5,7},{6,4},{7,5},{8,10},{9,11},{10,... | collective-permute-start | bytes 393224 | tf_op jit(solution)/shard_map/ppermute | solution.py:215
  5.9 3.6 %collective-permute-start = (f32[8,128]{1,0:T(8,128)S(1)}, f32[8,128]{1,0:T(8,128)S(1)}, u32[]{:S(2)}, u32[]{:S(2)}) collective-permute-start(f32[8,128]{1,0:T(8,128)S(1)} %get-tuple-element.14), channel_id=1, source_target_pairs={{0,8},{8,0},{16,24},{24,16},{1,9},{9,1},{17,25},{25,17},{2,10},{10... | collective-permute-start | bytes 12296 | tf_op jit(solution)/shard_map/ppermute | solution.py:215
  9.5 3.6 %collective-permute-start.1 = (f32[8,128]{1,0:T(8,128)S(1)}, f32[8,128]{1,0:T(8,128)S(1)}, u32[]{:S(2)}, u32[]{:S(2)}) collective-permute-start(f32[8,128]{1,0:T(8,128)S(1)} %add.60), channel_id=1, source_target_pairs={{0,16},{8,24},{16,0},{24,8},{1,17},{9,25},{17,1},{25,9},{2,18},{10... | collective-permute-start | bytes 12296 | tf_op jit(solution)/shard_map/ppermute | solution.py:215
  13.1 2.6 %copy-start.1 = (bf16[1,256,512]{2,1,0:T(8,128)(2,1)S(1)}, bf16[1,256,512]{2,1,0:T(8,128)(2,1)}, u32[]{:S(2)}) copy-start(bf16[1,256,512]{2,1,0:T(8,128)(2,1)} %param.3) | copy-start | bytes 786436
  13.2 7.0 %collective-permute-start.7 = (f32[264,128]{1,0:T(8,128)S(1)}, f32[264,128]{1,0:T(8,128)S(1)}, u32[]{:S(2)}, u32[]{:S(2)}) collective-permute-start(f32[264,128]{1,0:T(8,128)S(1)} %pad_maximum_fusion), channel_id=1, source_target_pairs={{0,6},{1,7},{2,4},{3,5},{4,2},{5,3},{6,0},{7,1},{8,14},{9,15},{10,... | collective-permute-start | bytes 405512 | tf_op jit(solution)/shard_map/ppermute | solution.py:215
  15.7 0.7 %copy-start.2 = (s32[1,8]{1,0:T(1,128)S(1)}, s32[1,8]{1,0:T(1,128)}, u32[]{:S(2)}) copy-start(s32[1,8]{1,0:T(1,128)} %picks_ref.1) | copy-start | bytes 100
  15.7 0.7 %copy-start.3 = (f32[64]{0:T(128)S(1)}, f32[64]{0:T(128)}, u32[]{:S(2)}) copy-start(f32[64]{0:T(128)} %angles_ref.1) | copy-start | bytes 772
  18.8 1.6 %collective-permute-start.2 = (f32[8,128]{1,0:T(8,128)S(1)}, f32[8,128]{1,0:T(8,128)S(1)}, u32[]{:S(2)}, u32[]{:S(2)}) collective-permute-start(f32[8,128]{1,0:T(8,128)S(1)} %add.61), channel_id=1, source_target_pairs={{0,1},{1,0},{2,3},{3,2},{4,5},{5,4},{6,7},{7,6},{8,9},{9,8},{10,11... | collective-permute-start | bytes 12296 | tf_op jit(solution)/shard_map/ppermute | solution.py:215
  20.2 3.2 %collective-permute-start.8 = (f32[264,128]{1,0:T(8,128)S(1)}, f32[264,128]{1,0:T(8,128)S(1)}, u32[]{:S(2)}, u32[]{:S(2)}) collective-permute-start(f32[264,128]{1,0:T(8,128)S(1)} %pad_maximum_fusion.1), channel_id=1, source_target_pairs={{0,1},{1,0},{2,3},{3,2},{4,5},{5,4},{6,7},{7,6},{8,9},{9,8},{10,11... | collective-permute-start | bytes 405512 | tf_op jit(solution)/shard_map/ppermute | solution.py:215
  20.3 4.6 %collective-permute-start.4 = (f32[8,128]{1,0:T(8,128)S(1)}, f32[8,128]{1,0:T(8,128)S(1)}, u32[]{:S(2)}, u32[]{:S(2)}) collective-permute-start(f32[8,128]{1,0:T(8,128)S(1)} %multiply_add_fusion.4), channel_id=1, source_target_pairs={{0,4},{1,5},{2,6},{3,7},{4,0},{5,1},{6,2},{7,3},{8,12},{9,13},{10,... | collective-permute-start | bytes 12296 | tf_op jit(solution)/shard_map/ppermute | solution.py:215
  22.5 3.6 %collective-permute-start.3 = (f32[8,128]{1,0:T(8,128)S(1)}, f32[8,128]{1,0:T(8,128)S(1)}, u32[]{:S(2)}, u32[]{:S(2)}) collective-permute-start(f32[8,128]{1,0:T(8,128)S(1)} %multiply_add_fusion.4), channel_id=1, source_target_pairs={{0,2},{1,3},{2,0},{3,1},{4,6},{5,7},{6,4},{7,5},{8,10},{9,11},{10,... | collective-permute-start | bytes 12296 | tf_op jit(solution)/shard_map/ppermute | solution.py:215

commit v8 on v7

--- a/solution.py
+++ b/solution.py
@@ -22,7 +22,7 @@
 PARAMS = pltpu.CompilerParams(vmem_limit_bytes=24 * 2**20)
 
 
-def gram_kernel(parity_ref, volts_ref, keep_ref, give_ref, power_ref, mixed_ref):
+def gram_kernel(parity_ref, volts_ref, keep_ref, give_ref, power_ref):
     antennas = volts_ref.shape[1] // 2
     segments = volts_ref.shape[0] // SEG
     half = antennas // 2
@@ -39,14 +39,14 @@
         squares = a.astype(F32) ** 2 + b.astype(F32) ** 2
         squares = jnp.sum(squares.reshape(-1, 8, antennas), axis=0)
         power = squares if power is None else forget * power + squares
-    mixed_ref[...] = mixed
     power_ref[...] = jnp.broadcast_to(jnp.sum(power, keepdims=True) / antennas, power_ref.shape)
-    parity = parity_ref[0]
+    is_odd = parity_ref[0] == 1
     lanes = keep_ref.shape[1]
     for n in range(antennas // lanes):
         rows, columns = slice(n * half, (n + 1) * half), slice(n * lanes, (n + 1) * lanes)
-        keep_ref[rows, :] = mixed_ref[pl.ds(pl.multiple_of(parity * half, half), half), columns]
-        give_ref[rows, :] = mixed_ref[pl.ds(pl.multiple_of((1 - parity) * half, half), half), columns]
+        upper, lower = mixed[:half, columns], mixed[half:, columns]
+        keep_ref[rows, :] = jnp.where(is_odd, lower, upper)
+        give_ref[rows, :] = jnp.where(is_odd, upper, lower)
 
 
 def split(value):
@@ -76,15 +76,15 @@
     return tuple(over(beside(p, q), beside(q, -p)) for p, q in parts)
 
 
-def square_kernel(parity_ref, own_ref, other_ref, cov_ref, square_ref, stats_ref, mixed_ref):
-    antennas, lanes = mixed_ref.shape[1], own_ref.shape[1]
+def square_kernel(parity_ref, own_ref, other_ref, cov_ref, square_ref, stats_ref):
+    antennas, lanes = cov_ref.shape[1], own_ref.shape[1]
     half = antennas // 2
-    parity = parity_ref[0]
-    for n in range(antennas // lanes):
-        rows, columns = slice(n * half, (n + 1) * half), slice(n * lanes, (n + 1) * lanes)
-        mixed_ref[pl.ds(pl.multiple_of(parity * half, half), half), columns] = own_ref[rows, :]
-        mixed_ref[pl.ds(pl.multiple_of((1 - parity) * half, half), half), columns] = other_ref[rows, :]
-    mixed = mixed_ref[...]
+    is_odd = parity_ref[0] == 1
+    blocks = [slice(n * half, (n + 1) * half) for n in range(antennas // lanes)]
+    mixed = over(
+        jnp.concatenate([jnp.where(is_odd, other_ref[b, :], own_ref[b, :]) for b in blocks], axis=1),
+        jnp.concatenate([jnp.where(is_odd, own_ref[b, :], other_ref[b, :]) for b in blocks], axis=1),
+    )
     flipped = mixed.T
     re, im = 0.5 * (mixed + flipped), 0.5 * (mixed - flipped)
     cov_ref[:antennas, :], cov_ref[antennas:, :] = re, im
@@ -127,15 +127,12 @@
         both = slice(2 * n * size, 2 * (n + 1) * size)
         return dot3((high_ref[both, :], low_ref[both, :]), first)
 
-    steps = {n: begin(n) for n in range(4)}
-    for n in range(CHUNKS):
+    steps = [begin(n) for n in range(CHUNKS)]
+    for n, step in enumerate(steps):
         rows = slice(n * size, (n + 1) * size)
-        step = steps.pop(n)
         w_u, w_v = w_ref[rows, left], w_ref[rows, right]
         u, v = keep_first * w_u + step[:size], keep_first * w_v + step[size:]
         step = dot3(turn(u, v), second)
-        if n + 4 < CHUNKS:
-            steps[n + 4] = begin(n + 4)
         done_ref[rows, left] = omega * (w_u + keep_second * u - step[:size])
         done_ref[rows, right] = omega * (w_v + keep_second * v - step[size:])
         pltpu.make_async_copy(done_ref.at[rows], out_ref.at[rows], sems.at[n]).start()
@@ -291,7 +288,6 @@
         ),
         in_specs=[SM, VM],
         out_specs=(VM, VM, VM),
-        scratch_shapes=[pltpu.VMEM((antennas, antennas), F32)],
         cost_estimate=pl.CostEstimate(
             flops=4 * rows * width * antennas, bytes_accessed=rows * width * 2, transcendentals=0
         ),
@@ -357,7 +353,6 @@
         ),
         in_specs=[SM, VM, VM],
         out_specs=(VM, VM, VM),
-        scratch_shapes=[pltpu.VMEM((antennas, antennas), F32)],
         cost_estimate=pl.CostEstimate(
             flops=6 * width * width * antennas, bytes_accessed=width * antennas * 8, transcendentals=0
         ),

time: 28.2 us -> 28.2 us (level)
  no operation moved by 1% of the time
where the time goes in v8:
time: 28.2 us; the launch traced here: 28 us
  starting transfers between devices  12.3 us (44%)
  waiting for transfers between devices  8.6 us (30%)
  Pallas kernels  5.24 us (19%)
  local copies, waits for them, and re-layouts  1.62 us (6%)
    ppermute x9, starting transfers between devices, exchange(): lax.ppermute(value, axis, [(i, i ^ mask) for i in range(lax.axis_size(axi...  12.3 us
    ppermute x9, waiting for transfers between devices, exchange(): lax.ppermute(value, axis, [(i, i ^ mask) for i in range(lax.axis_size(axi...  8.6 us
    pallas_call x1, Pallas kernels, steps(): pl.pallas_call(null_kernel, out_shape=(jax.ShapeDtypeStruct((rows, width)...  2.37 us
    pallas_call x1, Pallas kernels, steps(): pl.pallas_call(whiten_kernel, out_shape=jax.ShapeDtypeStruct((rows, width...  1.89 us
    unnamed x8, local copies, waits for them, and re-layouts  1.62 us
    pallas_call x1, Pallas kernels, steps(): pl.pallas_call(square_kernel, out_shape=(jax.ShapeDtypeStruct((width, ant...  0.62 us
  transfers between devices with their start and end apart: 9, of which 6 were waited for; matrix products, arithmetic and copies ran while one was open for 0% of the time, Pallas kernels for 11%

profile of v8, /device:TPU:0, one launch (start us, length us, event | category | flops | bytes accessed | tf_op | source)
XLA Modules:
  0.0 28.0 jit_solution(7967677469725574754)
XLA Ops:
  0.0 0.0 copy-start
  0.0 0.9 %copy-done = bf16[1,256,512]{2,1,0:T(8,128)(2,1)S(1)} copy-done((bf16[1,256,512]{2,1,0:T(8,128)(2,1)S(1)}, bf16[1,256,512]{2,1,0:T(8,128)(2,1)}, u32[]{:S(2)}) %copy-start) | copy-done | bytes 262168
  1.0 0.4 %segment_gram.1 = (f32[256,128]{1,0:T(8,128)S(1)}, f32[256,128]{1,0:T(8,128)S(1)}, f32[8,128]{1,0:T(8,128)S(1)}) custom-call(s32[1]{0:T(128)} %bitcast.parity_ref, bf16[256,512]{1,0:T(8,128)(2,1)S(1)} %bitcast.3), custom_call_target="tpu_custom_call" | custom-call | flops 134217728 | bytes 262144 | tf_op jit(solution)/shard_map/segment_gram/pallas_call | solution.py:282
  1.3 0.6 %collective-permute-start.5 = (f32[256,128]{1,0:T(8,128)S(1)}, f32[256,128]{1,0:T(8,128)S(1)}, u32[]{:S(2)}, u32[]{:S(2)}) collective-permute-start(f32[256,128]{1,0:T(8,128)S(1)} %get-tuple-element.16), channel_id=1, source_target_pairs={{0,1},{1,0},{2,3},{3,2},{4,5},{5,4},{6,7},{7,6},{8,9},{9,8},{10,11... | collective-permute-start | bytes 393224 | tf_op jit(solution)/shard_map/ppermute | solution.py:212
  1.9 1.0 %collective-permute-done.5 = f32[256,128]{1,0:T(8,128)S(1)} collective-permute-done((f32[256,128]{1,0:T(8,128)S(1)}, f32[256,128]{1,0:T(8,128)S(1)}, u32[]{:S(2)}, u32[]{:S(2)}) %collective-permute-start.5) | collective-permute-done | bytes 131104 | tf_op jit(solution)/shard_map/ppermute | solution.py:212
  2.9 3.0 %collective-permute-start.6 = (f32[256,128]{1,0:T(8,128)S(1)}, f32[256,128]{1,0:T(8,128)S(1)}, u32[]{:S(2)}, u32[]{:S(2)}) collective-permute-start(f32[256,128]{1,0:T(8,128)S(1)} %multiply_add_fusion.2), channel_id=1, source_target_pairs={{0,2},{1,3},{2,0},{3,1},{4,6},{5,7},{6,4},{7,5},{8,10},{9,11},{10,... | collective-permute-start | bytes 393224 | tf_op jit(solution)/shard_map/ppermute | solution.py:212
  5.9 1.5 %collective-permute-start = (f32[8,128]{1,0:T(8,128)S(1)}, f32[8,128]{1,0:T(8,128)S(1)}, u32[]{:S(2)}, u32[]{:S(2)}) collective-permute-start(f32[8,128]{1,0:T(8,128)S(1)} %get-tuple-element.14), channel_id=1, source_target_pairs={{0,8},{8,0},{16,24},{24,16},{1,9},{9,1},{17,25},{25,17},{2,10},{10... | collective-permute-start | bytes 12296 | tf_op jit(solution)/shard_map/ppermute | solution.py:212
  7.4 2.1 %collective-permute-done = f32[8,128]{1,0:T(8,128)S(1)} collective-permute-done((f32[8,128]{1,0:T(8,128)S(1)}, f32[8,128]{1,0:T(8,128)S(1)}, u32[]{:S(2)}, u32[]{:S(2)}) %collective-permute-start) | collective-permute-done | bytes 4128 | tf_op jit(solution)/shard_map/ppermute | solution.py:212
  9.5 1.5 %collective-permute-start.1 = (f32[8,128]{1,0:T(8,128)S(1)}, f32[8,128]{1,0:T(8,128)S(1)}, u32[]{:S(2)}, u32[]{:S(2)}) collective-permute-start(f32[8,128]{1,0:T(8,128)S(1)} %add.60), channel_id=1, source_target_pairs={{0,16},{8,24},{16,0},{24,8},{1,17},{9,25},{17,1},{25,9},{2,18},{10... | collective-permute-start | bytes 12296 | tf_op jit(solution)/shard_map/ppermute | solution.py:212
  11.0 2.1 %collective-permute-done.1 = f32[8,128]{1,0:T(8,128)S(1)} collective-permute-done((f32[8,128]{1,0:T(8,128)S(1)}, f32[8,128]{1,0:T(8,128)S(1)}, u32[]{:S(2)}, u32[]{:S(2)}) %collective-permute-start.1) | collective-permute-done | bytes 4128 | tf_op jit(solution)/shard_map/ppermute | solution.py:212
  13.1 0.0 collective-permute-done.6
  13.1 0.0 copy-start.1
  13.1 2.5 %collective-permute-start.7 = (f32[264,128]{1,0:T(8,128)S(1)}, f32[264,128]{1,0:T(8,128)S(1)}, u32[]{:S(2)}, u32[]{:S(2)}) collective-permute-start(f32[264,128]{1,0:T(8,128)S(1)} %pad_maximum_fusion), channel_id=1, source_target_pairs={{0,6},{1,7},{2,4},{3,5},{4,2},{5,3},{6,0},{7,1},{8,14},{9,15},{10,... | collective-permute-start | bytes 405512 | tf_op jit(solution)/shard_map/ppermute | solution.py:212
  15.7 0.0 copy-start.2
  15.7 0.0 copy-start.3
  15.7 0.0 copy-done.1
  15.7 0.6 %copy-done.2 = s32[1,8]{1,0:T(1,128)S(1)} copy-done((s32[1,8]{1,0:T(1,128)S(1)}, s32[1,8]{1,0:T(1,128)}, u32[]{:S(2)}) %copy-start.2) | copy-done | bytes 56
  16.3 0.0 copy-done.3
  16.4 2.4 %null.1 = (f32[256,512]{1,0:T(8,128)S(1)}, bf16[512,512]{1,0:T(8,128)(2,1)S(1)}, bf16[512,512]{1,0:T(8,128)(2,1)S(1)}) custom-call(s32[1,8]{1,0:T(1,128)S(1)} %copy-done.2, f32[64]{0:T(128)S(1)} %copy-done.3, bf16[256,512]{1,0:T(8,128)(2,1)S(1)} %bitcast.4), custom_call_target="tpu_custom_call" | custom-call | flops 67108864 | bytes 786432 | tf_op jit(solution)/shard_map/null/pallas_call | solution.py:331
  18.7 0.1 collective-permute-start.2
  18.8 1.3 %collective-permute-done.7 = f32[264,128]{1,0:T(8,128)S(1)} collective-permute-done((f32[264,128]{1,0:T(8,128)S(1)}, f32[264,128]{1,0:T(8,128)S(1)}, u32[]{:S(2)}, u32[]{:S(2)}) %collective-permute-start.7) | collective-permute-done | bytes 135200 | tf_op jit(solution)/shard_map/ppermute | solution.py:212
  20.1 0.1 broadcast_select_fusion
  20.2 0.1 collective-permute-start.8
  20.3 0.0 collective-permute-done.2
  20.3 2.2 %collective-permute-start.4 = (f32[8,128]{1,0:T(8,128)S(1)}, f32[8,128]{1,0:T(8,128)S(1)}, u32[]{:S(2)}, u32[]{:S(2)}) collective-permute-start(f32[8,128]{1,0:T(8,128)S(1)} %multiply_add_fusion.4), channel_id=1, source_target_pairs={{0,4},{1,5},{2,6},{3,7},{4,0},{5,1},{6,2},{7,3},{8,12},{9,13},{10,... | collective-permute-start | bytes 12296 | tf_op jit(solution)/shard_map/ppermute | solution.py:212
  22.5 0.9 %collective-permute-start.3 = (f32[8,128]{1,0:T(8,128)S(1)}, f32[8,128]{1,0:T(8,128)S(1)}, u32[]{:S(2)}, u32[]{:S(2)}) collective-permute-start(f32[8,128]{1,0:T(8,128)S(1)} %multiply_add_fusion.4), channel_id=1, source_target_pairs={{0,2},{1,3},{2,0},{3,1},{4,6},{5,7},{6,4},{7,5},{8,10},{9,11},{10,... | collective-permute-start | bytes 12296 | tf_op jit(solution)/shard_map/ppermute | solution.py:212
  23.4 0.0 collective-permute-done.8.other_ref
  23.4 0.6 %square.1 = (f32[512,256]{1,0:T(8,128)S(1)}, f32[512,256]{1,0:T(8,128)S(1)}, f32[16,128]{1,0:T(8,128)S(1)}) custom-call(s32[1]{0:T(128)} %bitcast.parity_ref, f32[256,128]{1,0:T(8,128)S(1)} %get-tuple-element.23.own_ref, f32[264,128]{1,0:T(8,128)S(1)} %collective-permute-done.8.other_ref), custom_call_target="tpu_custom_call" | custom-call | flops 402653184 | bytes 1048576 | tf_op jit(solution)/shard_map/square/pallas_call | solution.py:347
  24.0 0.8 %collective-permute-done.4 = f32[8,128]{1,0:T(8,128)S(1)} collective-permute-done((f32[8,128]{1,0:T(8,128)S(1)}, f32[8,128]{1,0:T(8,128)S(1)}, u32[]{:S(2)}, u32[]{:S(2)}) %collective-permute-start.4) | collective-permute-done | bytes 4128 | tf_op jit(solution)/shard_map/ppermute | solution.py:212
  24.9 1.2 %collective-permute-done.3 = f32[8,128]{1,0:T(8,128)S(1)} collective-permute-done((f32[8,128]{1,0:T(8,128)S(1)}, f32[8,128]{1,0:T(8,128)S(1)}, u32[]{:S(2)}, u32[]{:S(2)}) %collective-permute-start.3) | collective-permute-done | bytes 4128 | tf_op jit(solution)/shard_map/ppermute | solution.py:212
  26.1 1.9 %whiten.1 = f32[256,512]{1,0:T(8,128)} custom-call(f32[8,128]{1,0:T(8,128)S(1)} %multiply_add_fusion.3.band_ref, f32[16,128]{1,0:T(8,128)S(1)} %get-tuple-element.17.stats_ref, f32[512,256]{1,0:T(8,128)S(1)} %get-tuple-element.18.cov_ref, f32[512,256]{1,0:T(8,128)S(1)} %get-tuple-element.19.square_ref, f32[256,512]{1,0:T(8,128)S(1)} %get-tuple-element.20.w_ref, ...), custom_call_target="tpu_custom_call" | custom-call | flops 805306368 | bytes 1048576 | tf_op jit(solution)/shard_map/whiten/pallas_call | solution.py:363
  (9 shorter events, 0.1 us)
Async XLA Ops:
  0.0 0.9 %copy-start = (bf16[1,256,512]{2,1,0:T(8,128)(2,1)S(1)}, bf16[1,256,512]{2,1,0:T(8,128)(2,1)}, u32[]{:S(2)}) copy-start(bf16[1,256,512]{2,1,0:T(8,128)(2,1)} %param.3) | copy-start | bytes 786436
  1.3 1.5 %collective-permute-start.5 = (f32[256,128]{1,0:T(8,128)S(1)}, f32[256,128]{1,0:T(8,128)S(1)}, u32[]{:S(2)}, u32[]{:S(2)}) collective-permute-start(f32[256,128]{1,0:T(8,128)S(1)} %get-tuple-element.16), channel_id=1, source_target_pairs={{0,1},{1,0},{2,3},{3,2},{4,5},{5,4},{6,7},{7,6},{8,9},{9,8},{10,11... | collective-permute-start | bytes 393224 | tf_op jit(solution)/shard_map/ppermute | solution.py:212
  2.9 10.2 %collective-permute-start.6 = (f32[256,128]{1,0:T(8,128)S(1)}, f32[256,128]{1,0:T(8,128)S(1)}, u32[]{:S(2)}, u32[]{:S(2)}) collective-permute-start(f32[256,128]{1,0:T(8,128)S(1)} %multiply_add_fusion.2), channel_id=1, source_target_pairs={{0,2},{1,3},{2,0},{3,1},{4,6},{5,7},{6,4},{7,5},{8,10},{9,11},{10,... | collective-permute-start | bytes 393224 | tf_op jit(solution)/shard_map/ppermute | solution.py:212
  5.9 3.6 %collective-permute-start = (f32[8,128]{1,0:T(8,128)S(1)}, f32[8,128]{1,0:T(8,128)S(1)}, u32[]{:S(2)}, u32[]{:S(2)}) collective-permute-start(f32[8,128]{1,0:T(8,128)S(1)} %get-tuple-element.14), channel_id=1, source_target_pairs={{0,8},{8,0},{16,24},{24,16},{1,9},{9,1},{17,25},{25,17},{2,10},{10... | collective-permute-start | bytes 12296 | tf_op jit(solution)/shard_map/ppermute | solution.py:212
  9.5 3.6 %collective-permute-start.1 = (f32[8,128]{1,0:T(8,128)S(1)}, f32[8,128]{1,0:T(8,128)S(1)}, u32[]{:S(2)}, u32[]{:S(2)}) collective-permute-start(f32[8,128]{1,0:T(8,128)S(1)} %add.60), channel_id=1, source_target_pairs={{0,16},{8,24},{16,0},{24,8},{1,17},{9,25},{17,1},{25,9},{2,18},{10... | collective-permute-start | bytes 12296 | tf_op jit(solution)/shard_map/ppermute | solution.py:212
  13.1 2.6 %copy-start.1 = (bf16[1,256,512]{2,1,0:T(8,128)(2,1)S(1)}, bf16[1,256,512]{2,1,0:T(8,128)(2,1)}, u32[]{:S(2)}) copy-start(bf16[1,256,512]{2,1,0:T(8,128)(2,1)} %param.3) | copy-start | bytes 786436
  13.1 7.0 %collective-permute-start.7 = (f32[264,128]{1,0:T(8,128)S(1)}, f32[264,128]{1,0:T(8,128)S(1)}, u32[]{:S(2)}, u32[]{:S(2)}) collective-permute-start(f32[264,128]{1,0:T(8,128)S(1)} %pad_maximum_fusion), channel_id=1, source_target_pairs={{0,6},{1,7},{2,4},{3,5},{4,2},{5,3},{6,0},{7,1},{8,14},{9,15},{10,... | collective-permute-start | bytes 405512 | tf_op jit(solution)/shard_map/ppermute | solution.py:212
  15.7 0.7 %copy-start.2 = (s32[1,8]{1,0:T(1,128)S(1)}, s32[1,8]{1,0:T(1,128)}, u32[]{:S(2)}) copy-start(s32[1,8]{1,0:T(1,128)} %picks_ref.1) | copy-start | bytes 100
  15.7 0.7 %copy-start.3 = (f32[64]{0:T(128)S(1)}, f32[64]{0:T(128)}, u32[]{:S(2)}) copy-start(f32[64]{0:T(128)} %angles_ref.1) | copy-start | bytes 772
  18.7 1.5 %collective-permute-start.2 = (f32[8,128]{1,0:T(8,128)S(1)}, f32[8,128]{1,0:T(8,128)S(1)}, u32[]{:S(2)}, u32[]{:S(2)}) collective-permute-start(f32[8,128]{1,0:T(8,128)S(1)} %add.61), channel_id=1, source_target_pairs={{0,1},{1,0},{2,3},{3,2},{4,5},{5,4},{6,7},{7,6},{8,9},{9,8},{10,11... | collective-permute-start | bytes 12296 | tf_op jit(solution)/shard_map/ppermute | solution.py:212
  20.2 3.2 %collective-permute-start.8 = (f32[264,128]{1,0:T(8,128)S(1)}, f32[264,128]{1,0:T(8,128)S(1)}, u32[]{:S(2)}, u32[]{:S(2)}) collective-permute-start(f32[264,128]{1,0:T(8,128)S(1)} %pad_maximum_fusion.1), channel_id=1, source_target_pairs={{0,1},{1,0},{2,3},{3,2},{4,5},{5,4},{6,7},{7,6},{8,9},{9,8},{10,11... | collective-permute-start | bytes 405512 | tf_op jit(solution)/shard_map/ppermute | solution.py:212
  20.3 4.6 %collective-permute-start.4 = (f32[8,128]{1,0:T(8,128)S(1)}, f32[8,128]{1,0:T(8,128)S(1)}, u32[]{:S(2)}, u32[]{:S(2)}) collective-permute-start(f32[8,128]{1,0:T(8,128)S(1)} %multiply_add_fusion.4), channel_id=1, source_target_pairs={{0,4},{1,5},{2,6},{3,7},{4,0},{5,1},{6,2},{7,3},{8,12},{9,13},{10,... | collective-permute-start | bytes 12296 | tf_op jit(solution)/shard_map/ppermute | solution.py:212
  22.5 3.6 %collective-permute-start.3 = (f32[8,128]{1,0:T(8,128)S(1)}, f32[8,128]{1,0:T(8,128)S(1)}, u32[]{:S(2)}, u32[]{:S(2)}) collective-permute-start(f32[8,128]{1,0:T(8,128)S(1)} %multiply_add_fusion.4), channel_id=1, source_target_pairs={{0,2},{1,3},{2,0},{3,1},{4,6},{5,7},{6,4},{7,5},{8,10},{9,11},{10,... | collective-permute-start | bytes 12296 | tf_op jit(solution)/shard_map/ppermute | solution.py:212

commit v9 on v8

--- a/solution.py
+++ b/solution.py
@@ -22,31 +22,32 @@
 PARAMS = pltpu.CompilerParams(vmem_limit_bytes=24 * 2**20)
 
 
-def gram_kernel(parity_ref, volts_ref, keep_ref, give_ref, power_ref):
+def gram_kernel(part_ref, volts_ref, out_ref, *power_ref):
     antennas = volts_ref.shape[1] // 2
     segments = volts_ref.shape[0] // SEG
-    half = antennas // 2
+    half, lanes = antennas // 2, out_ref.shape[1]
     forget = 1.0 - 1.0 / HORIZON
+    start = pl.multiple_of(part_ref[0] * half, half)
     mixed = power = None
     for seg in range(segments):
-        a = volts_ref[seg * SEG : (seg + 1) * SEG, :antennas]
-        b = volts_ref[seg * SEG : (seg + 1) * SEG, antennas:]
-        a_t, b_t = a.T, b.T
+        rows = slice(seg * SEG, (seg + 1) * SEG)
+        a, b = volts_ref[rows, :antennas], volts_ref[rows, antennas:]
+        a_t = volts_ref[rows, pl.ds(start, half)].T
+        b_t = volts_ref[rows, pl.ds(antennas + start, half)].T
         left = jnp.concatenate([a_t, b_t, b_t, -a_t], axis=1)
         right = jnp.concatenate([a, b, a, b], axis=0)
         term = jnp.dot(left, right, preferred_element_type=F32)
         mixed = term if mixed is None else forget * mixed + term
-        squares = a.astype(F32) ** 2 + b.astype(F32) ** 2
-        squares = jnp.sum(squares.reshape(-1, 8, antennas), axis=0)
-        power = squares if power is None else forget * power + squares
-    power_ref[...] = jnp.broadcast_to(jnp.sum(power, keepdims=True) / antennas, power_ref.shape)
-    is_odd = parity_ref[0] == 1
-    lanes = keep_ref.shape[1]
+        if power_ref:
+            squares = a.astype(F32) ** 2 + b.astype(F32) ** 2
+            squares = jnp.sum(squares.reshape(-1, 8, antennas), axis=0)
+            power = squares if power is None else forget * power + squares
+    if power_ref:
+        power_ref[0][...] = jnp.broadcast_to(
+            jnp.sum(power, keepdims=True) / antennas, power_ref[0].shape
+        )
     for n in range(antennas // lanes):
-        rows, columns = slice(n * half, (n + 1) * half), slice(n * lanes, (n + 1) * lanes)
-        upper, lower = mixed[:half, columns], mixed[half:, columns]
-        keep_ref[rows, :] = jnp.where(is_odd, lower, upper)
-        give_ref[rows, :] = jnp.where(is_odd, upper, lower)
+        out_ref[n * half : (n + 1) * half, :] = mixed[:, n * lanes : (n + 1) * lanes]
 
 
 def split(value):
@@ -279,22 +280,20 @@
     is_odd = core == 1
     decay = (1.0 - 1.0 / HORIZON) ** segments
 
-    keep, give, power = pl.pallas_call(
-        gram_kernel,
-        out_shape=(
-            jax.ShapeDtypeStruct((half * antennas // LANES, LANES), F32),
-            jax.ShapeDtypeStruct((half * antennas // LANES, LANES), F32),
-            jax.ShapeDtypeStruct((8, LANES), F32),
-        ),
-        in_specs=[SM, VM],
-        out_specs=(VM, VM, VM),
-        cost_estimate=pl.CostEstimate(
-            flops=4 * rows * width * antennas, bytes_accessed=rows * width * 2, transcendentals=0
-        ),
-        compiler_params=PARAMS,
-        name="segment_gram",
-    )(parity, voltage)
-
+    def gram(part, *more):
+        return pl.pallas_call(
+            gram_kernel,
+            out_shape=(jax.ShapeDtypeStruct((half * antennas // LANES, LANES), F32), *more),
+            in_specs=[SM, VM],
+            out_specs=(VM,) * (1 + len(more)),
+            cost_estimate=pl.CostEstimate(
+                flops=2 * rows * width * antennas, bytes_accessed=rows * width * 2, transcendentals=0
+            ),
+            compiler_params=PARAMS,
+        )(part, voltage)
+
+    give, power = gram(1 - parity, jax.ShapeDtypeStruct((8, LANES), F32))
+    (keep,) = gram(parity)
     got = exchange(give, "tm", 1)
     mine, theirs = jnp.where(is_odd, 1.0, decay), jnp.where(is_odd, decay, 1.0)
     pair = mine * keep + theirs * got

time: 28.2 us -> 28.1 us (level)
  waiting for transfers between devices: 8.6 us -> 8.19 us
    ppermute x9, waiting for transfers between devices: 8.6 us -> 8.19 us  [exchange(): lax.ppermute(value, axis, [(i, i ^ mask) for i in range(lax.axis_size(axi...]
  transfers between devices with their start and end apart: 9 -> 9, of which waited for: 6 -> 6; matrix products, arithmetic and copies ran while one was open for 0% -> 0% of each run, Pallas kernels for 11% -> 12%
where the time goes in v9:
time: 28.1 us; the launch traced here: 27.9 us
  starting transfers between devices  12.4 us (44%)
  waiting for transfers between devices  8.19 us (29%)
  Pallas kernels  5.44 us (19%)
  local copies, waits for them, and re-layouts  1.73 us (6%)
    ppermute x9, starting transfers between devices, exchange(): lax.ppermute(value, axis, [(i, i ^ mask) for i in range(lax.axis_size(axi...  12.4 us
    ppermute x9, waiting for transfers between devices, exchange(): lax.ppermute(value, axis, [(i, i ^ mask) for i in range(lax.axis_size(axi...  8.19 us
    pallas_call x1, Pallas kernels, steps(): pl.pallas_call(null_kernel, out_shape=(jax.ShapeDtypeStruct((rows, width)...  2.36 us
    pallas_call x1, Pallas kernels, steps(): pl.pallas_call(whiten_kernel, out_shape=jax.ShapeDtypeStruct((rows, width...  1.9 us
    unnamed x8, local copies, waits for them, and re-layouts  1.72 us
    pallas_call x1, Pallas kernels, steps(): pl.pallas_call(square_kernel, out_shape=(jax.ShapeDtypeStruct((width, ant...  0.62 us
  transfers between devices with their start and end apart: 9, of which 6 were waited for; matrix products, arithmetic and copies ran while one was open for 0% of the time, Pallas kernels for 12%

profile of v9, /device:TPU:0, one launch (start us, length us, event | category | flops | bytes accessed | tf_op | source)
XLA Modules:
  0.0 27.9 jit_solution(16973601966800759879)
XLA Ops:
  0.0 0.0 copy-start
  0.0 0.9 %copy-done = bf16[1,256,512]{2,1,0:T(8,128)(2,1)S(1)} copy-done((bf16[1,256,512]{2,1,0:T(8,128)(2,1)S(1)}, bf16[1,256,512]{2,1,0:T(8,128)(2,1)}, u32[]{:S(2)}) %copy-start) | copy-done | bytes 262168
  1.0 0.0 copy-start.1
  1.0 0.3 shard_map.37
  1.2 0.6 %collective-permute-start.5 = (f32[256,128]{1,0:T(8,128)S(1)}, f32[256,128]{1,0:T(8,128)S(1)}, u32[]{:S(2)}, u32[]{:S(2)}) collective-permute-start(f32[256,128]{1,0:T(8,128)S(1)} %get-tuple-element.14), channel_id=1, source_target_pairs={{0,1},{1,0},{2,3},{3,2},{4,5},{5,4},{6,7},{7,6},{8,9},{9,8},{10,11... | collective-permute-start | bytes 393224 | tf_op jit(solution)/shard_map/ppermute | solution.py:213
  1.8 0.1 copy-done.1
  1.9 0.3 shard_map.38
  2.2 0.6 %collective-permute-done.5 = f32[256,128]{1,0:T(8,128)S(1)} collective-permute-done((f32[256,128]{1,0:T(8,128)S(1)}, f32[256,128]{1,0:T(8,128)S(1)}, u32[]{:S(2)}, u32[]{:S(2)}) %collective-permute-start.5) | collective-permute-done | bytes 131104 | tf_op jit(solution)/shard_map/ppermute | solution.py:213
  2.8 3.0 %collective-permute-start.6 = (f32[256,128]{1,0:T(8,128)S(1)}, f32[256,128]{1,0:T(8,128)S(1)}, u32[]{:S(2)}, u32[]{:S(2)}) collective-permute-start(f32[256,128]{1,0:T(8,128)S(1)} %multiply_add_fusion.2), channel_id=1, source_target_pairs={{0,2},{1,3},{2,0},{3,1},{4,6},{5,7},{6,4},{7,5},{8,10},{9,11},{10,... | collective-permute-start | bytes 393224 | tf_op jit(solution)/shard_map/ppermute | solution.py:213
  5.8 1.5 %collective-permute-start = (f32[8,128]{1,0:T(8,128)S(1)}, f32[8,128]{1,0:T(8,128)S(1)}, u32[]{:S(2)}, u32[]{:S(2)}) collective-permute-start(f32[8,128]{1,0:T(8,128)S(1)} %get-tuple-element.13), channel_id=1, source_target_pairs={{0,8},{8,0},{16,24},{24,16},{1,9},{9,1},{17,25},{25,17},{2,10},{10... | collective-permute-start | bytes 12296 | tf_op jit(solution)/shard_map/ppermute | solution.py:213
  7.3 2.1 %collective-permute-done = f32[8,128]{1,0:T(8,128)S(1)} collective-permute-done((f32[8,128]{1,0:T(8,128)S(1)}, f32[8,128]{1,0:T(8,128)S(1)}, u32[]{:S(2)}, u32[]{:S(2)}) %collective-permute-start) | collective-permute-done | bytes 4128 | tf_op jit(solution)/shard_map/ppermute | solution.py:213
  9.4 1.5 %collective-permute-start.1 = (f32[8,128]{1,0:T(8,128)S(1)}, f32[8,128]{1,0:T(8,128)S(1)}, u32[]{:S(2)}, u32[]{:S(2)}) collective-permute-start(f32[8,128]{1,0:T(8,128)S(1)} %add.60), channel_id=1, source_target_pairs={{0,16},{8,24},{16,0},{24,8},{1,17},{9,25},{17,1},{25,9},{2,18},{10... | collective-permute-start | bytes 12296 | tf_op jit(solution)/shard_map/ppermute | solution.py:213
  10.9 2.1 %collective-permute-done.1 = f32[8,128]{1,0:T(8,128)S(1)} collective-permute-done((f32[8,128]{1,0:T(8,128)S(1)}, f32[8,128]{1,0:T(8,128)S(1)}, u32[]{:S(2)}, u32[]{:S(2)}) %collective-permute-start.1) | collective-permute-done | bytes 4128 | tf_op jit(solution)/shard_map/ppermute | solution.py:213
  13.0 0.0 collective-permute-done.6
  13.1 2.5 %collective-permute-start.7 = (f32[264,128]{1,0:T(8,128)S(1)}, f32[264,128]{1,0:T(8,128)S(1)}, u32[]{:S(2)}, u32[]{:S(2)}) collective-permute-start(f32[264,128]{1,0:T(8,128)S(1)} %pad_maximum_fusion), channel_id=1, source_target_pairs={{0,6},{1,7},{2,4},{3,5},{4,2},{5,3},{6,0},{7,1},{8,14},{9,15},{10,... | collective-permute-start | bytes 405512 | tf_op jit(solution)/shard_map/ppermute | solution.py:213
  15.6 0.0 copy-start.2
  15.6 0.0 copy-start.3
  15.6 0.7 %copy-done.2 = s32[1,8]{1,0:T(1,128)S(1)} copy-done((s32[1,8]{1,0:T(1,128)S(1)}, s32[1,8]{1,0:T(1,128)}, u32[]{:S(2)}) %copy-start.2) | copy-done | bytes 56
  16.3 0.0 copy-done.3
  16.3 2.4 %null.1 = (f32[256,512]{1,0:T(8,128)S(1)}, bf16[512,512]{1,0:T(8,128)(2,1)S(1)}, bf16[512,512]{1,0:T(8,128)(2,1)S(1)}) custom-call(s32[1,8]{1,0:T(1,128)S(1)} %copy-done.2, f32[64]{0:T(128)S(1)} %copy-done.3, bf16[256,512]{1,0:T(8,128)(2,1)S(1)} %bitcast.5), custom_call_target="tpu_custom_call" | custom-call | flops 67108864 | bytes 786432 | tf_op jit(solution)/shard_map/null/pallas_call | solution.py:330
  18.6 0.1 collective-permute-start.2
  18.7 1.3 %collective-permute-done.7 = f32[264,128]{1,0:T(8,128)S(1)} collective-permute-done((f32[264,128]{1,0:T(8,128)S(1)}, f32[264,128]{1,0:T(8,128)S(1)}, u32[]{:S(2)}, u32[]{:S(2)}) %collective-permute-start.7) | collective-permute-done | bytes 135200 | tf_op jit(solution)/shard_map/ppermute | solution.py:213
  20.0 0.1 broadcast_select_fusion
  20.1 0.1 collective-permute-start.8
  20.2 0.0 collective-permute-done.2
  20.2 2.2 %collective-permute-start.4 = (f32[8,128]{1,0:T(8,128)S(1)}, f32[8,128]{1,0:T(8,128)S(1)}, u32[]{:S(2)}, u32[]{:S(2)}) collective-permute-start(f32[8,128]{1,0:T(8,128)S(1)} %multiply_add_fusion.4), channel_id=1, source_target_pairs={{0,4},{1,5},{2,6},{3,7},{4,0},{5,1},{6,2},{7,3},{8,12},{9,13},{10,... | collective-permute-start | bytes 12296 | tf_op jit(solution)/shard_map/ppermute | solution.py:213
  22.4 0.9 %collective-permute-start.3 = (f32[8,128]{1,0:T(8,128)S(1)}, f32[8,128]{1,0:T(8,128)S(1)}, u32[]{:S(2)}, u32[]{:S(2)}) collective-permute-start(f32[8,128]{1,0:T(8,128)S(1)} %multiply_add_fusion.4), channel_id=1, source_target_pairs={{0,2},{1,3},{2,0},{3,1},{4,6},{5,7},{6,4},{7,5},{8,10},{9,11},{10,... | collective-permute-start | bytes 12296 | tf_op jit(solution)/shard_map/ppermute | solution.py:213
  23.3 0.0 collective-permute-done.8.other_ref
  23.3 0.6 %square.1 = (f32[512,256]{1,0:T(8,128)S(1)}, f32[512,256]{1,0:T(8,128)S(1)}, f32[16,128]{1,0:T(8,128)S(1)}) custom-call(s32[1]{0:T(128)} %bitcast.part_ref.parity_ref, f32[256,128]{1,0:T(8,128)S(1)} %get-tuple-element.21.own_ref, f32[264,128]{1,0:T(8,128)S(1)} %collective-permute-done.8.other_ref), custom_call_target="tpu_custom_call" | custom-call | flops 402653184 | bytes 1048576 | tf_op jit(solution)/shard_map/square/pallas_call | solution.py:346
  23.9 0.8 %collective-permute-done.4 = f32[8,128]{1,0:T(8,128)S(1)} collective-permute-done((f32[8,128]{1,0:T(8,128)S(1)}, f32[8,128]{1,0:T(8,128)S(1)}, u32[]{:S(2)}, u32[]{:S(2)}) %collective-permute-start.4) | collective-permute-done | bytes 4128 | tf_op jit(solution)/shard_map/ppermute | solution.py:213
  24.8 1.2 %collective-permute-done.3 = f32[8,128]{1,0:T(8,128)S(1)} collective-permute-done((f32[8,128]{1,0:T(8,128)S(1)}, f32[8,128]{1,0:T(8,128)S(1)}, u32[]{:S(2)}, u32[]{:S(2)}) %collective-permute-start.3) | collective-permute-done | bytes 4128 | tf_op jit(solution)/shard_map/ppermute | solution.py:213
  26.0 1.9 %whiten.1 = f32[256,512]{1,0:T(8,128)} custom-call(f32[8,128]{1,0:T(8,128)S(1)} %multiply_add_fusion.3.band_ref, f32[16,128]{1,0:T(8,128)S(1)} %get-tuple-element.15.stats_ref, f32[512,256]{1,0:T(8,128)S(1)} %get-tuple-element.16.cov_ref, f32[512,256]{1,0:T(8,128)S(1)} %get-tuple-element.17.square_ref, f32[256,512]{1,0:T(8,128)S(1)} %get-tuple-element.18.w_ref, ...), custom_call_target="tpu_custom_call" | custom-call | flops 805306368 | bytes 1048576 | tf_op jit(solution)/shard_map/whiten/pallas_call | solution.py:362
  (9 shorter events, 0.1 us)
Async XLA Ops:
  0.0 0.9 %copy-start = (bf16[1,256,512]{2,1,0:T(8,128)(2,1)S(1)}, bf16[1,256,512]{2,1,0:T(8,128)(2,1)}, u32[]{:S(2)}) copy-start(bf16[1,256,512]{2,1,0:T(8,128)(2,1)} %param.3) | copy-start | bytes 786436
  1.0 0.9 %copy-start.1 = (bf16[1,256,512]{2,1,0:T(8,128)(2,1)S(1)}, bf16[1,256,512]{2,1,0:T(8,128)(2,1)}, u32[]{:S(2)}) copy-start(bf16[1,256,512]{2,1,0:T(8,128)(2,1)} %param.3) | copy-start | bytes 786436
  1.2 1.5 %collective-permute-start.5 = (f32[256,128]{1,0:T(8,128)S(1)}, f32[256,128]{1,0:T(8,128)S(1)}, u32[]{:S(2)}, u32[]{:S(2)}) collective-permute-start(f32[256,128]{1,0:T(8,128)S(1)} %get-tuple-element.14), channel_id=1, source_target_pairs={{0,1},{1,0},{2,3},{3,2},{4,5},{5,4},{6,7},{7,6},{8,9},{9,8},{10,11... | collective-permute-start | bytes 393224 | tf_op jit(solution)/shard_map/ppermute | solution.py:213
  2.8 10.2 %collective-permute-start.6 = (f32[256,128]{1,0:T(8,128)S(1)}, f32[256,128]{1,0:T(8,128)S(1)}, u32[]{:S(2)}, u32[]{:S(2)}) collective-permute-start(f32[256,128]{1,0:T(8,128)S(1)} %multiply_add_fusion.2), channel_id=1, source_target_pairs={{0,2},{1,3},{2,0},{3,1},{4,6},{5,7},{6,4},{7,5},{8,10},{9,11},{10,... | collective-permute-start | bytes 393224 | tf_op jit(solution)/shard_map/ppermute | solution.py:213
  5.8 3.6 %collective-permute-start = (f32[8,128]{1,0:T(8,128)S(1)}, f32[8,128]{1,0:T(8,128)S(1)}, u32[]{:S(2)}, u32[]{:S(2)}) collective-permute-start(f32[8,128]{1,0:T(8,128)S(1)} %get-tuple-element.13), channel_id=1, source_target_pairs={{0,8},{8,0},{16,24},{24,16},{1,9},{9,1},{17,25},{25,17},{2,10},{10... | collective-permute-start | bytes 12296 | tf_op jit(solution)/shard_map/ppermute | solution.py:213
  9.4 3.6 %collective-permute-start.1 = (f32[8,128]{1,0:T(8,128)S(1)}, f32[8,128]{1,0:T(8,128)S(1)}, u32[]{:S(2)}, u32[]{:S(2)}) collective-permute-start(f32[8,128]{1,0:T(8,128)S(1)} %add.60), channel_id=1, source_target_pairs={{0,16},{8,24},{16,0},{24,8},{1,17},{9,25},{17,1},{25,9},{2,18},{10... | collective-permute-start | bytes 12296 | tf_op jit(solution)/shard_map/ppermute | solution.py:213
  13.1 7.0 %collective-permute-start.7 = (f32[264,128]{1,0:T(8,128)S(1)}, f32[264,128]{1,0:T(8,128)S(1)}, u32[]{:S(2)}, u32[]{:S(2)}) collective-permute-start(f32[264,128]{1,0:T(8,128)S(1)} %pad_maximum_fusion), channel_id=1, source_target_pairs={{0,6},{1,7},{2,4},{3,5},{4,2},{5,3},{6,0},{7,1},{8,14},{9,15},{10,... | collective-permute-start | bytes 405512 | tf_op jit(solution)/shard_map/ppermute | solution.py:213
  15.6 0.7 %copy-start.2 = (s32[1,8]{1,0:T(1,128)S(1)}, s32[1,8]{1,0:T(1,128)}, u32[]{:S(2)}) copy-start(s32[1,8]{1,0:T(1,128)} %picks_ref.1) | copy-start | bytes 100
  15.6 0.7 %copy-start.3 = (f32[64]{0:T(128)S(1)}, f32[64]{0:T(128)}, u32[]{:S(2)}) copy-start(f32[64]{0:T(128)} %angles_ref.1) | copy-start | bytes 772
  18.6 1.5 %collective-permute-start.2 = (f32[8,128]{1,0:T(8,128)S(1)}, f32[8,128]{1,0:T(8,128)S(1)}, u32[]{:S(2)}, u32[]{:S(2)}) collective-permute-start(f32[8,128]{1,0:T(8,128)S(1)} %add.61), channel_id=1, source_target_pairs={{0,1},{1,0},{2,3},{3,2},{4,5},{5,4},{6,7},{7,6},{8,9},{9,8},{10,11... | collective-permute-start | bytes 12296 | tf_op jit(solution)/shard_map/ppermute | solution.py:213
  20.1 3.2 %collective-permute-start.8 = (f32[264,128]{1,0:T(8,128)S(1)}, f32[264,128]{1,0:T(8,128)S(1)}, u32[]{:S(2)}, u32[]{:S(2)}) collective-permute-start(f32[264,128]{1,0:T(8,128)S(1)} %pad_maximum_fusion.1), channel_id=1, source_target_pairs={{0,1},{1,0},{2,3},{3,2},{4,5},{5,4},{6,7},{7,6},{8,9},{9,8},{10,11... | collective-permute-start | bytes 405512 | tf_op jit(solution)/shard_map/ppermute | solution.py:213
  20.2 4.6 %collective-permute-start.4 = (f32[8,128]{1,0:T(8,128)S(1)}, f32[8,128]{1,0:T(8,128)S(1)}, u32[]{:S(2)}, u32[]{:S(2)}) collective-permute-start(f32[8,128]{1,0:T(8,128)S(1)} %multiply_add_fusion.4), channel_id=1, source_target_pairs={{0,4},{1,5},{2,6},{3,7},{4,0},{5,1},{6,2},{7,3},{8,12},{9,13},{10,... | collective-permute-start | bytes 12296 | tf_op jit(solution)/shard_map/ppermute | solution.py:213
  22.4 3.6 %collective-permute-start.3 = (f32[8,128]{1,0:T(8,128)S(1)}, f32[8,128]{1,0:T(8,128)S(1)}, u32[]{:S(2)}, u32[]{:S(2)}) collective-permute-start(f32[8,128]{1,0:T(8,128)S(1)} %multiply_add_fusion.4), channel_id=1, source_target_pairs={{0,2},{1,3},{2,0},{3,1},{4,6},{5,7},{6,4},{7,5},{8,10},{9,11},{10,... | collective-permute-start | bytes 12296 | tf_op jit(solution)/shard_map/ppermute | solution.py:213

commit v10 on v9

--- a/solution.py
+++ b/solution.py
@@ -57,11 +57,9 @@
 
 def dot3(left, right):
     (lh, ll), (rh, rl) = left, right
-    return (
-        jnp.dot(lh, rh, preferred_element_type=F32)
-        + jnp.dot(lh, rl, preferred_element_type=F32)
-        + jnp.dot(ll, rh, preferred_element_type=F32)
-    )
+    count = lh.shape[0]
+    both = jnp.dot(jnp.concatenate([lh, ll], axis=0), rh, preferred_element_type=F32)
+    return both[:count] + both[count:] + jnp.dot(lh, rl, preferred_element_type=F32)
 
 
 def beside(first, second):

time: 28.1 us -> 28.1 us (level)
  no operation moved by 1% of the time
where the time goes in v10:
time: 28.1 us; the launch traced here: 27.9 us
  starting transfers between devices  12.4 us (44%)
  waiting for transfers between devices  8.2 us (29%)
  Pallas kernels  5.39 us (19%)
  local copies, waits for them, and re-layouts  1.73 us (6%)
    ppermute x9, starting transfers between devices, exchange(): lax.ppermute(value, axis, [(i, i ^ mask) for i in range(lax.axis_size(axi...  12.4 us
    ppermute x9, waiting for transfers between devices, exchange(): lax.ppermute(value, axis, [(i, i ^ mask) for i in range(lax.axis_size(axi...  8.2 us
    pallas_call x1, Pallas kernels, steps(): pl.pallas_call(null_kernel, out_shape=(jax.ShapeDtypeStruct((rows, width)...  2.37 us
    pallas_call x1, Pallas kernels, steps(): pl.pallas_call(whiten_kernel, out_shape=jax.ShapeDtypeStruct((rows, width...  1.86 us
    unnamed x8, local copies, waits for them, and re-layouts  1.72 us
    pallas_call x1, Pallas kernels, steps(): pl.pallas_call(square_kernel, out_shape=(jax.ShapeDtypeStruct((width, ant...  0.61 us
  transfers between devices with their start and end apart: 9, of which 6 were waited for; matrix products, arithmetic and copies ran while one was open for 0% of the time, Pallas kernels for 12%

profile of v10, /device:TPU:0, one launch (start us, length us, event | category | flops | bytes accessed | tf_op | source)
XLA Modules:
  0.0 27.9 jit_solution(2258656915217724725)
XLA Ops:
  0.0 0.0 copy-start
  0.0 0.9 %copy-done = bf16[1,256,512]{2,1,0:T(8,128)(2,1)S(1)} copy-done((bf16[1,256,512]{2,1,0:T(8,128)(2,1)S(1)}, bf16[1,256,512]{2,1,0:T(8,128)(2,1)}, u32[]{:S(2)}) %copy-start) | copy-done | bytes 262168
  1.0 0.0 copy-start.1
  1.0 0.3 shard_map.37
  1.2 0.6 %collective-permute-start.5 = (f32[256,128]{1,0:T(8,128)S(1)}, f32[256,128]{1,0:T(8,128)S(1)}, u32[]{:S(2)}, u32[]{:S(2)}) collective-permute-start(f32[256,128]{1,0:T(8,128)S(1)} %get-tuple-element.14), channel_id=1, source_target_pairs={{0,1},{1,0},{2,3},{3,2},{4,5},{5,4},{6,7},{7,6},{8,9},{9,8},{10,11... | collective-permute-start | bytes 393224 | tf_op jit(solution)/shard_map/ppermute | solution.py:211
  1.8 0.1 copy-done.1
  1.9 0.3 shard_map.38
  2.2 0.6 %collective-permute-done.5 = f32[256,128]{1,0:T(8,128)S(1)} collective-permute-done((f32[256,128]{1,0:T(8,128)S(1)}, f32[256,128]{1,0:T(8,128)S(1)}, u32[]{:S(2)}, u32[]{:S(2)}) %collective-permute-start.5) | collective-permute-done | bytes 131104 | tf_op jit(solution)/shard_map/ppermute | solution.py:211
  2.8 3.0 %collective-permute-start.6 = (f32[256,128]{1,0:T(8,128)S(1)}, f32[256,128]{1,0:T(8,128)S(1)}, u32[]{:S(2)}, u32[]{:S(2)}) collective-permute-start(f32[256,128]{1,0:T(8,128)S(1)} %multiply_add_fusion.2), channel_id=1, source_target_pairs={{0,2},{1,3},{2,0},{3,1},{4,6},{5,7},{6,4},{7,5},{8,10},{9,11},{10,... | collective-permute-start | bytes 393224 | tf_op jit(solution)/shard_map/ppermute | solution.py:211
  5.8 1.5 %collective-permute-start = (f32[8,128]{1,0:T(8,128)S(1)}, f32[8,128]{1,0:T(8,128)S(1)}, u32[]{:S(2)}, u32[]{:S(2)}) collective-permute-start(f32[8,128]{1,0:T(8,128)S(1)} %get-tuple-element.13), channel_id=1, source_target_pairs={{0,8},{8,0},{16,24},{24,16},{1,9},{9,1},{17,25},{25,17},{2,10},{10... | collective-permute-start | bytes 12296 | tf_op jit(solution)/shard_map/ppermute | solution.py:211
  7.3 2.1 %collective-permute-done = f32[8,128]{1,0:T(8,128)S(1)} collective-permute-done((f32[8,128]{1,0:T(8,128)S(1)}, f32[8,128]{1,0:T(8,128)S(1)}, u32[]{:S(2)}, u32[]{:S(2)}) %collective-permute-start) | collective-permute-done | bytes 4128 | tf_op jit(solution)/shard_map/ppermute | solution.py:211
  9.4 1.5 %collective-permute-start.1 = (f32[8,128]{1,0:T(8,128)S(1)}, f32[8,128]{1,0:T(8,128)S(1)}, u32[]{:S(2)}, u32[]{:S(2)}) collective-permute-start(f32[8,128]{1,0:T(8,128)S(1)} %add.60), channel_id=1, source_target_pairs={{0,16},{8,24},{16,0},{24,8},{1,17},{9,25},{17,1},{25,9},{2,18},{10... | collective-permute-start | bytes 12296 | tf_op jit(solution)/shard_map/ppermute | solution.py:211
  10.9 2.1 %collective-permute-done.1 = f32[8,128]{1,0:T(8,128)S(1)} collective-permute-done((f32[8,128]{1,0:T(8,128)S(1)}, f32[8,128]{1,0:T(8,128)S(1)}, u32[]{:S(2)}, u32[]{:S(2)}) %collective-permute-start.1) | collective-permute-done | bytes 4128 | tf_op jit(solution)/shard_map/ppermute | solution.py:211
  13.0 0.0 collective-permute-done.6
  13.1 2.5 %collective-permute-start.7 = (f32[264,128]{1,0:T(8,128)S(1)}, f32[264,128]{1,0:T(8,128)S(1)}, u32[]{:S(2)}, u32[]{:S(2)}) collective-permute-start(f32[264,128]{1,0:T(8,128)S(1)} %pad_maximum_fusion), channel_id=1, source_target_pairs={{0,6},{1,7},{2,4},{3,5},{4,2},{5,3},{6,0},{7,1},{8,14},{9,15},{10,... | collective-permute-start | bytes 405512 | tf_op jit(solution)/shard_map/ppermute | solution.py:211
  15.6 0.0 copy-start.2
  15.6 0.0 copy-start.3
  15.6 0.7 %copy-done.2 = s32[1,8]{1,0:T(1,128)S(1)} copy-done((s32[1,8]{1,0:T(1,128)S(1)}, s32[1,8]{1,0:T(1,128)}, u32[]{:S(2)}) %copy-start.2) | copy-done | bytes 56
  16.3 0.0 copy-done.3
  16.3 2.4 %null.1 = (f32[256,512]{1,0:T(8,128)S(1)}, bf16[512,512]{1,0:T(8,128)(2,1)S(1)}, bf16[512,512]{1,0:T(8,128)(2,1)S(1)}) custom-call(s32[1,8]{1,0:T(1,128)S(1)} %copy-done.2, f32[64]{0:T(128)S(1)} %copy-done.3, bf16[256,512]{1,0:T(8,128)(2,1)S(1)} %bitcast.5), custom_call_target="tpu_custom_call" | custom-call | flops 67108864 | bytes 786432 | tf_op jit(solution)/shard_map/null/pallas_call | solution.py:328
  18.6 0.1 collective-permute-start.2
  18.7 1.3 %collective-permute-done.7 = f32[264,128]{1,0:T(8,128)S(1)} collective-permute-done((f32[264,128]{1,0:T(8,128)S(1)}, f32[264,128]{1,0:T(8,128)S(1)}, u32[]{:S(2)}, u32[]{:S(2)}) %collective-permute-start.7) | collective-permute-done | bytes 135200 | tf_op jit(solution)/shard_map/ppermute | solution.py:211
  20.0 0.1 broadcast_select_fusion
  20.1 0.1 collective-permute-start.8
  20.2 0.0 collective-permute-done.2
  20.2 2.2 %collective-permute-start.4 = (f32[8,128]{1,0:T(8,128)S(1)}, f32[8,128]{1,0:T(8,128)S(1)}, u32[]{:S(2)}, u32[]{:S(2)}) collective-permute-start(f32[8,128]{1,0:T(8,128)S(1)} %multiply_add_fusion.4), channel_id=1, source_target_pairs={{0,4},{1,5},{2,6},{3,7},{4,0},{5,1},{6,2},{7,3},{8,12},{9,13},{10,... | collective-permute-start | bytes 12296 | tf_op jit(solution)/shard_map/ppermute | solution.py:211
  22.4 0.9 %collective-permute-start.3 = (f32[8,128]{1,0:T(8,128)S(1)}, f32[8,128]{1,0:T(8,128)S(1)}, u32[]{:S(2)}, u32[]{:S(2)}) collective-permute-start(f32[8,128]{1,0:T(8,128)S(1)} %multiply_add_fusion.4), channel_id=1, source_target_pairs={{0,2},{1,3},{2,0},{3,1},{4,6},{5,7},{6,4},{7,5},{8,10},{9,11},{10,... | collective-permute-start | bytes 12296 | tf_op jit(solution)/shard_map/ppermute | solution.py:211
  23.3 0.0 collective-permute-done.8.other_ref
  23.3 0.6 %square.1 = (f32[512,256]{1,0:T(8,128)S(1)}, f32[512,256]{1,0:T(8,128)S(1)}, f32[16,128]{1,0:T(8,128)S(1)}) custom-call(s32[1]{0:T(128)} %bitcast.part_ref.parity_ref, f32[256,128]{1,0:T(8,128)S(1)} %get-tuple-element.21.own_ref, f32[264,128]{1,0:T(8,128)S(1)} %collective-permute-done.8.other_ref), custom_call_target="tpu_custom_call" | custom-call | flops 402653184 | bytes 1048576 | tf_op jit(solution)/shard_map/square/pallas_call | solution.py:344
  23.9 0.8 %collective-permute-done.4 = f32[8,128]{1,0:T(8,128)S(1)} collective-permute-done((f32[8,128]{1,0:T(8,128)S(1)}, f32[8,128]{1,0:T(8,128)S(1)}, u32[]{:S(2)}, u32[]{:S(2)}) %collective-permute-start.4) | collective-permute-done | bytes 4128 | tf_op jit(solution)/shard_map/ppermute | solution.py:211
  24.8 1.2 %collective-permute-done.3 = f32[8,128]{1,0:T(8,128)S(1)} collective-permute-done((f32[8,128]{1,0:T(8,128)S(1)}, f32[8,128]{1,0:T(8,128)S(1)}, u32[]{:S(2)}, u32[]{:S(2)}) %collective-permute-start.3) | collective-permute-done | bytes 4128 | tf_op jit(solution)/shard_map/ppermute | solution.py:211
  26.0 1.9 %whiten.1 = f32[256,512]{1,0:T(8,128)} custom-call(f32[8,128]{1,0:T(8,128)S(1)} %multiply_add_fusion.3.band_ref, f32[16,128]{1,0:T(8,128)S(1)} %get-tuple-element.15.stats_ref, f32[512,256]{1,0:T(8,128)S(1)} %get-tuple-element.16.cov_ref, f32[512,256]{1,0:T(8,128)S(1)} %get-tuple-element.17.square_ref, f32[256,512]{1,0:T(8,128)S(1)} %get-tuple-element.18.w_ref, ...), custom_call_target="tpu_custom_call" | custom-call | flops 805306368 | bytes 1048576 | tf_op jit(solution)/shard_map/whiten/pallas_call | solution.py:360
  (9 shorter events, 0.1 us)
Async XLA Ops:
  0.0 0.9 %copy-start = (bf16[1,256,512]{2,1,0:T(8,128)(2,1)S(1)}, bf16[1,256,512]{2,1,0:T(8,128)(2,1)}, u32[]{:S(2)}) copy-start(bf16[1,256,512]{2,1,0:T(8,128)(2,1)} %param.3) | copy-start | bytes 786436
  1.0 0.9 %copy-start.1 = (bf16[1,256,512]{2,1,0:T(8,128)(2,1)S(1)}, bf16[1,256,512]{2,1,0:T(8,128)(2,1)}, u32[]{:S(2)}) copy-start(bf16[1,256,512]{2,1,0:T(8,128)(2,1)} %param.3) | copy-start | bytes 786436
  1.2 1.5 %collective-permute-start.5 = (f32[256,128]{1,0:T(8,128)S(1)}, f32[256,128]{1,0:T(8,128)S(1)}, u32[]{:S(2)}, u32[]{:S(2)}) collective-permute-start(f32[256,128]{1,0:T(8,128)S(1)} %get-tuple-element.14), channel_id=1, source_target_pairs={{0,1},{1,0},{2,3},{3,2},{4,5},{5,4},{6,7},{7,6},{8,9},{9,8},{10,11... | collective-permute-start | bytes 393224 | tf_op jit(solution)/shard_map/ppermute | solution.py:211
  2.8 10.2 %collective-permute-start.6 = (f32[256,128]{1,0:T(8,128)S(1)}, f32[256,128]{1,0:T(8,128)S(1)}, u32[]{:S(2)}, u32[]{:S(2)}) collective-permute-start(f32[256,128]{1,0:T(8,128)S(1)} %multiply_add_fusion.2), channel_id=1, source_target_pairs={{0,2},{1,3},{2,0},{3,1},{4,6},{5,7},{6,4},{7,5},{8,10},{9,11},{10,... | collective-permute-start | bytes 393224 | tf_op jit(solution)/shard_map/ppermute | solution.py:211
  5.8 3.6 %collective-permute-start = (f32[8,128]{1,0:T(8,128)S(1)}, f32[8,128]{1,0:T(8,128)S(1)}, u32[]{:S(2)}, u32[]{:S(2)}) collective-permute-start(f32[8,128]{1,0:T(8,128)S(1)} %get-tuple-element.13), channel_id=1, source_target_pairs={{0,8},{8,0},{16,24},{24,16},{1,9},{9,1},{17,25},{25,17},{2,10},{10... | collective-permute-start | bytes 12296 | tf_op jit(solution)/shard_map/ppermute | solution.py:211
  9.4 3.6 %collective-permute-start.1 = (f32[8,128]{1,0:T(8,128)S(1)}, f32[8,128]{1,0:T(8,128)S(1)}, u32[]{:S(2)}, u32[]{:S(2)}) collective-permute-start(f32[8,128]{1,0:T(8,128)S(1)} %add.60), channel_id=1, source_target_pairs={{0,16},{8,24},{16,0},{24,8},{1,17},{9,25},{17,1},{25,9},{2,18},{10... | collective-permute-start | bytes 12296 | tf_op jit(solution)/shard_map/ppermute | solution.py:211
  13.1 7.0 %collective-permute-start.7 = (f32[264,128]{1,0:T(8,128)S(1)}, f32[264,128]{1,0:T(8,128)S(1)}, u32[]{:S(2)}, u32[]{:S(2)}) collective-permute-start(f32[264,128]{1,0:T(8,128)S(1)} %pad_maximum_fusion), channel_id=1, source_target_pairs={{0,6},{1,7},{2,4},{3,5},{4,2},{5,3},{6,0},{7,1},{8,14},{9,15},{10,... | collective-permute-start | bytes 405512 | tf_op jit(solution)/shard_map/ppermute | solution.py:211
  15.6 0.7 %copy-start.2 = (s32[1,8]{1,0:T(1,128)S(1)}, s32[1,8]{1,0:T(1,128)}, u32[]{:S(2)}) copy-start(s32[1,8]{1,0:T(1,128)} %picks_ref.1) | copy-start | bytes 100
  15.6 0.7 %copy-start.3 = (f32[64]{0:T(128)S(1)}, f32[64]{0:T(128)}, u32[]{:S(2)}) copy-start(f32[64]{0:T(128)} %angles_ref.1) | copy-start | bytes 772
  18.6 1.5 %collective-permute-start.2 = (f32[8,128]{1,0:T(8,128)S(1)}, f32[8,128]{1,0:T(8,128)S(1)}, u32[]{:S(2)}, u32[]{:S(2)}) collective-permute-start(f32[8,128]{1,0:T(8,128)S(1)} %add.61), channel_id=1, source_target_pairs={{0,1},{1,0},{2,3},{3,2},{4,5},{5,4},{6,7},{7,6},{8,9},{9,8},{10,11... | collective-permute-start | bytes 12296 | tf_op jit(solution)/shard_map/ppermute | solution.py:211
  20.1 3.2 %collective-permute-start.8 = (f32[264,128]{1,0:T(8,128)S(1)}, f32[264,128]{1,0:T(8,128)S(1)}, u32[]{:S(2)}, u32[]{:S(2)}) collective-permute-start(f32[264,128]{1,0:T(8,128)S(1)} %pad_maximum_fusion.1), channel_id=1, source_target_pairs={{0,1},{1,0},{2,3},{3,2},{4,5},{5,4},{6,7},{7,6},{8,9},{9,8},{10,11... | collective-permute-start | bytes 405512 | tf_op jit(solution)/shard_map/ppermute | solution.py:211
  20.2 4.6 %collective-permute-start.4 = (f32[8,128]{1,0:T(8,128)S(1)}, f32[8,128]{1,0:T(8,128)S(1)}, u32[]{:S(2)}, u32[]{:S(2)}) collective-permute-start(f32[8,128]{1,0:T(8,128)S(1)} %multiply_add_fusion.4), channel_id=1, source_target_pairs={{0,4},{1,5},{2,6},{3,7},{4,0},{5,1},{6,2},{7,3},{8,12},{9,13},{10,... | collective-permute-start | bytes 12296 | tf_op jit(solution)/shard_map/ppermute | solution.py:211
  22.4 3.6 %collective-permute-start.3 = (f32[8,128]{1,0:T(8,128)S(1)}, f32[8,128]{1,0:T(8,128)S(1)}, u32[]{:S(2)}, u32[]{:S(2)}) collective-permute-start(f32[8,128]{1,0:T(8,128)S(1)} %multiply_add_fusion.4), channel_id=1, source_target_pairs={{0,2},{1,3},{2,0},{3,1},{4,6},{5,7},{6,4},{7,5},{8,10},{9,11},{10,... | collective-permute-start | bytes 12296 | tf_op jit(solution)/shard_map/ppermute | solution.py:211
